TPU v7x, 8 devices: a whole 2x2x1 slice. The times are simulated.
8 devices in a mesh: dp: 2 (over z, y), cp: 4 (over x, core).
Axes of the slice: x: 2, y: 2, z: 1, core: 2. Of those that a mesh axis runs over, the one named last changes fastest.
Arguments:
- hidden: bfloat16 [32, 256, 2304], P('dp'), parts along dimension 0
- start_pos: int32 [32], P('dp'), parts along dimension 0
- cache_k: bfloat16 [32, 512, 1024], P('dp', 'cp'), parts along dimension 0
- cache_v: bfloat16 [32, 512, 1024], P('dp', 'cp'), parts along dimension 0
- w_q: bfloat16 [2304, 8, 256], replicated
- w_k: bfloat16 [2304, 4, 256], replicated
- w_v: bfloat16 [2304, 4, 256], replicated
- w_o: bfloat16 [8, 256, 2304], replicated
- w_gate: bfloat16 [2304, 9216], replicated
- w_up: bfloat16 [2304, 9216], replicated
- w_down: bfloat16 [9216, 2304], replicated
- norm_attn: bfloat16 [2304], replicated
- norm_mlp: bfloat16 [2304], replicated
Outputs:
- output 1: bfloat16 [32, 256, 2304], P('dp'), parts along dimension 0
- output 2: bfloat16 [32, 512, 1024], P('dp', 'cp'), parts along dimension 0
- output 3: bfloat16 [32, 512, 1024], P('dp', 'cp'), parts along dimension 0
There are 2 independent parts. A program takes and returns all parts, laid end to end along the dimension named above; an argument that names none is the same for every part.
All inputs are finite; a program needn't handle non-finite values.
Results may differ from a plain program's by a relative error of at most 0.0180753.
Values sent between devices are 32-bit elements.
A program may use at most 1 GiB of HBM per device.

v0:
```python
import jax
import jax.numpy as jnp
from jax import lax
from jax.sharding import PartitionSpec as P

NORM_EPS = 1e-6
ROPE_BASE = 1.0e4
MASK_FLOOR = -1.0e30


def rms_norm(hidden, gain):
    hid_f32 = hidden.astype(jnp.float32)
    inv_rms = lax.rsqrt(jnp.mean(hid_f32 * hid_f32, axis=-1, keepdims=True) + NORM_EPS)
    return (hid_f32 * inv_rms * (1.0 + gain.astype(jnp.float32))).astype(jnp.bfloat16)


def rotate(proj, positions):
    head_dim = proj.shape[-1]
    half_dim = head_dim // 2
    inv_freq = ROPE_BASE ** (-2.0 * jnp.arange(half_dim, dtype=jnp.float32) / head_dim)
    angles = positions.astype(jnp.float32)[:, :, None, None] * inv_freq
    cos_tab = jnp.cos(angles)
    sin_tab = jnp.sin(angles)
    first = proj[..., :half_dim]
    second = proj[..., half_dim:]
    return jnp.concatenate([first * cos_tab - second * sin_tab, second * cos_tab + first * sin_tab], axis=-1)


def project_chunk(hidden, start_pos, w_q, w_k, w_v, norm_attn):
    chunk_len = hidden.shape[1]
    head_dim = w_q.shape[2]
    normed = rms_norm(hidden, norm_attn)
    positions = start_pos[:, None] + jnp.arange(chunk_len, dtype=jnp.int32)[None, :]
    q_proj = jnp.einsum('bcd,dhe->bche', normed, w_q, preferred_element_type=jnp.float32)
    queries = (rotate(q_proj, positions) * head_dim ** -0.5).astype(jnp.bfloat16)
    k_proj = jnp.einsum('bcd,dhe->bche', normed, w_k, preferred_element_type=jnp.float32)
    k_new = rotate(k_proj, positions).astype(jnp.bfloat16)
    v_new = jnp.einsum('bcd,dhe->bche', normed, w_v, preferred_element_type=jnp.float32).astype(jnp.bfloat16)
    return queries, k_new, v_new


def partial_attend(scores, allowed, values):
    masked = jnp.where(allowed, scores, MASK_FLOOR)
    row_max = jnp.max(masked, axis=-1)
    weights = jnp.where(allowed, jnp.exp(masked - row_max[..., None]), 0.0)
    row_sum = jnp.sum(weights, axis=-1)
    weighted = jnp.einsum('bkcgs,bskd->bkcgd', weights.astype(jnp.bfloat16), values, preferred_element_type=jnp.float32)
    return row_max, weighted, row_sum


def combine_parts(first_max, first_num, first_den, second_max, second_num, second_den):
    both_max = jnp.maximum(first_max, second_max)
    first_w = jnp.exp(first_max - both_max)
    second_w = jnp.exp(second_max - both_max)
    total_num = first_num * first_w[..., None] + second_num * second_w[..., None]
    total_den = first_den * first_w + second_den * second_w
    return (total_num / total_den[..., None]).astype(jnp.bfloat16)


def finish_layer(hidden, attended, w_o, w_gate, w_up, w_down, norm_mlp):
    kv_heads, group_size, head_dim = attended.shape[1], attended.shape[3], attended.shape[4]
    w_o_grp = w_o.reshape(kv_heads, group_size, head_dim, w_o.shape[2])
    attn_out = jnp.einsum('bkcgd,kgde->bce', attended, w_o_grp, preferred_element_type=jnp.float32)
    residual = (hidden.astype(jnp.float32) + attn_out).astype(jnp.bfloat16)
    normed_mlp = rms_norm(residual, norm_mlp)
    gate_proj = jnp.einsum('bcd,df->bcf', normed_mlp, w_gate, preferred_element_type=jnp.float32)
    up_proj = jnp.einsum('bcd,df->bcf', normed_mlp, w_up, preferred_element_type=jnp.float32)
    gated_mid = (jax.nn.gelu(gate_proj, approximate=True) * up_proj).astype(jnp.bfloat16)
    down_proj = jnp.einsum('bcf,fd->bcd', gated_mid, w_down, preferred_element_type=jnp.float32)
    return (residual.astype(jnp.float32) + down_proj).astype(jnp.bfloat16)


def write_rows(cache_rows, new_rows, offset):
    shard_len = cache_rows.shape[0]
    chunk_len = new_rows.shape[0]
    blank = jnp.zeros((shard_len, new_rows.shape[1]), new_rows.dtype)
    padded = jnp.concatenate([blank, new_rows, blank], axis=0)
    window = lax.dynamic_slice_in_dim(padded, shard_len - offset, shard_len, axis=0)
    local_pos = jnp.arange(shard_len, dtype=jnp.int32)
    inside = (local_pos >= offset) & (local_pos < offset + chunk_len)
    return jnp.where(inside[:, None], window, cache_rows)


def solution(mesh):
    def local_layer(hidden, start_pos, cache_k, cache_v, w_q, w_k, w_v, w_o, w_gate, w_up, w_down, norm_attn, norm_mlp):
        n_seq, chunk_len = hidden.shape[0], hidden.shape[1]
        shard_len = cache_k.shape[1]
        n_heads, head_dim = w_q.shape[1], w_q.shape[2]
        kv_heads = w_k.shape[1]
        group_size = n_heads // kv_heads
        shard_lo = lax.axis_index('cp') * shard_len
        queries, k_new, v_new = project_chunk(hidden, start_pos, w_q, w_k, w_v, norm_attn)
        q_grp = queries.reshape(n_seq, chunk_len, kv_heads, group_size, head_dim)
        keys_here = cache_k.reshape(n_seq, shard_len, kv_heads, head_dim)
        vals_here = cache_v.reshape(n_seq, shard_len, kv_heads, head_dim)
        key_pos = shard_lo + jnp.arange(shard_len, dtype=jnp.int32)
        hist_ok = (key_pos[None, :] < start_pos[:, None])[:, None, None, None, :]
        hist_scores = jnp.einsum('bckgd,bskd->bkcgs', q_grp, keys_here, preferred_element_type=jnp.float32)
        hist_max, hist_num, hist_den = partial_attend(hist_scores, hist_ok, vals_here)
        glob_max = lax.pmax(hist_max, 'cp')
        rescale = jnp.exp(hist_max - glob_max)
        packed = jnp.concatenate([hist_num * rescale[..., None], (hist_den * rescale)[..., None]], axis=-1)
        packed = lax.psum(packed, 'cp')
        query_idx = jnp.arange(chunk_len, dtype=jnp.int32)
        own_ok = (query_idx[None, :] <= query_idx[:, None])[None, None, :, None, :]
        own_scores = jnp.einsum('bckgd,bjkd->bkcgj', q_grp, k_new, preferred_element_type=jnp.float32)
        own_max, own_num, own_den = partial_attend(own_scores, own_ok, v_new)
        attended = combine_parts(glob_max, packed[..., :head_dim], packed[..., head_dim], own_max, own_num, own_den)
        hidden_out = finish_layer(hidden, attended, w_o, w_gate, w_up, w_down, norm_mlp)
        kv_width = kv_heads * head_dim
        offsets = start_pos - shard_lo
        new_k = jax.vmap(write_rows)(cache_k, k_new.reshape(n_seq, chunk_len, kv_width), offsets)
        new_v = jax.vmap(write_rows)(cache_v, v_new.reshape(n_seq, chunk_len, kv_width), offsets)
        return hidden_out, new_k, new_v

    group_spec = P('dp', None, None)
    cache_spec = P('dp', 'cp', None)
    whole_spec = P()
    return jax.shard_map(
        local_layer,
        mesh=mesh,
        in_specs=(group_spec, P('dp'), cache_spec, cache_spec, whole_spec, whole_spec, whole_spec, whole_spec, whole_spec, whole_spec, whole_spec, whole_spec, whole_spec),
        out_specs=(group_spec, cache_spec, cache_spec),
        check_vma=False,
    )
```

profile of v0, /device:TPU:0, one launch (start us, length us, event | category | flops | bytes accessed | tf_op | source)
XLA Modules:
  0.0 1626.3 jit_solution(15331401894894793928)
XLA Ops:
  10.0 8.4 fusion.15
  18.4 7.8 reshape.165
  26.2 12.7 copy.16
  38.9 7.3 multiply_cosine_fusion
  46.2 49.6 %fusion.57 = f32[16,256,8,256]{1,3,2,0:T(8,128)} fusion(bf16[2304,8,256]{0,2,1:T(8,128)(2,1)} %copy.16, bf16[16,256,2304]{2,1,0:T(8,128)(2,1)} %param.13, f32[2304]{0:T(1024)S(1)} %convert_add_fusion.3, f32[16,256]{1,0:T(8,128)S(1)} %add_rsqrt_fusion.1), kind=kOutput, calls=%fused_computation.65 | convolution fusion | flops 38692454400 | bytes 61891584 | tf_op jit(solution)/shard_map/bcd,dhe->bche/dot_general | solution.py:34
  95.9 22.1 %multiply_subtract_fusion = (f32[16,256,8,128]{1,3,2,0:T(8,128)}, f32[16,256,8,128]{1,3,2,0:T(8,128)}) fusion(f32[16,256,8,256]{1,3,2,0:T(8,128)} %fusion.57, f32[16,256,128]{1,2,0:T(8,128)S(1)} %get-tuple-element.53, f32[16,256,128]{1,2,0:T(8,128)S(1)} %get-tuple-element.52), kind=kLoop, calls=%fused_computation.60 | loop fusion | flops 25165824 | bytes 71303168 | tf_op jit(solution)/shard_map/sub | solution.py:26
  117.9 17.6 %copy.17 = f32[16,256,4,2,128]{4,1,3,2,0:T(8,128)} copy(f32[16,256,4,2,128]{1,4,3,2,0:T(8,128)} %bitcast.102) | data formatting | bytes 33554432 | tf_op jit(solution)/shard_map/concatenate | solution.py:26
  135.5 17.6 %copy.18 = f32[16,256,4,2,128]{4,1,3,2,0:T(8,128)} copy(f32[16,256,4,2,128]{1,4,3,2,0:T(8,128)} %bitcast.101) | data formatting | bytes 33554432 | tf_op jit(solution)/shard_map/concatenate | solution.py:26
  153.1 19.3 %select_reduce_fusion.1 = (f32[16,4,256,2]{2,3,1,0:T(2,128)}, f32[16,4,256,2,128]{2,4,3,1,0:T(8,128)}) fusion(pred[16,128]{1,0:T(8,128)(4,1)S(1)} %copy-done.5, bf16[16,128,4,256,1]{3,2,1,0,4:T(4,128)(2,1)} %bitcast.106, f32[16,256,4,2,128]{4,1,3,2,0:T(8,128)} %copy.18, f32[16,256,4,2,128]{4,1,3,2,0:T(8,128)} %copy.17), kind=kOutput, calls=%fused_computation.62 | convolution fusion | flops 2181005312 | bytes 54659072 | tf_op jit(solution)/shard_map/bckgd,bskd->bkcgs/dot_general | solution.py:98
  181.0 8.5 copy.23
  189.5 8.5 copy.25
  197.9 25.7 %convolution_convert_fusion = bf16[16,256,4,256]{1,3,2,0:T(8,128)(2,1)} fusion(bf16[2304,4,256]{0,2,1:T(8,128)(2,1)} %copy.25, bf16[16,256,2304]{2,1,0:T(8,128)(2,1)} %param.13, f32[2304]{0:T(1024)S(1)} %convert_add_fusion.3, f32[16,256]{1,0:T(8,128)S(1)} %add_rsqrt_fusion.1), kind=kOutput, calls=%fused_computation.76 | convolution fusion | flops 19369295872 | bytes 32007168 | tf_op jit(solution)/shard_map/bcd,dhe->bche/dot_general | solution.py:38
  223.7 12.3 copy.29
  236.0 26.4 %fusion.69 = f32[16,256,4,256]{1,3,2,0:T(8,128)} fusion(bf16[2304,4,256]{0,2,1:T(8,128)(2,1)} %copy.23, bf16[16,256,2304]{2,1,0:T(8,128)(2,1)} %param.13, f32[2304]{0:T(1024)S(1)} %convert_add_fusion.3, f32[16,256]{1,0:T(8,128)S(1)} %add_rsqrt_fusion.1), kind=kOutput, calls=%fused_computation.78 | convolution fusion | flops 19365101568 | bytes 40395776 | tf_op jit(solution)/shard_map/bcd,dhe->bche/dot_general | solution.py:36
  262.4 9.4 multiply_subtract_fusion.1
  271.9 7.7 maximum_convert_fusion
  279.6 12.3 copy.28
  291.9 8.5 fusion.55
  300.9 18.7 %pad_maximum_fusion.1 = (bf16[16,512,1024]{2,1,0:T(8,128)(2,1)}, bf16[16,512,1024]{2,1,0:T(8,128)(2,1)}) fusion(bf16[16,128,1024]{2,1,0:T(8,128)(2,1)S(1)} %broadcast.162, bf16[16,256,1024]{2,1,0:T(8,128)(2,1)} %copy.29, bf16[16,256,1024]{2,1,0:T(8,128)(2,1)} %copy.28), kind=kLoop, calls=%fused_computation.44 | loop fusion | flops 83886080 | bytes 54525952 | tf_op jit(solution)/shard_map/vmap()/concatenate | solution.py:77
  320.9 17.3 %broadcast_multiply_fusion = f32[16,4,256,2,256]{2,4,3,1,0:T(8,128)} fusion(f32[16,4,256,2]{2,3,1,0:T(2,128)S(1)} %get-tuple-element.41, bf16[16,128,4,256,1]{1,3,4,2,0:T(8,128)(2,1)} %bitcast.104, f32[16,4,256,2,128]{2,4,3,1,0:T(8,128)} %get-tuple-element.57, f32[16,4,256,2]{2,3,1,0:T(2,128)S(1)} %copy-done.2, pred[16,128]{1,0:T(8,128)(4,1)S(1)} %copy-done.5), kind=kOutput, calls=%fused_computation.57 | convolution fusion | flops 2172649472 | bytes 54790144 | tf_op jit(solution)/shard_map/bkcgs,bskd->bkcgd/dot_general | solution.py:47
  338.1 23.2 %pad_maximum_fusion = f32[16,4,256,2,257]{2,4,3,1,0:T(8,128)} fusion(f32[16,4,256,2,1]{2,4,3,1,0:T(1,128)S(1)} %copy.22, f32[16,4,256,2,256]{2,4,3,1,0:T(8,128)} %broadcast_multiply_fusion), kind=kLoop, calls=%fused_computation.33 | loop fusion | flops 8421376 | bytes 67371008 | tf_op jit(solution)/shard_map/concatenate | solution.py:102
  363.9 58.0 %while.3 = (s32[]{:T(128)}, bf16[16,512,1024]{2,1,0:T(8,128)(2,1)}, s32[16,3]{0,1:T(4,128)S(1)}, bf16[16,128,1024]{2,1,0:T(8,128)(2,1)}, s32[]{:T(128)}) while((s32[]{:T(128)}, bf16[16,512,1024]{2,1,0:T(8,128)(2,1)}, s32[16,3]{0,1:T(4,128)S(1)}, bf16[16,128,1024]{2,1,0:T(8,128)(2,1)}, s32[]{:T(128)}) %tuple.50), condition=%wide.while_cond.1, body=%wide.while_body.1.sunk | while | flops 2 | bytes 525429 | solution.py:78
  424.4 58.1 %while.2 = (s32[]{:T(128)}, bf16[16,512,1024]{2,1,0:T(8,128)(2,1)}, s32[16,3]{0,1:T(4,128)S(1)}, bf16[16,128,1024]{2,1,0:T(8,128)(2,1)}, s32[]{:T(128)}) while((s32[]{:T(128)}, bf16[16,512,1024]{2,1,0:T(8,128)(2,1)}, s32[16,3]{0,1:T(4,128)S(1)}, bf16[16,128,1024]{2,1,0:T(8,128)(2,1)}, s32[]{:T(128)}) %tuple.60), condition=%wide.while_cond, body=%wide.while_body.sunk | while | flops 2 | bytes 525429 | solution.py:78
  482.5 9.9 broadcast_select_fusion
  492.4 24.4 %select_reduce_fusion = (f32[16,4,256,2]{2,3,1,0:T(2,128)S(1)}, f32[16,4,256,2,256]{2,4,3,1,0:T(8,128)}) fusion(pred[256,256]{0,1:T(8,128)(4,1)S(1)} %copy-done.4, f32[16,256,4,2,128]{4,1,3,2,0:T(8,128)} %copy.18, f32[16,256,4,2,128]{4,1,3,2,0:T(8,128)} %copy.17, bf16[16,256,4,128]{1,3,2,0:T(8,128)(2,1)} %get-tuple-element.49, ...), kind=kOutput, calls=%fused_computation.41 | convolution fusion | flops 4353654784 | bytes 75694080 | tf_op jit(solution)/shard_map/bckgd,bjkd->bkcgj/dot_general | solution.py:106
  516.8 14.3 fusion.31
  531.1 403.5 %all-reduce.6.cloned.1.call-done = f32[16,4,256,2,257]{2,4,3,1,0:T(8,128)} async-done(((f32[16,4,256,2,257]{2,4,3,1,0:T(8,128)}), f32[16,4,256,2,257]{2,4,3,1,0:T(8,128)}) %all-reduce.6.cloned.1.call-update) | async-done | bytes 33685520 | tf_op jit(solution)/shard_map/psum | solution.py:103
  936.2 32.1 %fusion.26.clone.1.clone.4 = bf16[16,4,256,2,256]{2,4,3,1,0:T(8,128)(2,1)} fusion(f32[16,4,256,2,257]{2,4,3,1,0:T(8,128)} %all-reduce.6.cloned.1.call-done, f32[16,4,256,2,256]{2,4,3,1,0:T(8,128)} %get-tuple-element.59, f32[16,4,256,2]{2,3,1,0:T(2,128)S(1)} %get-tuple-element.37, ...), kind=kOutput, calls=%fused_computation.40.clone.clone.clone.clone.clone.1 | convolution fusion | flops 4370464768 | bytes 92864512 | tf_op jit(solution)/shard_map/bkcgs,bskd->bkcgd/dot_general | solution.py:47
  968.2 51.5 %fusion.19 = (f32[16,256]{1,0:T(8,128)S(1)}, bf16[16,256,2304]{2,1,0:T(8,128)(2,1)}) fusion(bf16[4,2,256,2304,1]{3,2,1,0,4:T(8,128)(2,1)} %bitcast.107, bf16[16,256,2304]{2,1,0:T(8,128)(2,1)} %param.13, bf16[16,4,256,2,256]{2,4,3,1,0:T(8,128)(2,1)} %fusion.26.clone.1.clone.4), kind=kOutput, calls=%fused_computation.29 | convolution fusion | flops 38711324672 | bytes 63979520 | tf_op jit(solution)/shard_map/bkcgd,kgde->bce/dot_general | solution.py:63
  1019.8 188.4 %fusion.11 = f32[16,256,9216]{2,1,0:T(8,128)} fusion(bf16[2304,9216]{1,0:T(8,128)(2,1)} %param.22, bf16[16,256,2304]{2,1,0:T(8,128)(2,1)} %get-tuple-element.61, f32[2304]{0:T(1024)S(1)} %copy-done.6, f32[16,256]{1,0:T(8,128)S(1)} %add_rsqrt_fusion), kind=kOutput, calls=%fused_computation.22 | convolution fusion | flops 173983924224 | bytes 212362240 | tf_op jit(solution)/shard_map/bcd,df->bcf/dot_general | solution.py:67
  1208.2 220.5 %fusion.8.clone.6 = bf16[16,256,9216]{2,1,0:T(8,128)(2,1)} fusion(f32[16,256,9216]{2,1,0:T(8,128)} %fusion.11, bf16[2304,9216]{1,0:T(8,128)(2,1)} %param.21, bf16[16,256,2304]{2,1,0:T(8,128)(2,1)} %get-tuple-element.61, f32[2304]{0:T(1024)S(1)} %copy-done.6, f32[16,256]{1,0:T(8,128)S(1)} %add_rsqrt_fusion), kind=kOutput, calls=%fused_computation.13.clone.clone.clone.clone.clone.1 | convolution fusion | flops 174361411584 | bytes 287859712 | tf_op jit(solution)/shard_map/bcd,df->bcf/dot_general | solution.py:66
  1428.6 190.4 %fusion.22 = bf16[16,256,2304]{2,1,0:T(8,128)(2,1)} fusion(bf16[16,256,2304]{2,1,0:T(8,128)(2,1)} %get-tuple-element.61, bf16[9216,2304]{1,0:T(8,128)(2,1)} %param.23, bf16[16,256,9216]{2,1,0:T(8,128)(2,1)} %fusion.8.clone.6), kind=kOutput, calls=%fused_computation.32 | convolution fusion | flops 173974487040 | bytes 155713536 | tf_op jit(solution)/shard_map/bcf,fd->bcd/dot_general | solution.py:69
  (143 shorter events, 135.8 us)
Async XLA Ops:
  7.2 312.5 %all-reduce.4.cloned.1.call-start = ((), (), s32[]{:S(2)}) async-start(), calls=%async_computation | async-start | bytes 262144 | tf_op jit(solution)/shard_map/pmax | solution.py:100
  46.2 49.6 %copy-start = (f32[16,256,128]{1,2,0:T(8,128)}, f32[16,256,128]{1,2,0:T(8,128)S(1)}, u32[]{:S(2)}) copy-start(f32[16,256,128]{1,2,0:T(8,128)S(1)} %get-tuple-element.53) | copy-start | bytes 6291460
  135.5 17.6 %copy-start.5 = (pred[16,128]{1,0:T(8,128)(4,1)S(1)}, pred[16,128]{1,0:T(8,128)(4,1)}, u32[]{:S(2)}) copy-start(pred[16,128]{1,0:T(8,128)(4,1)} %broadcast_compare_fusion) | copy-start | bytes 6148
  153.1 19.4 %copy-start.9 = (s32[16]{0:T(128)S(1)}, s32[16]{0:T(128)}, u32[]{:S(2)}) copy-start(s32[16]{0:T(128)} %param.14) | copy-start | bytes 196
  153.1 20.7 %copy-start.8 = (bf16[2304]{0:T(1024)(128)(2,1)S(1)}, bf16[2304]{0:T(1024)(128)(2,1)}, u32[]{:S(2)}) copy-start(bf16[2304]{0:T(1024)(128)(2,1)} %param.25) | copy-start | bytes 13828
  172.5 762.1 %all-reduce.6.cloned.1.call-start = ((), (), s32[]{:S(2)}) async-start(), calls=%async_computation.1 | async-start | bytes 69206016 | tf_op jit(solution)/shard_map/psum | solution.py:103
  236.0 26.5 %copy-start.1 = (f32[16,256,128]{1,2,0:T(8,128)S(1)}, f32[16,256,128]{1,2,0:T(8,128)}, u32[]{:S(2)}) copy-start(f32[16,256,128]{1,2,0:T(8,128)} %copy-done) | copy-start | bytes 6291460
  271.9 20.0 %copy-start.2 = (f32[16,4,256,2]{2,3,1,0:T(2,128)S(1)}, f32[16,4,256,2]{2,3,1,0:T(2,128)}, u32[]{:S(2)}) copy-start(f32[16,4,256,2]{2,3,1,0:T(2,128)} %get-tuple-element.56) | copy-start | bytes 393220
  361.3 121.2 %copy-start.7 = (pred[16,128]{1,0:T(8,128)(4,1)S(1)}, pred[16,128]{1,0:T(8,128)(4,1)}, u32[]{:S(2)}) copy-start(pred[16,128]{1,0:T(8,128)(4,1)} %fusion.81) | copy-start | bytes 6148
  421.9 70.5 %copy-start.4 = (pred[256,256]{0,1:T(8,128)(4,1)S(1)}, pred[256,256]{0,1:T(8,128)(4,1)}, u32[]{:S(2)}) copy-start(pred[256,256]{0,1:T(8,128)(4,1)} %iota_compare_fusion) | copy-start | bytes 196612
  516.8 419.1 %copy-start.3 = (f32[16,4,256,2]{2,3,1,0:T(2,128)S(1)}, f32[16,4,256,2]{2,3,1,0:T(2,128)}, u32[]{:S(2)}) copy-start(f32[16,4,256,2]{2,3,1,0:T(2,128)} %all-reduce.4.cloned.1.call-done) | copy-start | bytes 393220
  968.2 51.5 %copy-start.6 = (f32[2304]{0:T(1024)S(1)}, f32[2304]{0:T(1024)}, u32[]{:S(2)}) copy-start(f32[2304]{0:T(1024)} %convert_add_fusion.2) | copy-start | bytes 27652
Sparse Core Ops, SparseCore 0:
  172.6 28.9 all-reduce.3
  361.4 573.1 all-reduce.5
where the time goes:
time: 1640 us; the launch traced here: 1630 us
  matrix products  846 us (52%)
  waiting for transfers between devices  404 us (25%)
  local copies, waits for them, and re-layouts  227 us (14%)
  other arithmetic  135 us (8%)
    psum x1, waiting for transfers between devices, local_layer(): packed = lax.psum(packed, 'cp')  404 us
    dot_general x1, matrix products, finish_layer(): jnp.einsum('bcd,df->bcf', normed_mlp, w_gate, preferred_element_type=jnp....  220 us
    dot_general x1, matrix products, finish_layer(): jnp.einsum('bcf,fd->bcd', gated_mid, w_down, preferred_element_type=jnp.f...  190 us
    dot_general x1, matrix products, finish_layer(): jnp.einsum('bcd,df->bcf', normed_mlp, w_up, preferred_element_type=jnp.fl...  188 us
    gather x96, local copies, waits for them, and re-layouts  116 us
    dot_general x1, matrix products, finish_layer(): jnp.einsum('bkcgd,kgde->bce', attended, w_o_grp, preferred_element_type=j...  51.5 us
    dot_general x1, matrix products, project_chunk(): jnp.einsum('bcd,dhe->bche', normed, w_q, preferred_element_type=jnp.float32)  49.6 us
    dot_general x2, matrix products, partial_attend(): jnp.einsum('bkcgs,bskd->bkcgd', weights.astype(jnp.bfloat16), values, pre...  49.3 us
  transfers between devices with their start and end apart: 2, of which 1 were waited for; matrix products, arithmetic and copies ran while one was open for 19% of the time, Pallas kernels for 0%

commit v1 on v0

v1 whole, which is shorter than its diff:
```python
import functools

import jax
import jax.numpy as jnp
from jax import lax
from jax.experimental import pallas as pl
from jax.experimental.pallas import tpu as pltpu
from jax.sharding import PartitionSpec as P

NORM_EPS = 1e-6
ROPE_BASE = 1.0e4
MASK_FLOOR = -1.0e30
GELU_C = 0.7978845608028654

UNIT = 32
N_P1, N_P2, N_P3 = 2, 6, 18
FF_BLK = 768
F32 = jnp.float32
BF16 = jnp.bfloat16


def rms_norm(x, gain):
    inv = lax.rsqrt(jnp.mean(x * x, axis=-1, keepdims=True) + NORM_EPS)
    return (x * inv * (1.0 + gain)).astype(BF16)


def rotate(x, cos, sin):
    half = x.shape[-1] // 2
    first, second = x[:, :half], x[:, half:]
    return jnp.concatenate([first * cos - second * sin, second * cos + first * sin], axis=-1)


def gelu_tanh(x):
    return 0.5 * x * (1.0 + jnp.tanh(GELU_C * (x + 0.044715 * (x * x * x))))


def dot(a, b):
    return jnp.dot(a, b, preferred_element_type=F32)


def dot_t(a, b):
    return lax.dot_general(a, b, (((1,), (1,)), ((), ())), preferred_element_type=F32)


def pack_kernel(n_out, seq_ref, row_ref, ck_ref, cv_ref, *rest):
    outs = rest[: len(n_out)]
    raw, wide, in_sem, out_sem = rest[len(n_out):]
    total = sum(n_out)

    def in_copies(u):
        src = pl.ds(pl.multiple_of(row_ref[u], UNIT), UNIT)
        return (
            pltpu.make_async_copy(ck_ref.at[seq_ref[u], src, :], raw.at[u, 0], in_sem.at[u, 0]),
            pltpu.make_async_copy(cv_ref.at[seq_ref[u], src, :], raw.at[u, 1], in_sem.at[u, 1]),
        )

    @pl.loop(0, total)
    def _(u):
        for copy in in_copies(u):
            copy.start()

    base = 0
    for out, n in zip(outs, n_out):
        @pl.loop(0, n)
        def _(k, out=out, base=base):
            u = base + k
            for copy in in_copies(u):
                copy.wait()
            wide[u, :, :1024] = raw[u, 0].astype(F32)
            wide[u, :, 1024:] = raw[u, 1].astype(F32)
            pltpu.make_async_copy(wide.at[u], out.at[k], out_sem.at[u]).start()
        base += n
    base = 0
    for out, n in zip(outs, n_out):
        @pl.loop(0, n)
        def _(k, out=out, base=base):
            pltpu.make_async_copy(wide.at[base + k], out.at[k], out_sem.at[base + k]).wait()
        base += n


def pack_units(cache_k, cache_v, seqs, rows, n_out, name):
    total = sum(n_out)
    return pl.pallas_call(
        functools.partial(pack_kernel, n_out),
        out_shape=[jax.ShapeDtypeStruct((n, UNIT, 2048), F32) for n in n_out],
        grid_spec=pltpu.PrefetchScalarGridSpec(
            num_scalar_prefetch=2,
            grid=(),
            in_specs=[pl.BlockSpec(memory_space=pl.ANY)] * 2,
            out_specs=[pl.BlockSpec(memory_space=pl.ANY)] * len(n_out),
            scratch_shapes=[
                pltpu.VMEM((total, 2, UNIT, 1024), BF16),
                pltpu.VMEM((total, UNIT, 2048), F32),
                pltpu.SemaphoreType.DMA((total, 2)),
                pltpu.SemaphoreType.DMA((total,)),
            ],
        ),
        compiler_params=pltpu.CompilerParams(vmem_limit_bytes=48 * 2**20),
        cost_estimate=pl.CostEstimate(flops=100_000_000, bytes_accessed=total * UNIT * 2048 * 6, transcendentals=0),
        name=name,
    )(seqs, rows, cache_k, cache_v)


def blank_kernel(*refs):
    pass


def blank(n, count):
    return pl.pallas_call(
        blank_kernel,
        out_shape=[jax.ShapeDtypeStruct((n, UNIT, 2048), F32)] * count,
        out_specs=[pl.BlockSpec(memory_space=pl.ANY)] * count,
        name="blank",
    )()


def layer_kernel(n_ff, n_pieces, sc_ref, h_ref, ga_ref, gm_ref, cos_ref, sin_ref, wq_ref, wk_ref, wv_ref, wo_ref,
                 wg_ref, wu_ref, wd_ref, ck_ref, cv_ref, sib_ref, full_ref, fullf_ref, *rest):
    pieces = rest[: 2 * n_pieces]
    out_ref, act, acc, stage, hist, sem, own_sem = rest[2 * n_pieces:]
    step = pl.program_id(0)
    x_pos, core = sc_ref[2], sc_ref[3]
    start = sc_ref[1]
    per_half = 128 // UNIT
    piece_base = (0, N_P1, N_P1 + N_P2, N_P1 + N_P2 + N_P3)

    def unit_copies(hh, u):
        k = hh * per_half + u
        dst = stage.at[pl.ds(pl.multiple_of(k * UNIT, UNIT), UNIT), :]
        live = u < sc_ref[9 + hh]
        far = x_pos == 1
        direct = core == hh
        ovf = sc_ref[4] == 1
        pos = sc_ref[7 + hh] + u
        out = [
            (live & (x_pos == 0) & (core != hh), sib_ref.at[sc_ref[5] * per_half + u]),
            (live & far & ovf & direct, full_ref.at[sc_ref[6] * per_half + u]),
            (live & far & ovf & jnp.logical_not(direct), fullf_ref.at[sc_ref[6] * per_half + u]),
        ]
        for p in range(n_pieces):
            here = live & far & jnp.logical_not(ovf) & (pos >= piece_base[p]) & (pos < piece_base[p + 1])
            idx = jnp.clip(pos - piece_base[p], 0, piece_base[p + 1] - piece_base[p] - 1)
            out.append((here & direct, pieces[2 * p].at[idx]))
            out.append((here & jnp.logical_not(direct), pieces[2 * p + 1].at[idx]))
        return [(c, pltpu.make_async_copy(src, dst, sem.at[k])) for c, src in out]

    def own_copies(hh):
        rows = pl.ds(hh * 128, 128)
        return (
            pltpu.make_async_copy(ck_ref.at[sc_ref[0]], hist.at[rows, pl.ds(0, 1024)], own_sem.at[0]),
            pltpu.make_async_copy(cv_ref.at[sc_ref[0]], hist.at[rows, pl.ds(1024, 1024)], own_sem.at[1]),
        )

    @pl.when(step == 0)
    def _():
        for hh in range(2):
            @pl.loop(0, per_half)
            def _(u, hh=hh):
                for cond, copy in unit_copies(hh, u):
                    @pl.when(cond)
                    def _(copy=copy):
                        copy.start()

            @pl.when((x_pos == 0) & (core == hh))
            def _(hh=hh):
                for copy in own_copies(hh):
                    copy.start()
        act[...] = rms_norm(h_ref[0].astype(F32), ga_ref[...].astype(F32))
        acc[...] = jnp.zeros_like(acc)
        for hh in range(2):
            @pl.loop(0, per_half)
            def _(u, hh=hh):
                for cond, copy in unit_copies(hh, u):
                    @pl.when(cond)
                    def _(copy=copy):
                        copy.wait()

            @pl.when((x_pos == 0) & (core == hh))
            def _(hh=hh):
                for copy in own_copies(hh):
                    copy.wait()

            @pl.when((x_pos == 1) | (core != hh))
            def _(hh=hh):
                hist[hh * 128:(hh + 1) * 128, :] = stage[hh * 128:(hh + 1) * 128, :].astype(BF16)

    @pl.when(step < 4)
    def _():
        cos, sin = cos_ref[0], sin_ref[0]
        a = act[...]
        k_new = rotate(dot(a, wk_ref[0]), cos, sin).astype(BF16)
        v_new = dot(a, wv_ref[0]).astype(BF16)
        off = pl.multiple_of(step * 256, 256)
        k_old = hist[:, pl.ds(off, 256)]
        row = lax.broadcasted_iota(jnp.int32, (256, 256), 0)
        col = lax.broadcasted_iota(jnp.int32, (256, 256), 1)
        v_old = jnp.where(row < start, hist[:, pl.ds(off + 1024, 256)], jnp.zeros((), BF16))
        old_ok = col < start
        new_ok = col <= row
        heads = []
        for j in range(2):
            q = (rotate(dot(a, wq_ref[j]), cos, sin) * 0.0625).astype(BF16)
            s_old = jnp.where(old_ok, dot_t(q, k_old), MASK_FLOOR)
            s_new = jnp.where(new_ok, dot_t(q, k_new), MASK_FLOOR)
            top = jnp.maximum(jnp.max(s_old, axis=-1, keepdims=True), jnp.max(s_new, axis=-1, keepdims=True))
            p_old = jnp.where(old_ok, jnp.exp(s_old - top), 0.0)
            p_new = jnp.where(new_ok, jnp.exp(s_new - top), 0.0)
            den = jnp.sum(p_old, axis=-1, keepdims=True) + jnp.sum(p_new, axis=-1, keepdims=True)
            num = dot(p_old.astype(BF16), v_old) + dot(p_new.astype(BF16), v_new)
            heads.append((num / den).astype(BF16))
        acc[...] += dot(jnp.concatenate(heads, axis=-1), wo_ref[...])

    @pl.when(step == 3)
    def _():
        res = (h_ref[0].astype(F32) + acc[...]).astype(BF16).astype(F32)
        act[...] = rms_norm(res, gm_ref[...].astype(F32))
        acc[...] = res

    @pl.when(step >= 4)
    def _():
        c = act[...]
        mid = (gelu_tanh(dot(c, wg_ref[...])) * dot(c, wu_ref[...])).astype(BF16)
        acc[...] += dot(mid, wd_ref[...])

    @pl.when(step == n_ff + 3)
    def _():
        out_ref[...] = acc[...].astype(BF16).astype(F32)


def run_layer(slot, scalars, hidden, ga, gm, cos, sin, wq, wk, wv, wo, wg, wu, wd, ck, cv, sib, full, fullf, pieces):
    n_ff = wg.shape[1] // FF_BLK
    n_pieces = len(pieces) // 2
    att = lambda i, *_: jnp.minimum(i, 3)
    ffn = lambda i, *_: jnp.clip(i - 4, 0, n_ff - 1)
    one = pl.Buffered(1)
    any_spec = pl.BlockSpec(memory_space=pl.ANY)
    d = hidden.shape[2]
    flops = 2 * 256 * d * (2048 * 2 + 1024 * 2 + 3 * wg.shape[1]) + 1_100_000_000
    return pl.pallas_call(
        functools.partial(layer_kernel, n_ff, n_pieces),
        out_shape=jax.ShapeDtypeStruct((256, d), F32),
        grid_spec=pltpu.PrefetchScalarGridSpec(
            num_scalar_prefetch=1,
            grid=(n_ff + 4,),
            in_specs=[
                pl.BlockSpec((1, 256, d), lambda i, sc: (sc[0], 0, 0), pipeline_mode=one),
                pl.BlockSpec((1, d), lambda i, sc: (0, 0), pipeline_mode=one),
                pl.BlockSpec((1, d), lambda i, sc: (0, 0), pipeline_mode=one),
                pl.BlockSpec((1, 256, 128), lambda i, sc: (slot, 0, 0), pipeline_mode=one),
                pl.BlockSpec((1, 256, 128), lambda i, sc: (slot, 0, 0), pipeline_mode=one),
                pl.BlockSpec((2, d, 256), lambda i, sc: (att(i), 0, 0)),
                pl.BlockSpec((1, d, 256), lambda i, sc: (att(i), 0, 0)),
                pl.BlockSpec((1, d, 256), lambda i, sc: (att(i), 0, 0)),
                pl.BlockSpec((512, d), lambda i, sc: (att(i), 0)),
                pl.BlockSpec((d, FF_BLK), lambda i, sc: (0, ffn(i))),
                pl.BlockSpec((d, FF_BLK), lambda i, sc: (0, ffn(i))),
                pl.BlockSpec((FF_BLK, d), lambda i, sc: (ffn(i), 0)),
            ] + [any_spec] * (5 + 2 * n_pieces),
            out_specs=pl.BlockSpec((256, d), lambda i, sc: (0, 0), pipeline_mode=one),
            scratch_shapes=[
                pltpu.VMEM((256, d), BF16),
                pltpu.VMEM((256, d), F32),
                pltpu.VMEM((256, 2048), F32),
                pltpu.VMEM((256, 2048), BF16),
                pltpu.SemaphoreType.DMA((8,)),
                pltpu.SemaphoreType.DMA((2,)),
            ],
        ),
        compiler_params=pltpu.CompilerParams(vmem_limit_bytes=62 * 2**20),
        cost_estimate=pl.CostEstimate(flops=flops, bytes_accessed=160_000_000, transcendentals=0),
        name=f"layer_{slot}",
    )(scalars, hidden, ga, gm, cos, sin, wq, wk, wv, wo, wg, wu, wd, ck, cv, sib, full, fullf, *pieces)


def window_kernel(sc_ref, h_ref, ga_ref, cos_ref, sin_ref, wk_ref, wv_ref, ck_ref, cv_ref, ok_ref, ov_ref):
    step = pl.program_id(0)
    lo = sc_ref[16]
    a_rows, inside = [], []
    for j in range(2):
        first = lo - sc_ref[2 * step + j]
        want = first + lax.broadcasted_iota(jnp.int32, (128, 256), 0)
        have = lax.broadcasted_iota(jnp.int32, (128, 256), 1)
        pick = jnp.where(want == have, 1.0, 0.0).astype(BF16)
        a_rows.append(dot(pick, h_ref[j]))
        idx = first + lax.broadcasted_iota(jnp.int32, (128, 256), 0)
        inside.append((idx >= 0) & (idx < 256))
    a = rms_norm(jnp.concatenate(a_rows, axis=0), ga_ref[...].astype(F32))
    cos = jnp.concatenate([cos_ref[...]] * 2, axis=0)
    sin = jnp.concatenate([sin_ref[...]] * 2, axis=0)
    for g in range(4):
        k = rotate(dot(a, wk_ref[g]), cos, sin).astype(BF16)
        v = dot(a, wv_ref[g]).astype(BF16)
        cols = slice(g * 256, (g + 1) * 256)
        for j in range(2):
            rows = slice(j * 128, (j + 1) * 128)
            ok_ref[j, :, cols] = jnp.where(inside[j], k[rows], ck_ref[j, :, cols])
            ov_ref[j, :, cols] = jnp.where(inside[j], v[rows], cv_ref[j, :, cols])


def write_windows(scalars, hidden, ga, cos, sin, wk, wv, cache_k, cache_v):
    n_seq, rows, width = cache_k.shape
    d = hidden.shape[2]
    one = pl.Buffered(1)
    cache_spec = pl.BlockSpec((2, rows, width), lambda i, sc: (i, 0, 0))
    return pl.pallas_call(
        window_kernel,
        out_shape=[jax.ShapeDtypeStruct(cache_k.shape, BF16)] * 2,
        grid_spec=pltpu.PrefetchScalarGridSpec(
            num_scalar_prefetch=1,
            grid=(n_seq // 2,),
            in_specs=[
                pl.BlockSpec((2, 256, d), lambda i, sc: (i, 0, 0)),
                pl.BlockSpec((1, d), lambda i, sc: (0, 0), pipeline_mode=one),
                pl.BlockSpec((rows, 128), lambda i, sc: (0, 0), pipeline_mode=one),
                pl.BlockSpec((rows, 128), lambda i, sc: (0, 0), pipeline_mode=one),
                pl.BlockSpec((4, d, 256), lambda i, sc: (0, 0, 0), pipeline_mode=one),
                pl.BlockSpec((4, d, 256), lambda i, sc: (0, 0, 0), pipeline_mode=one),
                cache_spec,
                cache_spec,
            ],
            out_specs=[cache_spec, cache_spec],
        ),
        compiler_params=pltpu.CompilerParams(vmem_limit_bytes=56 * 2**20),
        cost_estimate=pl.CostEstimate(flops=2 * n_seq * rows * d * 2 * width, bytes_accessed=60_000_000, transcendentals=0),
        name="cache_window",
    )(scalars, hidden, ga, cos, sin, wk, wv, cache_k, cache_v)


def place_kernel(seq_ref, own_ref, sib_ref, crs_ref, dia_ref, *rest):
    out_ref = rest[-1]
    src = pl.program_id(0)
    for k, ref in enumerate((own_ref, sib_ref, crs_ref, dia_ref)):
        @pl.when(src == k)
        def _(ref=ref):
            out_ref[0] = ref[...].astype(BF16)


def place_rows(seqs, parts, out, n_seq, slot):
    rows, d = parts[0].shape
    n_blk = 2
    blk = rows // n_blk

    def part_map(k):
        def index(src, b, sq):
            return (jnp.where(src == k, b, jnp.where(src < k, 0, n_blk - 1)), 0)
        return index

    in_specs = [pl.BlockSpec((blk, d), part_map(k)) for k in range(4)]
    args = [seqs, *parts]
    aliases = {}
    if out is not None:
        in_specs.append(pl.BlockSpec(memory_space=pl.ANY))
        aliases = {5: 0}
        args.append(out)
    return pl.pallas_call(
        place_kernel,
        out_shape=jax.ShapeDtypeStruct((n_seq, rows, d), BF16),
        grid_spec=pltpu.PrefetchScalarGridSpec(
            num_scalar_prefetch=1,
            grid=(4, n_blk),
            in_specs=in_specs,
            out_specs=pl.BlockSpec((1, blk, d), lambda src, b, sq: (sq[src], b, 0)),
        ),
        input_output_aliases=aliases,
        cost_estimate=pl.CostEstimate(flops=10_000_000, bytes_accessed=4 * rows * d * 6, transcendentals=0),
        name=f"place_{slot}",
    )(*args)


def solution(mesh):
    d2d = [(0, 1), (1, 0), (2, 3), (3, 2)]
    cross = [(0, 2), (1, 3), (2, 0), (3, 1)]

    def local_layer(hidden, start_pos, cache_k, cache_v, w_q, w_k, w_v, w_o, w_gate, w_up, w_down, norm_attn, norm_mlp):
        n_seq, chunk_len, d = hidden.shape
        shard_len = cache_k.shape[1]
        i32 = jnp.int32
        me = lax.axis_index('cp').astype(i32)
        x_pos, core = me // 2, me % 2
        per_half = shard_len // UNIT

        sid = jnp.arange(n_seq, dtype=i32)
        before = (start_pos[None, :] < start_pos[:, None]) | (
            (start_pos[None, :] == start_pos[:, None]) & (sid[None, :] < sid[:, None]))
        rank = jnp.sum(before.astype(i32), axis=1)
        onehot = (rank[None, :] == sid[:, None]).astype(i32)
        order = jnp.sum(onehot * sid[None, :], axis=1)
        length = jnp.sum(onehot * start_pos[None, :], axis=1)

        slot = jnp.arange(4, dtype=i32)
        src_x = jnp.stack([x_pos, x_pos, 1 - x_pos, 1 - x_pos])[:, None]
        src_c = jnp.stack([core, 1 - core, core, 1 - core])[:, None]
        idx8 = 2 * slot[None, :] + ((src_c + slot[None, :]) % 2)
        ranks = 8 * (1 - src_x) + idx8
        pick = (ranks[:, :, None] == sid[None, None, :]).astype(i32)
        seq_tbl = jnp.sum(pick * order[None, None, :], axis=-1)
        my_len = jnp.sum(pick[0] * length[None, :], axis=-1)

        halves = jnp.arange(2, dtype=i32)[:, None]
        cnt = jnp.clip((length[None, :8] - halves * shard_len + UNIT - 1) // UNIT, 0, per_half)
        ends = jnp.cumsum(cnt, axis=1) + halves * N_P1
        pos = ends - cnt
        over = (ends[0, 7] > N_P1 + N_P2 + N_P3) | (ends[1, 7] > N_P1 + N_P2) | (ends[0, 1] > N_P1) | (ends[1, 1] > N_P1)
        over = lax.pmax(over.astype(i32), ('dp', 'cp'))

        my_cnt8 = jnp.clip((my_len[None, :] - halves * shard_len + UNIT - 1) // UNIT, 0, per_half)
        pick8 = (idx8[0][:, None] == jnp.arange(8, dtype=i32)[None, :]).astype(i32)
        my_pos = jnp.sum(pick8[None] * pos[:, None, :], axis=-1)
        scal = jnp.stack([
            seq_tbl[0], my_len, jnp.broadcast_to(x_pos, (4,)), jnp.broadcast_to(core, (4,)),
            jnp.broadcast_to(over, (4,)), slot, idx8[0], my_pos[0], my_pos[1], my_cnt8[0], my_cnt8[1],
        ], axis=1)

        def pick_order(rk):
            return jnp.sum((rk[:, None] == sid[None, :]).astype(i32) * order[None, :], axis=-1)

        my_ends = jnp.where(core == 0, ends[0], ends[1])
        my_start = jnp.where(core == 0, pos[0], pos[1])
        p_all = jnp.arange(N_P1 + N_P2 + N_P3, dtype=i32)
        p_rank = jnp.minimum(jnp.sum((my_ends[None, :] <= p_all[:, None]).astype(i32), axis=1), 7)
        p_first = jnp.sum((p_rank[:, None] == jnp.arange(8, dtype=i32)[None, :]).astype(i32) * my_start[None, :], axis=1)
        p_unit = jnp.clip(p_all - p_first, 0, per_half - 1)
        b_all = jnp.arange(4 * per_half, dtype=i32)
        b_slot = b_all // per_half
        b_rank = 8 + 2 * b_slot + ((1 - core + b_slot) % 2)
        pack_seq = jnp.concatenate([pick_order(p_rank), pick_order(b_rank)])
        pack_row = jnp.concatenate([p_unit, b_all % per_half]) * UNIT
        p1, p2, p3, sib_src = pack_units(cache_k, cache_v, pack_seq, pack_row, (N_P1, N_P2, N_P3, 4 * per_half), "pack")
        p1d = lax.ppermute(p1, 'cp', [(0, 2)])
        sib = lax.ppermute(sib_src, 'cp', [(0, 1), (1, 0)])
        p1f = lax.ppermute(p1d, 'cp', [(2, 3)])
        p2d = lax.ppermute(p2, 'cp', [(0, 2), (1, 3)])
        p2f = lax.ppermute(p2d, 'cp', [(2, 3), (3, 2)])
        p3d = lax.ppermute(p3, 'cp', [(0, 2)])
        p3f = lax.ppermute(p3d, 'cp', [(2, 3)])

        def send_all(_):
            f_all = jnp.arange(8 * per_half, dtype=i32)
            (everything,) = pack_units(cache_k, cache_v, pick_order(f_all // per_half), (f_all % per_half) * UNIT,
                                       (8 * per_half,), "pack_full")
            got = lax.ppermute(everything, 'cp', [(0, 2), (1, 3)])
            return got, lax.ppermute(got, 'cp', [(2, 3), (3, 2)])

        full, full_f = lax.cond(over > 0, send_all, lambda _: tuple(blank(8 * per_half, 2)), 0)

        head_dim = w_q.shape[2]
        inv_freq = ROPE_BASE ** (-2.0 * jnp.arange(head_dim // 2, dtype=F32) / head_dim)
        own_pos = my_len[:, None] + jnp.arange(chunk_len, dtype=i32)[None, :]
        angles = own_pos.astype(F32)[:, :, None] * inv_freq
        cos, sin = jnp.cos(angles), jnp.sin(angles)
        win_lo = me * shard_len
        win_angles = (win_lo + jnp.arange(shard_len, dtype=i32)).astype(F32)[:, None] * inv_freq
        win_cos, win_sin = jnp.cos(win_angles), jnp.sin(win_angles)
        wq = w_q.transpose(1, 0, 2)
        wk = w_k.transpose(1, 0, 2)
        wv = w_v.transpose(1, 0, 2)
        wo = w_o.reshape(-1, d)
        ga, gm = norm_attn[None, :], norm_mlp[None, :]

        out = None
        parts = []
        for t in range(4):
            pieces = (p1d, p1f) if t == 0 else (p1d, p1f, p2d, p2f, p3d, p3f)
            own = run_layer(t, scal[t], hidden, ga, gm, cos, sin, wq, wk, wv, wo, w_gate, w_up, w_down,
                            cache_k, cache_v, sib, full, full_f, pieces)
            crs = lax.ppermute(own, 'cp', cross)
            near = lax.ppermute(own, 'cp', d2d)
            dia = lax.ppermute(crs, 'cp', d2d)
            parts.append((own, near, crs, dia))
        new_k, new_v = write_windows(jnp.concatenate([start_pos, win_lo[None]]), hidden, ga, win_cos, win_sin, wk, wv,
                                     cache_k, cache_v)
        for t in range(4):
            out = place_rows(seq_tbl[:, t], parts[t], out, n_seq, t)
        return out, new_k, new_v

    group_spec = P('dp', None, None)
    cache_spec = P('dp', 'cp', None)
    whole_spec = P()
    return jax.shard_map(
        local_layer,
        mesh=mesh,
        in_specs=(group_spec, P('dp'), cache_spec, cache_spec) + (whole_spec,) * 9,
        out_specs=(group_spec, cache_spec, cache_spec),
        check_vma=False,
    )
```

time: 1640 us -> 620 us (0.38)
  matrix products: 846 us -> 0 us
  Pallas kernels: 0 us -> 360 us
  waiting for transfers between devices: 404 us -> 100 us
  local copies, waits for them, and re-layouts: 227 us -> 26.1 us
  other arithmetic: 135 us -> 8.2 us
  blocking collectives: 0 us -> 89 us
  starting transfers between devices: 0.08 us -> 24.9 us
    dot_general x11 -> x0, matrix products: 846 us -> none  [the longest x1 220 us: finish_layer(): jnp.einsum('bcd,df->bcf', normed_mlp, w_gate, preferred_element_type=jnp....]
    psum x1 -> x0, waiting for transfers between devices: 404 us -> none  [local_layer(): packed = lax.psum(packed, 'cp')]
    pallas_call x0 -> x11, Pallas kernels: none -> 360 us  [the longest x4 281 us: run_layer(): pl.pallas_call(functools.partial(layer_kernel, n_ff, n_pieces), out_shape...]
    gather x96 -> x0, local copies, waits for them, and re-layouts: 116 us -> none
    ppermute x0 -> x19, waiting for transfers between devices: none -> 100 us  [the longest x4 96.9 us: local_layer(): crs = lax.ppermute(own, 'cp', cross)]
    pmax x0 -> x1, blocking collectives: none -> 89 us  [local_layer(): over = lax.pmax(over.astype(i32), ('dp', 'cp'))]
    concatenate x2, other arithmetic: 41.9 us -> 0.68 us  [the longest x1 0.61 us: local_layer(): jnp.concatenate([start_pos, win_lo[None]])]
    concatenate x2 -> x0, local copies, waits for them, and re-layouts: 35.2 us -> none  [rotate(): jnp.concatenate([first * cos_tab - second * sin_tab, second * cos_tab + f...]
  transfers between devices with their start and end apart: 2 -> 19, of which waited for: 1 -> 3; matrix products, arithmetic and copies ran while one was open for 19% -> 5% of each run, Pallas kernels for 0% -> 56%
where the time goes in v1:
time: 620 us; the launch traced here: 613 us
  Pallas kernels  360 us (58%)
  waiting for transfers between devices  100 us (16%)
  blocking collectives  89 us (14%)
  local copies, waits for them, and re-layouts  26.1 us (4%)
  starting transfers between devices  24.9 us (4%)
  other arithmetic  8.2 us (1%)
    pallas_call x4, Pallas kernels, run_layer(): pl.pallas_call(functools.partial(layer_kernel, n_ff, n_pieces), out_shape...  281 us
    ppermute x4, waiting for transfers between devices, local_layer(): crs = lax.ppermute(own, 'cp', cross)  96.9 us
    pmax x1, blocking collectives, local_layer(): over = lax.pmax(over.astype(i32), ('dp', 'cp'))  89 us
    pallas_call x4, Pallas kernels, place_rows(): pl.pallas_call(place_kernel, out_shape=jax.ShapeDtypeStruct((n_seq, rows,...  39.5 us
    pallas_call x1, Pallas kernels, write_windows(): pl.pallas_call(window_kernel, out_shape=[jax.ShapeDtypeStruct(cache_k.sha...  31.9 us
    unnamed x23, local copies, waits for them, and re-layouts  12.8 us
  transfers between devices with their start and end apart: 19, of which 3 were waited for; matrix products, arithmetic and copies ran while one was open for 5% of the time, Pallas kernels for 56%

profile of v1, /device:TPU:0, one launch (start us, length us, event | category | flops | bytes accessed | tf_op | source)
XLA Modules:
  0.0 613.2 jit_solution(16234045754718660655)
XLA Ops:
  0.7 0.9 convert_reduce_fusion
  1.6 0.8 select_reduce_fusion.3
  3.4 7.8 %pack.1 = (f32[2,32,2048]{2,1,0:T(8,128)S(1)}, f32[6,32,2048]{2,1,0:T(8,128)S(1)}, f32[18,32,2048]{2,1,0:T(8,128)}, f32[16,32,2048]{2,1,0:T(8,128)}) custom-call(s32[42]{0:T(128)S(1)} %pad_add_fusion.1.seq_ref, s32[42]{0:T(128)S(1)} %add_multiply_fusion.row_ref, bf16[16,128,1024]{2,1,0:T(8,128)(2,1)} %ck_ref.11, bf16[16,128,1024]{2,1,0:T(8,128)(2,1)} %cv_ref.11), custom_call_target="tpu_custom_call" | custom-call | flops 100000000 | bytes 16515072 | tf_op jit(solution)/shard_map/pack/pallas_call | solution.py:83
  11.1 7.5 %collective-permute-start.7 = (f32[18,32,2048]{2,1,0:T(8,128)}, f32[18,32,2048]{2,1,0:T(8,128)}, u32[]{:S(2)}, u32[]{:S(2)}) collective-permute-start(f32[18,32,2048]{2,1,0:T(8,128)} %get-tuple-element.28), channel_id=1, source_target_pairs={{0,2},{4,6}} | collective-permute-start | bytes 14155784 | tf_op jit(solution)/shard_map/ppermute | solution.py:434
  18.6 1.9 collective-permute-start.2
  20.5 1.3 collective-permute-start.3
  21.9 2.4 collective-permute-start.5
  25.3 8.6 %copy_bitcast_fusion.1 = (bf16[4,2304,256]{2,1,0:T(8,128)(2,1)}, bf16[4,2304,256]{2,1,0:T(8,128)(2,1)}) fusion(bf16[2304,4,256]{2,1,0:T(4,128)(2,1)} %param.21, bf16[2304,4,256]{2,1,0:T(4,128)(2,1)} %param.20), kind=kLoop, calls=%fused_computation.8 | loop fusion | bytes 18874368 | tf_op jit(solution)/shard_map/transpose | solution.py:456
  37.1 89.0 %pmax.7 = s32[]{:T(128)} all-reduce(s32[]{:T(128)} %bitcast.7), channel_id=1, replica_groups=mesh['dp'=2,'cp'=4] {'dp','cp'}, use_global_device_ids=true, to_apply=%region_6.7 | all-reduce | flops 1 | bytes 8 | tf_op jit(solution)/shard_map/pmax | solution.py:404
  130.7 9.4 %copy.58 = bf16[2304,8,256]{2,0,1:T(8,128)(2,1)} copy(bf16[2304,8,256]{2,1,0:T(8,128)(2,1)} %param.19) | data formatting | bytes 18874368 | tf_op args[4]
  140.2 3.0 multiply_sine_fusion
  143.2 3.0 collective-permute-start.8
  146.3 0.8 copy-done.4
  147.1 69.9 %layer_0.1.own_ref = f32[256,2304]{1,0:T(8,128)} custom-call(s32[11]{0:T(128)} %get-tuple-element.41.sc_ref, bf16[16,256,2304]{2,1,0:T(8,128)(2,1)} %h_ref.9, bf16[1,2304]{1,0:T(2,128)(2,1)} %broadcast_in_dim.6.ga_ref, bf16[1,2304]{1,0:T(2,128)(2,1)} %broadcast_in_dim.7.gm_ref, f32[4,256,128]{2,1,0:T(8,128)} %get-tuple-element.40.cos_ref, ...), custom_call_target="tpu_custom_call" | custom-call | flops 40962666496 | bytes 160000000 | tf_op jit(solution)/shard_map/layer_0/pallas_call | solution.py:239
  217.0 3.5 collective-permute-start.19
  220.4 1.3 collective-permute-start.6
  221.7 47.9 %collective-permute-done.19.crs_ref = f32[256,2304]{1,0:T(8,128)} collective-permute-done((f32[256,2304]{1,0:T(8,128)}, f32[256,2304]{1,0:T(8,128)}, u32[]{:S(2)}, u32[]{:S(2)}) %collective-permute-start.19) | collective-permute-done | bytes 2359328 | tf_op jit(solution)/shard_map/ppermute | solution.py:466
  269.6 1.1 copy-done.2
  270.7 70.3 %layer_3.1.own_ref = f32[256,2304]{1,0:T(8,128)} custom-call(s32[11]{0:T(128)} %get-tuple-element.44.sc_ref, bf16[16,256,2304]{2,1,0:T(8,128)(2,1)} %h_ref.9, bf16[1,2304]{1,0:T(2,128)(2,1)} %broadcast_in_dim.6.ga_ref, bf16[1,2304]{1,0:T(2,128)(2,1)} %broadcast_in_dim.7.gm_ref, f32[4,256,128]{2,1,0:T(8,128)} %get-tuple-element.40.cos_ref, ...), custom_call_target="tpu_custom_call" | custom-call | flops 40962666496 | bytes 160000000 | tf_op jit(solution)/shard_map/layer_3/pallas_call | solution.py:239
  341.3 70.4 %layer_2.1.own_ref = f32[256,2304]{1,0:T(8,128)} custom-call(s32[11]{0:T(128)} %get-tuple-element.43.sc_ref, bf16[16,256,2304]{2,1,0:T(8,128)(2,1)} %h_ref.9, bf16[1,2304]{1,0:T(2,128)(2,1)} %broadcast_in_dim.6.ga_ref, bf16[1,2304]{1,0:T(2,128)(2,1)} %broadcast_in_dim.7.gm_ref, f32[4,256,128]{2,1,0:T(8,128)} %get-tuple-element.40.cos_ref, ...), custom_call_target="tpu_custom_call" | custom-call | flops 40962666496 | bytes 160000000 | tf_op jit(solution)/shard_map/layer_2/pallas_call | solution.py:239
  411.7 1.8 collective-permute-start.13
  413.5 70.6 %layer_1.1.own_ref = f32[256,2304]{1,0:T(8,128)} custom-call(s32[11]{0:T(128)} %get-tuple-element.42.sc_ref, bf16[16,256,2304]{2,1,0:T(8,128)(2,1)} %h_ref.9, bf16[1,2304]{1,0:T(2,128)(2,1)} %broadcast_in_dim.6.ga_ref, bf16[1,2304]{1,0:T(2,128)(2,1)} %broadcast_in_dim.7.gm_ref, f32[4,256,128]{2,1,0:T(8,128)} %get-tuple-element.40.cos_ref, ...), custom_call_target="tpu_custom_call" | custom-call | flops 40962666496 | bytes 160000000 | tf_op jit(solution)/shard_map/layer_1/pallas_call | solution.py:239
  485.1 3.4 collective-permute-done.15.sib_ref
  488.7 49.0 %collective-permute-done.16.crs_ref = f32[256,2304]{1,0:T(8,128)} collective-permute-done((f32[256,2304]{1,0:T(8,128)}, f32[256,2304]{1,0:T(8,128)}, u32[]{:S(2)}, u32[]{:S(2)}) %collective-permute-start.16) | collective-permute-done | bytes 2359328 | tf_op jit(solution)/shard_map/ppermute | solution.py:466
  538.4 0.8 slice_reduce_fusion
  539.1 1.0 multiply_sine_fusion.1
  540.1 31.9 %cache_window.1 = (bf16[16,128,1024]{2,1,0:T(8,128)(2,1)}, bf16[16,128,1024]{2,1,0:T(8,128)(2,1)}) custom-call(s32[17]{0:T(128)} %pad_add_fusion.2.sc_ref, bf16[16,256,2304]{2,1,0:T(8,128)(2,1)} %h_ref.9, bf16[1,2304]{1,0:T(2,128)(2,1)} %broadcast_in_dim.6.ga_ref, f32[128,128]{1,0:T(8,128)} %get-tuple-element.48.cos_ref, ...), custom_call_target="tpu_custom_call" | custom-call | flops 19327352832 | bytes 60000000 | tf_op jit(solution)/shard_map/cache_window/pallas_call | solution.py:305
  571.9 9.9 %place_0.1.rest_0_ = bf16[16,256,2304]{2,1,0:T(8,128)(2,1)} custom-call(s32[4]{0:T(128)} %get-tuple-element.31.seq_ref, f32[256,2304]{1,0:T(8,128)} %layer_0.1.own_ref, f32[256,2304]{1,0:T(8,128)} %collective-permute-done.18.sib_ref, f32[256,2304]{1,0:T(8,128)} %collective-permute-done.19.crs_ref, f32[256,2304]{1,0:T(8,128)} %collective-permute-done.20.dia_ref), custom_call_target="tpu_custom_call" | custom-call | flops 10000000 | bytes 14155776 | tf_op jit(solution)/shard_map/place_0/pallas_call | solution.py:355
  581.8 9.9 %place_1.1.rest_0_ = bf16[16,256,2304]{2,1,0:T(8,128)(2,1)} custom-call(s32[4]{0:T(128)} %get-tuple-element.32.seq_ref, f32[256,2304]{1,0:T(8,128)} %layer_1.1.own_ref, f32[256,2304]{1,0:T(8,128)} %collective-permute-done.15.sib_ref, f32[256,2304]{1,0:T(8,128)} %collective-permute-done.16.crs_ref, ...), custom_call_target="tpu_custom_call", output_to_operand_aliasing={{}: (5, {})} | custom-call | flops 10000000 | bytes 14155776 | tf_op jit(solution)/shard_map/place_1/pallas_call | solution.py:355
  591.7 9.9 %place_2.1.rest_0_ = bf16[16,256,2304]{2,1,0:T(8,128)(2,1)} custom-call(s32[4]{0:T(128)} %get-tuple-element.33.seq_ref, f32[256,2304]{1,0:T(8,128)} %layer_2.1.own_ref, f32[256,2304]{1,0:T(8,128)} %collective-permute-done.12.sib_ref, f32[256,2304]{1,0:T(8,128)} %collective-permute-done.13.crs_ref, ...), custom_call_target="tpu_custom_call", output_to_operand_aliasing={{}: (5, {})} | custom-call | flops 10000000 | bytes 14155776 | tf_op jit(solution)/shard_map/place_2/pallas_call | solution.py:355
  601.6 1.5 copy-done.5
  603.1 9.9 %place_3.1 = bf16[16,256,2304]{2,1,0:T(8,128)(2,1)} custom-call(s32[4]{0:T(128)} %get-tuple-element.34.seq_ref, f32[256,2304]{1,0:T(8,128)} %layer_3.1.own_ref, f32[256,2304]{1,0:T(8,128)} %copy-done.5, f32[256,2304]{1,0:T(8,128)} %collective-permute-done.10.crs_ref, f32[256,2304]{1,0:T(8,128)} %collective-permute-done.11.dia_ref, ...), custom_call_target="tpu_custom_call", output_to_operand_aliasing={{}: (5, {})} | custom-call | flops 10000000 | bytes 14155776 | tf_op jit(solution)/shard_map/place_3/pallas_call | solution.py:355
  (98 shorter events, 8.7 us)
Async XLA Ops:
  11.1 132.1 %collective-permute-start.7 = (f32[18,32,2048]{2,1,0:T(8,128)}, f32[18,32,2048]{2,1,0:T(8,128)}, u32[]{:S(2)}, u32[]{:S(2)}) collective-permute-start(f32[18,32,2048]{2,1,0:T(8,128)} %get-tuple-element.28), channel_id=1, source_target_pairs={{0,2},{4,6}} | collective-permute-start | bytes 14155784 | tf_op jit(solution)/shard_map/ppermute | solution.py:434
  18.6 128.4 %collective-permute-start.2 = (f32[16,32,2048]{2,1,0:T(8,128)}, f32[16,32,2048]{2,1,0:T(8,128)}, u32[]{:S(2)}, u32[]{:S(2)}) collective-permute-start(f32[16,32,2048]{2,1,0:T(8,128)} %get-tuple-element.23), channel_id=1, source_target_pairs={{0,1},{1,0},{4,5},{5,4}} | collective-permute-start | bytes 12582920 | tf_op jit(solution)/shard_map/ppermute | solution.py:430
  20.5 107.6 %collective-permute-start.3 = (f32[2,32,2048]{2,1,0:T(8,128)S(1)}, f32[2,32,2048]{2,1,0:T(8,128)S(1)}, u32[]{:S(2)}, u32[]{:S(2)}) collective-permute-start(f32[2,32,2048]{2,1,0:T(8,128)S(1)} %get-tuple-element.26), channel_id=1, source_target_pairs={{0,2},{4,6}} | collective-permute-start | bytes 1572872 | tf_op jit(solution)/shard_map/ppermute | solution.py:429
  21.9 198.5 %collective-permute-start.5 = (f32[6,32,2048]{2,1,0:T(8,128)S(1)}, f32[6,32,2048]{2,1,0:T(8,128)}, u32[]{:S(2)}, u32[]{:S(2)}) collective-permute-start(f32[6,32,2048]{2,1,0:T(8,128)S(1)} %get-tuple-element.27), channel_id=1, source_target_pairs={{0,2},{1,3},{4,6},{5,7}} | collective-permute-start | bytes 4718600 | tf_op jit(solution)/shard_map/ppermute | solution.py:432
  25.1 8.8 %copy-start.6 = (s32[4,4]{1,0:T(4,128)}, s32[4,4]{1,0:T(4,128)S(1)}, u32[]{:S(2)}) copy-start(s32[4,4]{1,0:T(4,128)S(1)} %select_reduce_fusion.4) | copy-start | bytes 196
  25.2 104.3 %copy-start.8 = (bf16[2304]{0:T(1024)(128)(2,1)S(1)}, bf16[2304]{0:T(1024)(128)(2,1)}, u32[]{:S(2)}) copy-start(bf16[2304]{0:T(1024)(128)(2,1)} %param.26) | copy-start | bytes 13828
  25.2 104.9 %copy-start.9 = (bf16[2304]{0:T(1024)(128)(2,1)S(1)}, bf16[2304]{0:T(1024)(128)(2,1)}, u32[]{:S(2)}) copy-start(bf16[2304]{0:T(1024)(128)(2,1)} %param.27) | copy-start | bytes 13828
  128.1 12.0 %copy-start.3 = (f32[2,32,2048]{2,1,0:T(8,128)}, f32[2,32,2048]{2,1,0:T(8,128)S(1)}, u32[]{:S(2)}) copy-start(f32[2,32,2048]{2,1,0:T(8,128)S(1)} %collective-permute-done.3.rest_0_) | copy-start | bytes 1572868
  128.1 18.1 %collective-permute-start.4 = (f32[2,32,2048]{2,1,0:T(8,128)S(1)}, f32[2,32,2048]{2,1,0:T(8,128)S(1)}, u32[]{:S(2)}, u32[]{:S(2)}) collective-permute-start(f32[2,32,2048]{2,1,0:T(8,128)S(1)} %collective-permute-done.3.rest_0_), channel_id=1, source_target_pairs={{2,3},{6,7}} | collective-permute-start | bytes 1572872 | tf_op jit(solution)/shard_map/ppermute | solution.py:431
  128.8 11.3 %copy-start.10 = (f32[128]{0:T(128)}, f32[128]{0:T(128)S(1)}, u32[]{:S(2)}) copy-start(f32[128]{0:T(128)S(1)} %multiply_power_fusion) | copy-start | bytes 1540
  143.2 126.4 %collective-permute-start.8 = (f32[18,32,2048]{2,1,0:T(8,128)}, f32[18,32,2048]{2,1,0:T(8,128)}, u32[]{:S(2)}, u32[]{:S(2)}) collective-permute-start(f32[18,32,2048]{2,1,0:T(8,128)} %collective-permute-done.7.rest_4_), channel_id=1, source_target_pairs={{2,3},{6,7}} | collective-permute-start | bytes 14155784 | tf_op jit(solution)/shard_map/ppermute | solution.py:435
  146.3 0.8 copy-start.4
  217.0 52.6 %collective-permute-start.19 = (f32[256,2304]{1,0:T(8,128)}, f32[256,2304]{1,0:T(8,128)}, u32[]{:S(2)}, u32[]{:S(2)}) collective-permute-start(f32[256,2304]{1,0:T(8,128)} %layer_0.1.own_ref), channel_id=1, source_target_pairs={{0,2},{1,3},{2,0},{3,1},{4,6},{5,7},{6,4},{7,5}} | collective-permute-start | bytes 7077896 | tf_op jit(solution)/shard_map/ppermute | solution.py:466
  220.4 49.2 %collective-permute-start.6 = (f32[6,32,2048]{2,1,0:T(8,128)}, f32[6,32,2048]{2,1,0:T(8,128)S(1)}, u32[]{:S(2)}, u32[]{:S(2)}) collective-permute-start(f32[6,32,2048]{2,1,0:T(8,128)} %collective-permute-done.5.rest_2_), channel_id=1, source_target_pairs={{2,3},{3,2},{6,7},{7,6}} | collective-permute-start | bytes 4718600 | tf_op jit(solution)/shard_map/ppermute | solution.py:433
  221.7 262.4 %collective-permute-start.18 = (f32[256,2304]{1,0:T(8,128)}, f32[256,2304]{1,0:T(8,128)}, u32[]{:S(2)}, u32[]{:S(2)}) collective-permute-start(f32[256,2304]{1,0:T(8,128)} %layer_0.1.own_ref), channel_id=1, source_target_pairs={{0,1},{1,0},{2,3},{3,2},{4,5},{5,4},{6,7},{7,6}} | collective-permute-start | bytes 7077896 | tf_op jit(solution)/shard_map/ppermute | solution.py:467
  269.6 214.7 %collective-permute-start.20 = (f32[256,2304]{1,0:T(8,128)}, f32[256,2304]{1,0:T(8,128)}, u32[]{:S(2)}, u32[]{:S(2)}) collective-permute-start(f32[256,2304]{1,0:T(8,128)} %collective-permute-done.19.crs_ref), channel_id=1, source_target_pairs={{0,1},{1,0},{2,3},{3,2},{4,5},{5,4},{6,7},{7,6}} | collective-permute-start | bytes 7077896 | tf_op jit(solution)/shard_map/ppermute | solution.py:468
  269.6 1.1 copy-start.2
  341.1 143.6 %collective-permute-start.10 = (f32[256,2304]{1,0:T(8,128)}, f32[256,2304]{1,0:T(8,128)}, u32[]{:S(2)}, u32[]{:S(2)}) collective-permute-start(f32[256,2304]{1,0:T(8,128)} %layer_3.1.own_ref), channel_id=1, source_target_pairs={{0,2},{1,3},{2,0},{3,1},{4,6},{5,7},{6,4},{7,5}} | collective-permute-start | bytes 7077896 | tf_op jit(solution)/shard_map/ppermute | solution.py:466
  411.7 73.1 %collective-permute-start.13 = (f32[256,2304]{1,0:T(8,128)}, f32[256,2304]{1,0:T(8,128)}, u32[]{:S(2)}, u32[]{:S(2)}) collective-permute-start(f32[256,2304]{1,0:T(8,128)} %layer_2.1.own_ref), channel_id=1, source_target_pairs={{0,2},{1,3},{2,0},{3,1},{4,6},{5,7},{6,4},{7,5}} | collective-permute-start | bytes 7077896 | tf_op jit(solution)/shard_map/ppermute | solution.py:466
  413.5 124.3 %copy-start.12 = (s32[16]{0:T(128)S(1)}, s32[16]{0:T(128)}, u32[]{:S(2)}) copy-start(s32[16]{0:T(128)} %param.16) | copy-start | bytes 196
  413.5 124.9 %copy-start.7 = (s32[4,4]{1,0:T(4,128)S(1)}, s32[4,4]{1,0:T(4,128)}, u32[]{:S(2)}) copy-start(s32[4,4]{1,0:T(4,128)} %copy-done.6) | copy-start | bytes 196
  413.5 125.7 %copy-start.11 = (f32[128]{0:T(128)S(1)}, f32[128]{0:T(128)}, u32[]{:S(2)}) copy-start(f32[128]{0:T(128)} %copy-done.10) | copy-start | bytes 1540
  484.1 4.5 collective-permute-start.15
  484.1 53.6 %collective-permute-start.16 = (f32[256,2304]{1,0:T(8,128)}, f32[256,2304]{1,0:T(8,128)}, u32[]{:S(2)}, u32[]{:S(2)}) collective-permute-start(f32[256,2304]{1,0:T(8,128)} %layer_1.1.own_ref), channel_id=1, source_target_pairs={{0,2},{1,3},{2,0},{3,1},{4,6},{5,7},{6,4},{7,5}} | collective-permute-start | bytes 7077896 | tf_op jit(solution)/shard_map/ppermute | solution.py:466
  484.3 117.3 %collective-permute-start.9 = (f32[256,2304]{1,0:T(8,128)}, f32[256,2304]{1,0:T(8,128)S(1)}, u32[]{:S(2)}, u32[]{:S(2)}) collective-permute-start(f32[256,2304]{1,0:T(8,128)} %layer_3.1.own_ref), channel_id=1, source_target_pairs={{0,1},{1,0},{2,3},{3,2},{4,5},{5,4},{6,7},{7,6}} | collective-permute-start | bytes 7077896 | tf_op jit(solution)/shard_map/ppermute | solution.py:467
  484.6 107.1 %collective-permute-start.12 = (f32[256,2304]{1,0:T(8,128)}, f32[256,2304]{1,0:T(8,128)}, u32[]{:S(2)}, u32[]{:S(2)}) collective-permute-start(f32[256,2304]{1,0:T(8,128)} %layer_2.1.own_ref), channel_id=1, source_target_pairs={{0,1},{1,0},{2,3},{3,2},{4,5},{5,4},{6,7},{7,6}} | collective-permute-start | bytes 7077896 | tf_op jit(solution)/shard_map/ppermute | solution.py:467
  484.8 116.8 %collective-permute-start.11 = (f32[256,2304]{1,0:T(8,128)}, f32[256,2304]{1,0:T(8,128)}, u32[]{:S(2)}, u32[]{:S(2)}) collective-permute-start(f32[256,2304]{1,0:T(8,128)} %collective-permute-done.10.crs_ref), channel_id=1, source_target_pairs={{0,1},{1,0},{2,3},{3,2},{4,5},{5,4},{6,7},{7,6}} | collective-permute-start | bytes 7077896 | tf_op jit(solution)/shard_map/ppermute | solution.py:468
  488.6 103.1 %collective-permute-start.14 = (f32[256,2304]{1,0:T(8,128)}, f32[256,2304]{1,0:T(8,128)}, u32[]{:S(2)}, u32[]{:S(2)}) collective-permute-start(f32[256,2304]{1,0:T(8,128)} %collective-permute-done.13.crs_ref), channel_id=1, source_target_pairs={{0,1},{1,0},{2,3},{3,2},{4,5},{5,4},{6,7},{7,6}} | collective-permute-start | bytes 7077896 | tf_op jit(solution)/shard_map/ppermute | solution.py:468
  537.7 44.1 %collective-permute-start.17 = (f32[256,2304]{1,0:T(8,128)}, f32[256,2304]{1,0:T(8,128)}, u32[]{:S(2)}, u32[]{:S(2)}) collective-permute-start(f32[256,2304]{1,0:T(8,128)} %collective-permute-done.16.crs_ref), channel_id=1, source_target_pairs={{0,1},{1,0},{2,3},{3,2},{4,5},{5,4},{6,7},{7,6}} | collective-permute-start | bytes 7077896 | tf_op jit(solution)/shard_map/ppermute | solution.py:468
  601.6 1.5 copy-start.5

commit v2 on v0

v2 whole, which is shorter than its diff:
```python
import functools

import jax
import jax.numpy as jnp
from jax import lax
from jax.experimental import pallas as pl
from jax.experimental.pallas import tpu as pltpu
from jax.sharding import PartitionSpec as P


NORM_EPS = 1e-6
ROPE_BASE = 1.0e4
MASK_FLOOR = -1.0e30
GELU_C = 0.7978845608028654

UNIT = 16
PER_HALF = 128 // UNIT
PIECES = (5, 13, 10, 22)
BASE = (0, 5, 18, 28, 50)
N_PACK = BASE[-1]
N_SIB = 4 * PER_HALF
ROW = 16
BLK = 512
DEPTH = 3
F32 = jnp.float32
BF16 = jnp.bfloat16


def rms_norm(x, gain):
    inv = lax.rsqrt(jnp.mean(x * x, axis=-1, keepdims=True) + NORM_EPS)
    return (x * inv * (1.0 + gain)).astype(BF16)


def rotate(x, cos, sin):
    half = x.shape[-1] // 2
    first, second = x[:, :half], x[:, half:]
    return jnp.concatenate([first * cos - second * sin, second * cos + first * sin], axis=-1)


def gelu_tanh(x):
    return 0.5 * x * (1.0 + jnp.tanh(GELU_C * (x + 0.044715 * (x * x * x))))


def dot(a, b):
    return jnp.dot(a, b, preferred_element_type=F32)


def dot_t(a, b):
    return lax.dot_general(a, b, (((1,), (1,)), ((), ())), preferred_element_type=F32)


def make_plan(start_ref, table, order, length, pos, cnt):
    me = lax.axis_index('cp')
    x_pos, core = me // 2, me % 2
    starts = [start_ref[i] for i in range(16)]
    for i in range(16):
        rank = jnp.int32(0)
        for j in range(16):
            if j != i:
                ahead = (starts[j] <= starts[i]) if j < i else (starts[j] < starts[i])
                rank = rank + ahead.astype(jnp.int32)
        order[rank] = i
        length[rank] = starts[i]
    over = jnp.int32(0)
    for hh in range(2):
        at = jnp.int32(0 if hh == 0 else BASE[2])
        for j in range(8):
            n = jnp.clip((length[j] - 128 * hh + UNIT - 1) // UNIT, 0, PER_HALF)
            pos[hh * 8 + j] = at
            cnt[hh * 8 + j] = n
            at = at + n
            if hh == 0 and j == 1:
                over = over | (at > BASE[1]).astype(jnp.int32)
            if hh == 0 and j == 3:
                over = over | (at > BASE[2]).astype(jnp.int32)
            if hh == 1 and j == 3:
                over = over | (at > BASE[2]).astype(jnp.int32)
        over = over | (at > (BASE[4] if hh == 0 else BASE[3])).astype(jnp.int32)
    for t in range(4):
        for k in range(4):
            xx = x_pos if k < 2 else 1 - x_pos
            cc = core if k % 2 == 0 else 1 - core
            place = 2 * t + (cc + t) % 2
            rank = 8 * (1 - xx) + place
            table[ROW * t + k] = order[rank]
            if k == 0:
                table[ROW * t + 4] = length[rank]
                table[ROW * t + 5] = x_pos
                table[ROW * t + 6] = core
                table[ROW * t + 7] = place
                for hh in range(2):
                    table[ROW * t + 8 + hh] = pos[hh * 8 + place]
                    table[ROW * t + 10 + hh] = jnp.clip((length[rank] - 128 * hh + UNIT - 1) // UNIT, 0, PER_HALF)
    table[64] = over
    return x_pos, core


def pack_kernel(start_ref, ck_ref, cv_ref, table, over_ref, *rest):
    outs = rest[:5]
    order, length, pos, cnt, raw, wide, in_sem, out_sem = rest[5:]
    x_pos, core = make_plan(start_ref, table, order, length, pos, cnt)
    over_ref[0, 0] = table[64]
    d = 1024

    def copies(seq, row, where):
        rows = pl.ds(pl.multiple_of(row, UNIT), UNIT)
        return (
            pltpu.make_async_copy(ck_ref.at[seq, rows, :], raw.at[where, :, pl.ds(0, d)], in_sem.at[where, 0]),
            pltpu.make_async_copy(cv_ref.at[seq, rows, :], raw.at[where, :, pl.ds(d, d)], in_sem.at[where, 1]),
        )

    def each_unit(act):
        for j in range(8):
            @pl.loop(0, PER_HALF)
            def _(u, j=j):
                where = pos[core * 8 + j] + u

                @pl.when((u < cnt[core * 8 + j]) & (where < N_PACK))
                def _():
                    for copy in copies(order[j], u * UNIT, where):
                        act(copy)
        for t in range(4):
            seq = order[8 + 2 * t + (1 - core + t) % 2]

            @pl.loop(0, PER_HALF)
            def _(u, t=t, seq=seq):
                for copy in copies(seq, u * UNIT, N_PACK + t * PER_HALF + u):
                    act(copy)

    sizes = PIECES + (N_SIB,)
    starts = BASE[:4] + (N_PACK,)

    def out_copy(k):
        return pltpu.make_async_copy(wide.at[pl.ds(starts[k], sizes[k])], outs[k], out_sem.at[k])

    @pl.when(x_pos == 0)
    def _():
        each_unit(lambda copy: copy.start())
        each_unit(lambda copy: copy.wait())
        for k in range(5):
            @pl.loop(0, sizes[k])
            def _(u, k=k):
                wide[starts[k] + u] = raw[starts[k] + u].astype(F32)

            out_copy(k).start()
        for k in range(5):
            out_copy(k).wait()


def plan_and_pack(start_pos, cache_k, cache_v):
    any_spec = pl.BlockSpec(memory_space=pl.ANY)
    smem = pl.BlockSpec(memory_space=pltpu.SMEM)
    total = N_PACK + N_SIB
    return pl.pallas_call(
        pack_kernel,
        out_shape=[jax.ShapeDtypeStruct((80,), jnp.int32), jax.ShapeDtypeStruct((1, 1), jnp.int32)]
        + [jax.ShapeDtypeStruct((n, UNIT, 2048), F32) for n in PIECES + (N_SIB,)],
        in_specs=[smem, any_spec, any_spec],
        out_specs=[smem, smem] + [any_spec] * 5,
        scratch_shapes=[
            pltpu.SMEM((16,), jnp.int32),
            pltpu.SMEM((16,), jnp.int32),
            pltpu.SMEM((16,), jnp.int32),
            pltpu.SMEM((16,), jnp.int32),
            pltpu.VMEM((total, UNIT, 2048), BF16),
            pltpu.VMEM((total, UNIT, 2048), F32),
            pltpu.SemaphoreType.DMA((total, 2)),
            pltpu.SemaphoreType.DMA((5,)),
        ],
        compiler_params=pltpu.CompilerParams(vmem_limit_bytes=40 * 2**20),
        cost_estimate=pl.CostEstimate(flops=20_000_000, bytes_accessed=16_000_000, transcendentals=0),
        name="pack",
    )(start_pos, cache_k, cache_v)


def pack_full_kernel(order_ref, ck_ref, cv_ref, out_ref, raw, wide, sem):
    d = 1024

    @pl.loop(0, 8)
    def _(j):
        seq = order_ref[j]
        copies = (
            pltpu.make_async_copy(ck_ref.at[seq], raw.at[:, pl.ds(0, d)], sem.at[0]),
            pltpu.make_async_copy(cv_ref.at[seq], raw.at[:, pl.ds(d, d)], sem.at[1]),
        )
        for copy in copies:
            copy.start()
        for copy in copies:
            copy.wait()
        wide[...] = raw[...].astype(F32)
        out = pltpu.make_async_copy(wide, out_ref.at[j], sem.at[2])
        out.start()
        out.wait()


def pack_full(order, cache_k, cache_v):
    any_spec = pl.BlockSpec(memory_space=pl.ANY)
    return pl.pallas_call(
        pack_full_kernel,
        out_shape=jax.ShapeDtypeStruct((8, 128, 2048), F32),
        in_specs=[pl.BlockSpec(memory_space=pltpu.SMEM), any_spec, any_spec],
        out_specs=any_spec,
        scratch_shapes=[
            pltpu.VMEM((128, 2048), BF16),
            pltpu.VMEM((128, 2048), F32),
            pltpu.SemaphoreType.DMA((3,)),
        ],
        name="pack_full",
    )(order, cache_k, cache_v)


def blank_kernel(*refs):
    pass


def blank(count):
    return pl.pallas_call(
        blank_kernel,
        out_shape=[jax.ShapeDtypeStruct((8, 128, 2048), F32)] * count,
        out_specs=[pl.BlockSpec(memory_space=pl.ANY)] * count,
        name="blank",
    )()


def layer_kernel(n_att, n_ff, n_pieces, slot, tab_ref, over_ref, ga_ref, gm_ref, cos_ref, sin_ref, h_ref, wq_ref, wk_ref,
                 wv_ref, wo_ref, wg_ref, wu_ref, wd_ref, ck_ref, cv_ref, sib_ref, full_ref, fullf_ref, *rest):
    pieces = rest[: 2 * n_pieces]
    out_ref, h_rows, act, acc, stage, hist, ring_a, ring_b, sem, own_sem, ring_sem = rest[2 * n_pieces:]
    base = ROW * slot
    seq, start, x_pos, core = tab_ref[base], tab_ref[base + 4], tab_ref[base + 5], tab_ref[base + 6]
    place = tab_ref[base + 7]
    ovf = over_ref[0] > 0

    def unit_copies(hh, u):
        k = hh * PER_HALF + u
        dst = stage.at[pl.ds(pl.multiple_of(k * UNIT, UNIT), UNIT), :]
        rows = pl.ds(pl.multiple_of(u * UNIT, UNIT), UNIT)
        live = u < tab_ref[base + 10 + hh]
        far = x_pos == 1
        direct = core == hh
        pos = tab_ref[base + 8 + hh] + u
        out = [
            (live & (x_pos == 0) & (core != hh), sib_ref.at[slot * PER_HALF + u]),
            (live & far & ovf & direct, full_ref.at[place, rows, :]),
            (live & far & ovf & jnp.logical_not(direct), fullf_ref.at[place, rows, :]),
        ]
        for p in range(n_pieces):
            here = live & far & jnp.logical_not(ovf) & (pos >= BASE[p]) & (pos < BASE[p + 1])
            idx = jnp.clip(pos - BASE[p], 0, PIECES[p] - 1)
            out.append((here & direct, pieces[2 * p].at[idx]))
            out.append((here & jnp.logical_not(direct), pieces[2 * p + 1].at[idx]))
        return [(c, pltpu.make_async_copy(src, dst, sem.at[k])) for c, src in out]

    def own_copies(hh):
        rows = pl.ds(hh * 128, 128)
        return (
            pltpu.make_async_copy(ck_ref.at[seq], hist.at[rows, pl.ds(0, 1024)], own_sem.at[0]),
            pltpu.make_async_copy(cv_ref.at[seq], hist.at[rows, pl.ds(1024, 1024)], own_sem.at[1]),
        )

    n_step = n_att + n_ff

    def weight_copies(i, kind):
        at = lax.rem(i, DEPTH)
        if kind == 0:
            lo, hi = pl.ds(0, 256), pl.ds(256, 256)
            return [
                pltpu.make_async_copy(wq_ref.at[2 * i], ring_a.at[2 * at, :, lo], ring_sem.at[at, 0]),
                pltpu.make_async_copy(wq_ref.at[2 * i + 1], ring_a.at[2 * at, :, hi], ring_sem.at[at, 1]),
                pltpu.make_async_copy(wk_ref.at[i], ring_a.at[2 * at + 1, :, lo], ring_sem.at[at, 2]),
                pltpu.make_async_copy(wv_ref.at[i], ring_a.at[2 * at + 1, :, hi], ring_sem.at[at, 3]),
                pltpu.make_async_copy(wo_ref.at[pl.ds(i * BLK, BLK), :], ring_b.at[at], ring_sem.at[at, 4]),
            ]
        cols = pl.ds(pl.multiple_of((i - n_att) * BLK, BLK), BLK)
        return [
            pltpu.make_async_copy(wg_ref.at[:, cols], ring_a.at[2 * at], ring_sem.at[at, 0]),
            pltpu.make_async_copy(wu_ref.at[:, cols], ring_a.at[2 * at + 1], ring_sem.at[at, 1]),
            pltpu.make_async_copy(wd_ref.at[cols, :], ring_b.at[at], ring_sem.at[at, 4]),
        ]

    def fetch(i):
        @pl.when(i < n_att)
        def _():
            for copy in weight_copies(i, 0):
                copy.start()

        @pl.when((i >= n_att) & (i < n_step))
        def _():
            for copy in weight_copies(i, 1):
                copy.start()

    row_copy = pltpu.make_async_copy(h_ref.at[seq], h_rows, own_sem.at[2])
    row_copy.start()
    for hh in range(2):
        @pl.when((x_pos == 0) & (core == hh))
        def _(hh=hh):
            for copy in own_copies(hh):
                copy.start()
    for copy in weight_copies(0, 0):
        copy.start()
    for hh in range(2):
        @pl.loop(0, PER_HALF)
        def _(u, hh=hh):
            for cond, copy in unit_copies(hh, u):
                @pl.when(cond)
                def _(copy=copy):
                    copy.start()
    for i in range(1, DEPTH):
        for copy in weight_copies(i, 0):
            copy.start()
    row_copy.wait()
    act[...] = rms_norm(h_rows[...].astype(F32), ga_ref[...].astype(F32))
    acc[...] = h_rows[...].astype(F32)
    for hh in range(2):
        @pl.loop(0, PER_HALF)
        def _(u, hh=hh):
            for cond, copy in unit_copies(hh, u):
                @pl.when(cond)
                def _(copy=copy):
                    copy.wait()

        @pl.when((x_pos == 0) & (core == hh))
        def _(hh=hh):
            for copy in own_copies(hh):
                copy.wait()

        @pl.when((x_pos == 1) | (core != hh))
        def _(hh=hh):
            hist[hh * 128:(hh + 1) * 128, :] = stage[hh * 128:(hh + 1) * 128, :].astype(BF16)

    @pl.loop(0, n_att)
    def _(i):
        at = lax.rem(i, DEPTH)
        for copy in weight_copies(i, 0):
            copy.wait()
        cos, sin = cos_ref[0], sin_ref[0]
        a = act[...]
        off = pl.multiple_of(i * 256, 256)
        row = lax.broadcasted_iota(jnp.int32, (256, 256), 0)
        v_old = jnp.where(row < start, hist[:, pl.ds(off + 1024, 256)], jnp.zeros((), BF16))
        kv = dot(a, ring_a[2 * at + 1])
        k_all = jnp.concatenate([hist[:, pl.ds(off, 256)], rotate(kv[:, :256], cos, sin).astype(BF16)], axis=0)
        v_all = jnp.concatenate([v_old, kv[:, 256:].astype(BF16)], axis=0)
        qq = dot(a, ring_a[2 * at])
        qs = [(rotate(qq[:, j * 256:(j + 1) * 256], cos, sin) * 0.0625).astype(BF16) for j in range(2)]
        row = lax.broadcasted_iota(jnp.int32, (256, 512), 0)
        col = lax.broadcasted_iota(jnp.int32, (256, 512), 1)
        ok = (col < start) | ((col >= 256) & (col - 256 <= row))
        scores = [jnp.where(ok, dot_t(q, k_all), MASK_FLOOR) for q in qs]
        tops = [jnp.max(s, axis=-1, keepdims=True) for s in scores]
        probs = [jnp.exp(s - top) for s, top in zip(scores, tops)]
        dens = [jnp.sum(p, axis=-1, keepdims=True) for p in probs]
        nums = [dot(p.astype(BF16), v_all) for p in probs]
        heads = [(num / den).astype(BF16) for num, den in zip(nums, dens)]
        acc[...] += dot(jnp.concatenate(heads, axis=-1), ring_b[at])
        fetch(i + DEPTH)

    res = acc[...].astype(BF16).astype(F32)
    act[...] = rms_norm(res, gm_ref[...].astype(F32))
    acc[...] = res

    @pl.loop(n_att, n_step)
    def _(i):
        at = lax.rem(i, DEPTH)
        for copy in weight_copies(i, 1):
            copy.wait()
        c = act[...]
        mid = (gelu_tanh(dot(c, ring_a[2 * at])) * dot(c, ring_a[2 * at + 1])).astype(BF16)
        acc[...] += dot(mid, ring_b[at])
        fetch(i + DEPTH)

    acc[...] = acc[...].astype(BF16).astype(F32)
    done = pltpu.make_async_copy(acc, out_ref, own_sem.at[3])
    done.start()
    done.wait()


def run_layer(slot, table, over, hidden, ga, gm, cos, sin, wq, wk, wv, wo, wg, wu, wd, ck, cv, sib, full, fullf, pieces):
    n_ff = wg.shape[1] // BLK
    n_pieces = len(pieces) // 2
    any_spec = pl.BlockSpec(memory_space=pl.ANY)
    smem = pl.BlockSpec(memory_space=pltpu.SMEM)
    vmem = pl.BlockSpec(memory_space=pltpu.VMEM)
    d = hidden.shape[2]
    flops = 2 * 256 * d * (2048 * 2 + 1024 * 2 + 3 * wg.shape[1]) + 1_100_000_000
    table_spec = pl.BlockSpec((1, 256, 128), lambda i: (slot, 0, 0))
    return pl.pallas_call(
        functools.partial(layer_kernel, 4, n_ff, n_pieces, slot),
        out_shape=jax.ShapeDtypeStruct((256, d), F32),
        grid=(1,),
        in_specs=[smem, smem, vmem, vmem, table_spec, table_spec] + [any_spec] * (13 + 2 * n_pieces),
        out_specs=any_spec,
        scratch_shapes=[
            pltpu.VMEM((256, d), BF16),
            pltpu.VMEM((256, d), BF16),
            pltpu.VMEM((256, d), F32),
            pltpu.VMEM((256, 2048), F32),
            pltpu.VMEM((256, 2048), BF16),
            pltpu.VMEM((2 * DEPTH, d, BLK), BF16),
            pltpu.VMEM((DEPTH, BLK, d), BF16),
            pltpu.SemaphoreType.DMA((2 * PER_HALF,)),
            pltpu.SemaphoreType.DMA((4,)),
            pltpu.SemaphoreType.DMA((DEPTH, 5)),
        ],
        compiler_params=pltpu.CompilerParams(vmem_limit_bytes=60 * 2**20),
        cost_estimate=pl.CostEstimate(flops=flops, bytes_accessed=160_000_000, transcendentals=0),
    )(table, over, ga, gm, cos, sin, hidden, wq, wk, wv, wo, wg, wu, wd, ck, cv, sib, full, fullf, *pieces)


def window_kernel(sc_ref, h_ref, ga_ref, cos_ref, sin_ref, wk_ref, wv_ref, ck_ref, cv_ref, ok_ref, ov_ref):
    step = pl.program_id(0)
    lo = lax.axis_index('cp') * 128
    a_rows, inside = [], []
    for j in range(2):
        first = lo - sc_ref[2 * step + j]
        want = first + lax.broadcasted_iota(jnp.int32, (128, 256), 0)
        have = lax.broadcasted_iota(jnp.int32, (128, 256), 1)
        pick = jnp.where(want == have, 1.0, 0.0).astype(BF16)
        a_rows.append(dot(pick, h_ref[j]))
        idx = first + lax.broadcasted_iota(jnp.int32, (128, 256), 0)
        inside.append((idx >= 0) & (idx < 256))
    a = rms_norm(jnp.concatenate(a_rows, axis=0), ga_ref[...].astype(F32))
    cos = jnp.concatenate([cos_ref[...]] * 2, axis=0)
    sin = jnp.concatenate([sin_ref[...]] * 2, axis=0)
    for g in range(4):
        k = rotate(dot(a, wk_ref[g]), cos, sin).astype(BF16)
        v = dot(a, wv_ref[g]).astype(BF16)
        cols = slice(g * 256, (g + 1) * 256)
        for j in range(2):
            rows = slice(j * 128, (j + 1) * 128)
            ok_ref[j, :, cols] = jnp.where(inside[j], k[rows], ck_ref[j, :, cols])
            ov_ref[j, :, cols] = jnp.where(inside[j], v[rows], cv_ref[j, :, cols])


def write_windows(scalars, hidden, ga, cos, sin, wk, wv, cache_k, cache_v):
    n_seq, rows, width = cache_k.shape
    d = hidden.shape[2]
    one = pl.Buffered(1)
    cache_spec = pl.BlockSpec((2, rows, width), lambda i, sc: (i, 0, 0))
    return pl.pallas_call(
        window_kernel,
        out_shape=[jax.ShapeDtypeStruct(cache_k.shape, BF16)] * 2,
        grid_spec=pltpu.PrefetchScalarGridSpec(
            num_scalar_prefetch=1,
            grid=(n_seq // 2,),
            in_specs=[
                pl.BlockSpec((2, 256, d), lambda i, sc: (i, 0, 0)),
                pl.BlockSpec((1, d), lambda i, sc: (0, 0), pipeline_mode=one),
                pl.BlockSpec((rows, 128), lambda i, sc: (0, 0), pipeline_mode=one),
                pl.BlockSpec((rows, 128), lambda i, sc: (0, 0), pipeline_mode=one),
                pl.BlockSpec((4, d, 256), lambda i, sc: (0, 0, 0), pipeline_mode=one),
                pl.BlockSpec((4, d, 256), lambda i, sc: (0, 0, 0), pipeline_mode=one),
                cache_spec,
                cache_spec,
            ],
            out_specs=[cache_spec, cache_spec],
        ),
        compiler_params=pltpu.CompilerParams(vmem_limit_bytes=56 * 2**20),
        cost_estimate=pl.CostEstimate(flops=2 * n_seq * rows * d * 2 * width, bytes_accessed=60_000_000, transcendentals=0),
        name="cache_window",
    )(scalars, hidden, ga, cos, sin, wk, wv, cache_k, cache_v)


def place_kernel(slot, n_part, blk, tab_ref, *rest):
    parts = rest[:n_part]
    out_ref, narrow, sem = rest[-3:]
    step, steps = pl.program_id(0), pl.num_programs(0)
    buf = lax.rem(step, 2)

    def copy(k, at, b):
        rows = pl.ds(pl.multiple_of(at * blk, blk), blk)
        return pltpu.make_async_copy(narrow.at[b, k], out_ref.at[tab_ref[ROW * slot + k], rows, :], sem.at[b, k])

    for k in range(n_part):
        @pl.when(step >= 2)
        def _(k=k):
            copy(k, step - 2, buf).wait()

        narrow[buf, k] = parts[k][...].astype(BF16)
        copy(k, step, buf).start()

    @pl.when(step == steps - 1)
    def _():
        for k in range(n_part):
            copy(k, step - 1, 1 - buf).wait()
            copy(k, step, buf).wait()


def place_rows(table, parts, out, n_seq, slot, blk=64):
    rows, d = parts[0].shape
    any_spec = pl.BlockSpec(memory_space=pl.ANY)
    n_part = len(parts)
    args = [table, *parts]
    in_specs = [pl.BlockSpec((blk, d), lambda i, tab: (i, 0))] * n_part
    aliases = {}
    if out is not None:
        in_specs.append(any_spec)
        aliases = {n_part + 1: 0}
        args.append(out)
    return pl.pallas_call(
        functools.partial(place_kernel, slot, n_part, blk),
        out_shape=jax.ShapeDtypeStruct((n_seq, rows, d), BF16),
        grid_spec=pltpu.PrefetchScalarGridSpec(
            num_scalar_prefetch=1,
            grid=(rows // blk,),
            in_specs=in_specs,
            out_specs=any_spec,
            scratch_shapes=[pltpu.VMEM((2, n_part, blk, d), BF16), pltpu.SemaphoreType.DMA((2, n_part))],
        ),
        input_output_aliases=aliases,
        cost_estimate=pl.CostEstimate(flops=10_000_000, bytes_accessed=n_part * rows * d * 6, transcendentals=0),
    )(*args)


def solution(mesh):
    d2d = [(0, 1), (1, 0), (2, 3), (3, 2)]
    cross = [(0, 2), (1, 3), (2, 0), (3, 1)]

    def send(x, pairs, axis='cp'):
        return lax.ppermute(x, axis, pairs)

    def body(hidden, start_pos, cache_k, cache_v, w_q, w_k, w_v, w_o, w_gate, w_up, w_down, norm_attn, norm_mlp):
        n_seq, chunk_len, d = hidden.shape
        shard_len = cache_k.shape[1]
        i32 = jnp.int32
        me = lax.axis_index('cp').astype(i32)

        table, over, p1, p2, p3a, p3b, sib_src = plan_and_pack(start_pos, cache_k, cache_v)
        over = jnp.maximum(over, send(over, [(0, 1), (1, 0)], 'dp'))[0]
        p1d = send(p1, [(0, 2)])
        sib = send(sib_src, [(0, 1), (1, 0)])
        p1f = send(p1d, [(2, 3)])
        p2d = send(p2, [(0, 2)])
        p2f = send(p2d, [(2, 3)])
        p3ad = send(p3a, [(0, 2), (1, 3)])
        p3af = send(p3ad, [(2, 3), (3, 2)])
        p3bd = send(p3b, [(0, 2)])
        p3bf = send(p3bd, [(2, 3)])

        def send_all(_):
            sid = jnp.arange(n_seq, dtype=i32)
            before = (start_pos[None, :] < start_pos[:, None]) | (
                (start_pos[None, :] == start_pos[:, None]) & (sid[None, :] < sid[:, None]))
            rank = jnp.sum(before.astype(i32), axis=1)
            order = jnp.sum((rank[None, :] == sid[:, None]).astype(i32) * sid[None, :], axis=1)
            got = lax.ppermute(pack_full(order, cache_k, cache_v), 'cp', [(0, 2), (1, 3)])
            return got, lax.ppermute(got, 'cp', [(2, 3), (3, 2)])

        full, full_f = lax.cond(over[0] > 0, send_all, lambda _: tuple(blank(2)), 0)

        head_dim = w_q.shape[2]
        inv_freq = ROPE_BASE ** (-2.0 * jnp.arange(head_dim // 2, dtype=F32) / head_dim)
        my_len = jnp.stack([table[ROW * t + 4] for t in range(4)])
        own_pos = my_len[:, None] + jnp.arange(chunk_len, dtype=i32)[None, :]
        angles = own_pos.astype(F32)[:, :, None] * inv_freq
        cos, sin = jnp.cos(angles), jnp.sin(angles)
        win_lo = me * shard_len
        win_angles = (win_lo + jnp.arange(shard_len, dtype=i32)).astype(F32)[:, None] * inv_freq
        win_cos, win_sin = jnp.cos(win_angles), jnp.sin(win_angles)
        wq = w_q.transpose(1, 0, 2)
        wk = w_k.transpose(1, 0, 2)
        wv = w_v.transpose(1, 0, 2)
        wo = w_o.reshape(-1, d)
        ga, gm = norm_attn[None, :], norm_mlp[None, :]

        parts = []
        tab = table
        for t in range(4):
            pieces = (p1d, p1f, p2d, p2f, p3ad, p3af, p3bd, p3bf)[: (2, 4, 8, 8)[t]]
            own = run_layer(t, tab, over, hidden, ga, gm, cos, sin, wq, wk, wv, wo, w_gate, w_up, w_down,
                            cache_k, cache_v, sib, full, full_f, pieces)
            tab, own = lax.optimization_barrier((tab, own))
            crs = send(own, cross)
            near = send(own, d2d)
            dia = send(crs, d2d)
            parts.append((own, near, crs, dia))
        start_late, _ = lax.optimization_barrier((start_pos, tab))
        new_k, new_v = write_windows(start_late, hidden, ga, win_cos, win_sin, wk, wv, cache_k, cache_v)
        out = None
        for t in range(3):
            out = place_rows(tab, parts[t], out, n_seq, t)
        out = place_rows(tab, parts[3], out, n_seq, 3)
        return out, new_k, new_v

    group_spec = P('dp', None, None)
    cache_spec = P('dp', 'cp', None)
    whole_spec = P()
    return jax.shard_map(
        body,
        mesh=mesh,
        in_specs=(group_spec, P('dp'), cache_spec, cache_spec) + (whole_spec,) * 9,
        out_specs=(group_spec, cache_spec, cache_spec),
        check_vma=False,
    )
```

time: 1640 us -> 453 us (0.28)
  matrix products: 846 us -> 0 us
  waiting for transfers between devices: 404 us -> 98.5 us
  Pallas kernels: 0 us -> 292 us
  local copies, waits for them, and re-layouts: 227 us -> 23.4 us
  other arithmetic: 135 us -> 6.66 us
  starting transfers between devices: 0.08 us -> 29.8 us
    dot_general x11 -> x0, matrix products: 846 us -> none  [the longest x1 220 us: finish_layer(): jnp.einsum('bcd,df->bcf', normed_mlp, w_gate, preferred_element_type=jnp....]
    psum x1 -> x0, waiting for transfers between devices: 404 us -> none  [local_layer(): packed = lax.psum(packed, 'cp')]
    pallas_call x0 -> x11, Pallas kernels: none -> 292 us  [the longest x4 224 us: run_layer(): pl.pallas_call(functools.partial(layer_kernel, 4, n_ff, n_pieces, slot),...]
    gather x96 -> x0, local copies, waits for them, and re-layouts: 116 us -> none
    ppermute x0 -> x22, waiting for transfers between devices: none -> 98.5 us  [send(): return lax.ppermute(x, axis, pairs)]
    concatenate x2 -> x0, other arithmetic: 41.9 us -> none  [the longest x1 23.2 us: local_layer(): jnp.concatenate([hist_num * rescale[..., None], (hist_den * rescale)[...,...]
    concatenate x2 -> x0, local copies, waits for them, and re-layouts: 35.2 us -> none  [rotate(): jnp.concatenate([first * cos_tab - second * sin_tab, second * cos_tab + f...]
    sub x2 -> x0, other arithmetic: 31.5 us -> none  [rotate(): first * cos_tab - second * sin_tab]
  transfers between devices with their start and end apart: 2 -> 22, of which waited for: 1 -> 3; matrix products, arithmetic and copies ran while one was open for 19% -> 6% of each run, Pallas kernels for 0% -> 61%
where the time goes in v2:
time: 453 us; the launch traced here: 452 us
  Pallas kernels  292 us (64%)
  waiting for transfers between devices  98.5 us (22%)
  starting transfers between devices  29.8 us (7%)
  local copies, waits for them, and re-layouts  23.4 us (5%)
  other arithmetic  6.66 us (1%)
    pallas_call x4, Pallas kernels, run_layer(): pl.pallas_call(functools.partial(layer_kernel, 4, n_ff, n_pieces, slot),...  224 us
    ppermute x22, waiting for transfers between devices, send(): return lax.ppermute(x, axis, pairs)  98.5 us
    pallas_call x1, Pallas kernels, write_windows(): pl.pallas_call(window_kernel, out_shape=[jax.ShapeDtypeStruct(cache_k.sha...  31.7 us
    ppermute x22, starting transfers between devices, send(): return lax.ppermute(x, axis, pairs)  29.8 us
    pallas_call x4, Pallas kernels, place_rows(): pl.pallas_call(functools.partial(place_kernel, slot, n_part, blk), out_sh...  26.5 us
    unnamed x23, local copies, waits for them, and re-layouts  12.9 us
    pallas_call x1, Pallas kernels, plan_and_pack(): pl.pallas_call(pack_kernel, out_shape=[jax.ShapeDtypeStruct((80,), jnp.in...  9.41 us
  transfers between devices with their start and end apart: 22, of which 3 were waited for; matrix products, arithmetic and copies ran while one was open for 6% of the time, Pallas kernels for 61%

profile of v2, /device:TPU:0, one launch (start us, length us, event | category | flops | bytes accessed | tf_op | source)
XLA Modules:
  0.0 452.4 jit_solution(17399715663796713797)
XLA Ops:
  0.6 9.4 %pack.1 = (s32[80]{0:T(128)S(1)}, s32[1,1]{1,0:T(1,128)}, f32[5,16,2048]{2,1,0:T(8,128)S(1)}, f32[13,16,2048]{2,1,0:T(8,128)}, f32[10,16,2048]{2,1,0:T(8,128)S(1...) custom-call(s32[16]{0:T(128)} %sc_ref, bf16[16,128,1024]{2,1,0:T(8,128)(2,1)} %ck_ref.11, ...), custom_call_target="tpu_custom_call" | custom-call | flops 20000000 | bytes 16000000 | tf_op jit(solution)/shard_map/pack/pallas_call | solution.py:154
  10.1 1.1 copy-done.1
  11.1 2.6 collective-permute-start.3
  13.8 2.8 collective-permute-start.10
  16.6 2.7 collective-permute-start.2
  19.3 2.1 collective-permute-start.4
  21.4 2.5 collective-permute-start.6
  25.3 2.4 collective-permute-start.8
  27.7 8.7 %copy_bitcast_fusion.1 = (bf16[4,2304,256]{2,1,0:T(8,128)(2,1)}, bf16[4,2304,256]{2,1,0:T(8,128)(2,1)}) fusion(bf16[2304,4,256]{2,1,0:T(4,128)(2,1)} %param.21, bf16[2304,4,256]{2,1,0:T(4,128)(2,1)} %param.20), kind=kLoop, calls=%fused_computation.7 | loop fusion | bytes 18874368 | tf_op jit(solution)/shard_map/transpose | solution.py:562
  36.9 9.4 %copy.28 = bf16[2304,8,256]{2,0,1:T(8,128)(2,1)} copy(bf16[2304,8,256]{2,1,0:T(8,128)(2,1)} %param.19) | data formatting | bytes 18874368 | tf_op args[4]
  47.6 20.5 %collective-permute-done.4.rest_0_ = f32[5,16,2048]{2,1,0:T(8,128)} collective-permute-done((f32[5,16,2048]{2,1,0:T(8,128)S(1)}, f32[5,16,2048]{2,1,0:T(8,128)}, u32[]{:S(2)}, u32[]{:S(2)}) %collective-permute-start.4) | collective-permute-done | bytes 655392 | tf_op jit(solution)/shard_map/ppermute | solution.py:520
  68.8 2.6 pad_add_fusion
  71.4 3.0 multiply_sine_fusion
  74.5 26.0 %collective-permute-done.8.rest_4_ = f32[10,16,2048]{2,1,0:T(8,128)} collective-permute-done((f32[10,16,2048]{2,1,0:T(8,128)}, f32[10,16,2048]{2,1,0:T(8,128)}, u32[]{:S(2)}, u32[]{:S(2)}) %collective-permute-start.8) | collective-permute-done | bytes 1310752 | tf_op jit(solution)/shard_map/ppermute | solution.py:520
  100.5 1.8 collective-permute-start.9
  102.3 1.8 collective-permute-start.7
  104.1 0.8 collective-permute-start.11
  105.0 0.8 copy-done.5
  105.8 55.9 %shard_map.148.rest_0_ = f32[256,2304]{1,0:T(8,128)} custom-call(s32[80]{0:T(128)} %copy-done, s32[1]{0:T(128)} %bitcast.over_ref, bf16[1,2304]{1,0:T(2,128)(2,1)} %broadcast_in_dim.4.ga_ref, bf16[1,2304]{1,0:T(2,128)(2,1)} %broadcast_in_dim.5.gm_ref, f32[4,256,128]{2,1,0:T(8,128)} %get-tuple-element.53.cos_ref, f32[4,256,128]{2,1,0:T(8,128)} %get-tuple-element.52.sin_ref, ...), custom_call_target="tpu_custom_call" | custom-call | flops 40962666496 | bytes 160000000 | tf_op jit(solution)/shard_map/pallas_call | solution.py:387
  161.7 4.7 %collective-permute-start.22 = (f32[256,2304]{1,0:T(8,128)}, f32[256,2304]{1,0:T(8,128)}, u32[]{:S(2)}, u32[]{:S(2)}) collective-permute-start(f32[256,2304]{1,0:T(8,128)} %shard_map.148.rest_0_), channel_id=1, source_target_pairs={{0,2},{1,3},{2,0},{3,1},{4,6},{5,7},{6,4},{7,5}} | collective-permute-start | bytes 7077896 | tf_op jit(solution)/shard_map/ppermute | solution.py:520
  166.4 55.8 %shard_map.149.rest_0_ = f32[256,2304]{1,0:T(8,128)} custom-call(s32[80]{0:T(128)} %copy-done, s32[1]{0:T(128)} %bitcast.over_ref, bf16[1,2304]{1,0:T(2,128)(2,1)} %broadcast_in_dim.4.ga_ref, bf16[1,2304]{1,0:T(2,128)(2,1)} %broadcast_in_dim.5.gm_ref, f32[4,256,128]{2,1,0:T(8,128)} %get-tuple-element.53.cos_ref, f32[4,256,128]{2,1,0:T(8,128)} %get-tuple-element.52.sin_ref, ...), custom_call_target="tpu_custom_call" | custom-call | flops 40962666496 | bytes 160000000 | tf_op jit(solution)/shard_map/pallas_call | solution.py:387
  223.3 1.6 copy-done.4
  224.8 56.2 %shard_map.150.rest_0_ = f32[256,2304]{1,0:T(8,128)} custom-call(s32[80]{0:T(128)} %copy-done, s32[1]{0:T(128)} %bitcast.over_ref, bf16[1,2304]{1,0:T(2,128)(2,1)} %broadcast_in_dim.4.ga_ref, bf16[1,2304]{1,0:T(2,128)(2,1)} %broadcast_in_dim.5.gm_ref, f32[4,256,128]{2,1,0:T(8,128)} %get-tuple-element.53.cos_ref, f32[4,256,128]{2,1,0:T(8,128)} %get-tuple-element.52.sin_ref, ...), custom_call_target="tpu_custom_call" | custom-call | flops 40962666496 | bytes 160000000 | tf_op jit(solution)/shard_map/pallas_call | solution.py:387
  281.1 1.9 collective-permute-start.16
  283.0 56.1 %shard_map.151.rest_0_ = f32[256,2304]{1,0:T(8,128)} custom-call(s32[80]{0:T(128)} %copy-done, s32[1]{0:T(128)} %bitcast.over_ref, bf16[1,2304]{1,0:T(2,128)(2,1)} %broadcast_in_dim.4.ga_ref, bf16[1,2304]{1,0:T(2,128)(2,1)} %broadcast_in_dim.5.gm_ref, f32[4,256,128]{2,1,0:T(8,128)} %get-tuple-element.53.cos_ref, f32[4,256,128]{2,1,0:T(8,128)} %get-tuple-element.52.sin_ref, ...), custom_call_target="tpu_custom_call" | custom-call | flops 40962666496 | bytes 160000000 | tf_op jit(solution)/shard_map/pallas_call | solution.py:387
  340.5 52.0 %collective-permute-done.13.rest_2_ = f32[256,2304]{1,0:T(8,128)} collective-permute-done((f32[256,2304]{1,0:T(8,128)}, f32[256,2304]{1,0:T(8,128)}, u32[]{:S(2)}, u32[]{:S(2)}) %collective-permute-start.13) | collective-permute-done | bytes 2359328 | tf_op jit(solution)/shard_map/ppermute | solution.py:520
  393.0 1.0 multiply_sine_fusion.1
  394.0 31.7 %cache_window.1 = (bf16[16,128,1024]{2,1,0:T(8,128)(2,1)}, bf16[16,128,1024]{2,1,0:T(8,128)(2,1)}) custom-call(s32[16]{0:T(128)S(1)} %copy-done.12, bf16[16,256,2304]{2,1,0:T(8,128)(2,1)} %h_ref.9, bf16[1,2304]{1,0:T(2,128)(2,1)} %broadcast_in_dim.4.ga_ref, f32[128,128]{1,0:T(8,128)} %get-tuple-element.55.cos_ref, f32[128,128]{1,0:T(8,128)} %get-tuple-element.54.sin_ref, ...), custom_call_target="tpu_custom_call" | custom-call | flops 19327352832 | bytes 60000000 | tf_op jit(solution)/shard_map/cache_window/pallas_call | solution.py:440
  425.7 6.6 %shard_map.152.rest_4_ = bf16[16,256,2304]{2,1,0:T(8,128)(2,1)} custom-call(s32[80]{0:T(128)} %copy-done, f32[256,2304]{1,0:T(8,128)} %shard_map.148.rest_0_, f32[256,2304]{1,0:T(8,128)} %collective-permute-done.21.rest_1_, f32[256,2304]{1,0:T(8,128)} %collective-permute-done.22.rest_2_, f32[256,2304]{1,0:T(8,128)} %collective-permute-done.23.rest_3_), custom_call_target="tpu_custom_call" | custom-call | flops 10000000 | bytes 14155776 | tf_op jit(solution)/shard_map/pallas_call | solution.py:500
  432.3 6.6 %shard_map.153.rest_4_ = bf16[16,256,2304]{2,1,0:T(8,128)(2,1)} custom-call(s32[80]{0:T(128)} %copy-done, f32[256,2304]{1,0:T(8,128)} %shard_map.149.rest_0_, f32[256,2304]{1,0:T(8,128)} %collective-permute-done.18.rest_1_, f32[256,2304]{1,0:T(8,128)} %collective-permute-done.19.rest_2_, ...), custom_call_target="tpu_custom_call", output_to_operand_aliasing={{}: (5, {})} | custom-call | flops 10000000 | bytes 14155776 | tf_op jit(solution)/shard_map/pallas_call | solution.py:500
  439.0 6.6 %shard_map.154.rest_4_ = bf16[16,256,2304]{2,1,0:T(8,128)(2,1)} custom-call(s32[80]{0:T(128)} %copy-done, f32[256,2304]{1,0:T(8,128)} %shard_map.150.rest_0_, f32[256,2304]{1,0:T(8,128)} %collective-permute-done.15.rest_1_, f32[256,2304]{1,0:T(8,128)} %collective-permute-done.16.rest_2_, ...), custom_call_target="tpu_custom_call", output_to_operand_aliasing={{}: (5, {})} | custom-call | flops 10000000 | bytes 14155776 | tf_op jit(solution)/shard_map/pallas_call | solution.py:500
  445.6 6.6 %shard_map.155 = bf16[16,256,2304]{2,1,0:T(8,128)(2,1)} custom-call(s32[80]{0:T(128)} %copy-done, f32[256,2304]{1,0:T(8,128)} %shard_map.151.rest_0_, f32[256,2304]{1,0:T(8,128)} %collective-permute-done.12.rest_1_, f32[256,2304]{1,0:T(8,128)} %collective-permute-done.13.rest_2_, ...), custom_call_target="tpu_custom_call", output_to_operand_aliasing={{}: (5, {})} | custom-call | flops 10000000 | bytes 14155776 | tf_op jit(solution)/shard_map/pallas_call | solution.py:500
  (57 shorter events, 5.7 us)
Async XLA Ops:
  0.6 24.6 %copy-start.11 = (s32[16]{0:T(128)S(1)}, s32[16]{0:T(128)}, u32[]{:S(2)}) copy-start(s32[16]{0:T(128)} %sc_ref) | copy-start | bytes 196
  10.1 1.1 copy-start.1
  11.1 35.8 %copy-start = (s32[80]{0:T(128)}, s32[80]{0:T(128)S(1)}, u32[]{:S(2)}) copy-start(s32[80]{0:T(128)S(1)} %get-tuple-element.44.tab_ref) | copy-start | bytes 964
  11.1 93.9 %collective-permute-start.3 = (f32[32,16,2048]{2,1,0:T(8,128)}, f32[32,16,2048]{2,1,0:T(8,128)}, u32[]{:S(2)}, u32[]{:S(2)}) collective-permute-start(f32[32,16,2048]{2,1,0:T(8,128)} %get-tuple-element.34), channel_id=1, source_target_pairs={{0,1},{1,0},{4,5},{5,4}} | collective-permute-start | bytes 12582920 | tf_op jit(solution)/shard_map/ppermute | solution.py:520
  13.8 90.4 %collective-permute-start.10 = (f32[22,16,2048]{2,1,0:T(8,128)S(1)}, f32[22,16,2048]{2,1,0:T(8,128)}, u32[]{:S(2)}, u32[]{:S(2)}) collective-permute-start(f32[22,16,2048]{2,1,0:T(8,128)S(1)} %get-tuple-element.42), channel_id=1, source_target_pairs={{0,2},{4,6}} | collective-permute-start | bytes 8650760 | tf_op jit(solution)/shard_map/ppermute | solution.py:520
  16.6 7.3 %collective-permute-start.2 = (s32[1,1]{1,0:T(1,128)}, s32[1,1]{1,0:T(1,128)}, u32[]{:S(2)}, u32[]{:S(2)}) collective-permute-start(s32[1,1]{1,0:T(1,128)} %get-tuple-element.33), channel_id=1, source_target_pairs={{0,4},{4,0},{1,5},{5,1},{2,6},{6,2},{3,7},{7,3}} | collective-permute-start | bytes 20 | tf_op jit(solution)/shard_map/ppermute | solution.py:520
  19.3 48.8 %collective-permute-start.4 = (f32[5,16,2048]{2,1,0:T(8,128)S(1)}, f32[5,16,2048]{2,1,0:T(8,128)}, u32[]{:S(2)}, u32[]{:S(2)}) collective-permute-start(f32[5,16,2048]{2,1,0:T(8,128)S(1)} %get-tuple-element.37), channel_id=1, source_target_pairs={{0,2},{4,6}} | collective-permute-start | bytes 1966088 | tf_op jit(solution)/shard_map/ppermute | solution.py:520
  21.4 80.9 %collective-permute-start.6 = (f32[13,16,2048]{2,1,0:T(8,128)}, f32[13,16,2048]{2,1,0:T(8,128)}, u32[]{:S(2)}, u32[]{:S(2)}) collective-permute-start(f32[13,16,2048]{2,1,0:T(8,128)} %get-tuple-element.39), channel_id=1, source_target_pairs={{0,2},{4,6}} | collective-permute-start | bytes 5111816 | tf_op jit(solution)/shard_map/ppermute | solution.py:520
  25.3 11.0 %copy-start.7 = (bf16[2304]{0:T(1024)(128)(2,1)S(1)}, bf16[2304]{0:T(1024)(128)(2,1)}, u32[]{:S(2)}) copy-start(bf16[2304]{0:T(1024)(128)(2,1)} %param.26) | copy-start | bytes 13828
  25.3 75.2 %collective-permute-start.8 = (f32[10,16,2048]{2,1,0:T(8,128)}, f32[10,16,2048]{2,1,0:T(8,128)}, u32[]{:S(2)}, u32[]{:S(2)}) collective-permute-start(f32[10,16,2048]{2,1,0:T(8,128)} %copy-done.1), channel_id=1, source_target_pairs={{0,2},{1,3},{4,6},{5,7}} | collective-permute-start | bytes 3932168 | tf_op jit(solution)/shard_map/ppermute | solution.py:520
  36.9 9.4 %copy-start.8 = (bf16[2304]{0:T(1024)(128)(2,1)S(1)}, bf16[2304]{0:T(1024)(128)(2,1)}, u32[]{:S(2)}) copy-start(bf16[2304]{0:T(1024)(128)(2,1)} %param.27) | copy-start | bytes 13828
  68.1 36.9 %collective-permute-start.5 = (f32[5,16,2048]{2,1,0:T(8,128)}, f32[5,16,2048]{2,1,0:T(8,128)S(1)}, u32[]{:S(2)}, u32[]{:S(2)}) collective-permute-start(f32[5,16,2048]{2,1,0:T(8,128)} %collective-permute-done.4.rest_0_), channel_id=1, source_target_pairs={{2,3},{6,7}} | collective-permute-start | bytes 1966088 | tf_op jit(solution)/shard_map/ppermute | solution.py:520
  68.8 36.2 %copy-start.9 = (f32[128]{0:T(128)}, f32[128]{0:T(128)S(1)}, u32[]{:S(2)}) copy-start(f32[128]{0:T(128)S(1)} %multiply_power_fusion) | copy-start | bytes 1540
  100.5 122.0 %collective-permute-start.9 = (f32[10,16,2048]{2,1,0:T(8,128)}, f32[10,16,2048]{2,1,0:T(8,128)}, u32[]{:S(2)}, u32[]{:S(2)}) collective-permute-start(f32[10,16,2048]{2,1,0:T(8,128)} %collective-permute-done.8.rest_4_), channel_id=1, source_target_pairs={{2,3},{3,2},{6,7},{7,6}} | collective-permute-start | bytes 3932168 | tf_op jit(solution)/shard_map/ppermute | solution.py:520
  102.3 64.2 %collective-permute-start.7 = (f32[13,16,2048]{2,1,0:T(8,128)}, f32[13,16,2048]{2,1,0:T(8,128)}, u32[]{:S(2)}, u32[]{:S(2)}) collective-permute-start(f32[13,16,2048]{2,1,0:T(8,128)} %collective-permute-done.6.rest_2_), channel_id=1, source_target_pairs={{2,3},{6,7}} | collective-permute-start | bytes 5111816 | tf_op jit(solution)/shard_map/ppermute | solution.py:520
  104.1 119.1 %collective-permute-start.11 = (f32[22,16,2048]{2,1,0:T(8,128)}, f32[22,16,2048]{2,1,0:T(8,128)S(1)}, u32[]{:S(2)}, u32[]{:S(2)}) collective-permute-start(f32[22,16,2048]{2,1,0:T(8,128)} %collective-permute-done.10.rest_6_), channel_id=1, source_target_pairs={{2,3},{6,7}} | collective-permute-start | bytes 8650760 | tf_op jit(solution)/shard_map/ppermute | solution.py:520
  161.7 177.4 %collective-permute-start.22 = (f32[256,2304]{1,0:T(8,128)}, f32[256,2304]{1,0:T(8,128)}, u32[]{:S(2)}, u32[]{:S(2)}) collective-permute-start(f32[256,2304]{1,0:T(8,128)} %shard_map.148.rest_0_), channel_id=1, source_target_pairs={{0,2},{1,3},{2,0},{3,1},{4,6},{5,7},{6,4},{7,5}} | collective-permute-start | bytes 7077896 | tf_op jit(solution)/shard_map/ppermute | solution.py:520
  166.4 173.1 %collective-permute-start.21 = (f32[256,2304]{1,0:T(8,128)}, f32[256,2304]{1,0:T(8,128)}, u32[]{:S(2)}, u32[]{:S(2)}) collective-permute-start(f32[256,2304]{1,0:T(8,128)} %shard_map.148.rest_0_), channel_id=1, source_target_pairs={{0,1},{1,0},{2,3},{3,2},{4,5},{5,4},{6,7},{7,6}} | collective-permute-start | bytes 7077896 | tf_op jit(solution)/shard_map/ppermute | solution.py:520
  222.3 117.2 %collective-permute-start.19 = (f32[256,2304]{1,0:T(8,128)}, f32[256,2304]{1,0:T(8,128)}, u32[]{:S(2)}, u32[]{:S(2)}) collective-permute-start(f32[256,2304]{1,0:T(8,128)} %shard_map.149.rest_0_), channel_id=1, source_target_pairs={{0,2},{1,3},{2,0},{3,1},{4,6},{5,7},{6,4},{7,5}} | collective-permute-start | bytes 7077896 | tf_op jit(solution)/shard_map/ppermute | solution.py:520
  222.5 117.5 %collective-permute-start.18 = (f32[256,2304]{1,0:T(8,128)}, f32[256,2304]{1,0:T(8,128)}, u32[]{:S(2)}, u32[]{:S(2)}) collective-permute-start(f32[256,2304]{1,0:T(8,128)} %shard_map.149.rest_0_), channel_id=1, source_target_pairs={{0,1},{1,0},{2,3},{3,2},{4,5},{5,4},{6,7},{7,6}} | collective-permute-start | bytes 7077896 | tf_op jit(solution)/shard_map/ppermute | solution.py:520
  223.3 1.6 copy-start.4
  281.0 59.0 %copy-start.6 = (f32[256,2304]{1,0:T(8,128)S(1)}, f32[256,2304]{1,0:T(8,128)}, u32[]{:S(2)}) copy-start(f32[256,2304]{1,0:T(8,128)} %shard_map.150.rest_0_) | copy-start | bytes 7077892
  281.0 112.0 %copy-start.10 = (f32[128]{0:T(128)S(1)}, f32[128]{0:T(128)}, u32[]{:S(2)}) copy-start(f32[128]{0:T(128)} %copy-done.9) | copy-start | bytes 1540
  281.0 113.0 %copy-start.12 = (s32[16]{0:T(128)S(1)}, s32[16]{0:T(128)}, u32[]{:S(2)}) copy-start(s32[16]{0:T(128)} %sc_ref) | copy-start | bytes 196
  281.1 59.0 %collective-permute-start.16 = (f32[256,2304]{1,0:T(8,128)}, f32[256,2304]{1,0:T(8,128)}, u32[]{:S(2)}, u32[]{:S(2)}) collective-permute-start(f32[256,2304]{1,0:T(8,128)} %shard_map.150.rest_0_), channel_id=1, source_target_pairs={{0,2},{1,3},{2,0},{3,1},{4,6},{5,7},{6,4},{7,5}} | collective-permute-start | bytes 7077896 | tf_op jit(solution)/shard_map/ppermute | solution.py:520
  339.1 53.4 %collective-permute-start.13 = (f32[256,2304]{1,0:T(8,128)}, f32[256,2304]{1,0:T(8,128)}, u32[]{:S(2)}, u32[]{:S(2)}) collective-permute-start(f32[256,2304]{1,0:T(8,128)} %shard_map.151.rest_0_), channel_id=1, source_target_pairs={{0,2},{1,3},{2,0},{3,1},{4,6},{5,7},{6,4},{7,5}} | collective-permute-start | bytes 7077896 | tf_op jit(solution)/shard_map/ppermute | solution.py:520
  339.5 53.0 %collective-permute-start.23 = (f32[256,2304]{1,0:T(8,128)}, f32[256,2304]{1,0:T(8,128)}, u32[]{:S(2)}, u32[]{:S(2)}) collective-permute-start(f32[256,2304]{1,0:T(8,128)} %collective-permute-done.22.rest_2_), channel_id=1, source_target_pairs={{0,1},{1,0},{2,3},{3,2},{4,5},{5,4},{6,7},{7,6}} | collective-permute-start | bytes 7077896 | tf_op jit(solution)/shard_map/ppermute | solution.py:520
  339.5 92.8 %collective-permute-start.20 = (f32[256,2304]{1,0:T(8,128)}, f32[256,2304]{1,0:T(8,128)}, u32[]{:S(2)}, u32[]{:S(2)}) collective-permute-start(f32[256,2304]{1,0:T(8,128)} %collective-permute-done.19.rest_2_), channel_id=1, source_target_pairs={{0,1},{1,0},{2,3},{3,2},{4,5},{5,4},{6,7},{7,6}} | collective-permute-start | bytes 7077896 | tf_op jit(solution)/shard_map/ppermute | solution.py:520
  340.0 98.9 %collective-permute-start.15 = (f32[256,2304]{1,0:T(8,128)S(1)}, f32[256,2304]{1,0:T(8,128)}, u32[]{:S(2)}, u32[]{:S(2)}) collective-permute-start(f32[256,2304]{1,0:T(8,128)S(1)} %copy-done.6), channel_id=1, source_target_pairs={{0,1},{1,0},{2,3},{3,2},{4,5},{5,4},{6,7},{7,6}} | collective-permute-start | bytes 7077896 | tf_op jit(solution)/shard_map/ppermute | solution.py:520
  340.1 98.9 %collective-permute-start.17 = (f32[256,2304]{1,0:T(8,128)}, f32[256,2304]{1,0:T(8,128)}, u32[]{:S(2)}, u32[]{:S(2)}) collective-permute-start(f32[256,2304]{1,0:T(8,128)} %collective-permute-done.16.rest_2_), channel_id=1, source_target_pairs={{0,1},{1,0},{2,3},{3,2},{4,5},{5,4},{6,7},{7,6}} | collective-permute-start | bytes 7077896 | tf_op jit(solution)/shard_map/ppermute | solution.py:520
  392.5 53.1 %collective-permute-start.12 = (f32[256,2304]{1,0:T(8,128)}, f32[256,2304]{1,0:T(8,128)}, u32[]{:S(2)}, u32[]{:S(2)}) collective-permute-start(f32[256,2304]{1,0:T(8,128)} %shard_map.151.rest_0_), channel_id=1, source_target_pairs={{0,1},{1,0},{2,3},{3,2},{4,5},{5,4},{6,7},{7,6}} | collective-permute-start | bytes 7077896 | tf_op jit(solution)/shard_map/ppermute | solution.py:520
  392.5 53.1 %collective-permute-start.14 = (f32[256,2304]{1,0:T(8,128)}, f32[256,2304]{1,0:T(8,128)}, u32[]{:S(2)}, u32[]{:S(2)}) collective-permute-start(f32[256,2304]{1,0:T(8,128)} %collective-permute-done.13.rest_2_), channel_id=1, source_target_pairs={{0,1},{1,0},{2,3},{3,2},{4,5},{5,4},{6,7},{7,6}} | collective-permute-start | bytes 7077896 | tf_op jit(solution)/shard_map/ppermute | solution.py:520
  (1 other events, 0.8 us)

commit v3 on v0

v3 whole, which is shorter than its diff:
```python
import functools
import math

import jax
import jax.numpy as jnp
from jax import lax
from jax.experimental import pallas as pl
from jax.experimental.pallas import tpu as pltpu
from jax.sharding import PartitionSpec as P


NORM_EPS = 1e-6
ROPE_BASE = 1.0e4
MASK_FLOOR = -1.0e30
GELU_C = 0.7978845608028654

UNIT = 16
HALF = 128
HEAD = 2 * HALF
WIDE = 4 * HEAD
KV_WIDE = 2 * WIDE
PER_HALF = HALF // UNIT
A_UNITS, C_UNITS = 10, 5
WHOLE_B, WHOLE_D = (3, 4, 7), (5, 6)
A_ROWS, C_ROWS = A_UNITS * UNIT, C_UNITS * UNIT
B_ROWS, D_ROWS, S_ROWS = len(WHOLE_B) * HALF, len(WHOLE_D) * HALF, 4 * HALF
ROW = 16
OUT_BLK = 512
BLK = 768
VMEM_BESIDE = 48_100_000
VMEM_ALL = 66_900_000
DEPTH = 2
DEPTH_B = 3
F32 = jnp.float32
BF16 = jnp.bfloat16


def rms_norm(x, gain):
    inv = lax.rsqrt(jnp.mean(x * x, axis=-1, keepdims=True) + NORM_EPS)
    return (x * inv * (1.0 + gain)).astype(BF16)


def rotate(x, cos, sin):
    half = x.shape[-1] // 2
    first, second = x[:, :half], x[:, half:]
    return jnp.concatenate([first * cos - second * sin, second * cos + first * sin], axis=-1)


def gelu_tanh(x):
    return 0.5 * x * (1.0 + jnp.tanh(GELU_C * (x + 0.044715 * (x * x * x))))


def dot(a, b):
    return jnp.dot(a, b, preferred_element_type=F32)


def dot_t(a, b):
    return lax.dot_general(a, b, (((1,), (1,)), ((), ())), preferred_element_type=F32)


def sort_lengths(start_ref, order, length):
    starts = [start_ref[i] for i in range(16)]
    for i in range(16):
        rank = jnp.int32(0)
        for j in range(16):
            if j != i:
                ahead = (starts[j] <= starts[i]) if j < i else (starts[j] < starts[i])
                rank = rank + ahead.astype(jnp.int32)
        order[rank] = i
        length[rank] = starts[i]


def place_units(length, pos, cnt):
    over = jnp.int32(0)
    for half, places, room in ((0, (0,), 0), (0, (1, 2), A_UNITS), (1, (0, 1, 2, 3), 0), (1, (4, 7), C_UNITS), (1, (5, 6), C_UNITS)):
        at = jnp.int32(0)
        for j in places:
            n = jnp.clip((length[j] - half * HALF + UNIT - 1) // UNIT, 0, PER_HALF)
            pos[half * 8 + j] = at
            cnt[half * 8 + j] = n
            at = at + n
        over = over | (at > room).astype(jnp.int32)
    return over


def make_plan(start_ref, table, order, length, pos, cnt):
    me = lax.axis_index('cp')
    x_pos, core = me // 2, me % 2
    sort_lengths(start_ref, order, length)
    over = place_units(length, pos, cnt)
    for t in range(4):
        for k in range(4):
            xx = x_pos if k < 2 else 1 - x_pos
            cc = core if k % 2 == 0 else 1 - core
            place = 2 * t + (cc + t) % 2
            rank = 8 * (1 - xx) + place
            table[ROW * t + k] = order[rank]
            if k == 0:
                table[ROW * t + 4] = length[rank]
                table[ROW * t + 5] = x_pos
                table[ROW * t + 6] = core
                table[ROW * t + 7] = place
                for half in range(2):
                    table[ROW * t + 8 + half] = pos[half * 8 + place]
                    table[ROW * t + 10 + half] = jnp.clip((length[rank] - HALF * half + UNIT - 1) // UNIT, 0, PER_HALF)
    table[64] = over
    return x_pos, core, over


def pack_kernel(start_ref, ck_ref, cv_ref, ga_ref, gm_ref, table, over_ref, cos_ref, sin_ref, ga_out, gm_out, *rest):
    outs = rest[:6]
    order, length, pos, cnt, raw, wide, in_sem, out_sem = rest[6:]
    x_pos, core, over = make_plan(start_ref, table, order, length, pos, cnt)
    over_ref[0] = over
    first = dict(A=0, B=A_ROWS, D=A_ROWS + B_ROWS, E=0, O=C_ROWS, S=A_ROWS + B_ROWS + D_ROWS)
    size = dict(A=A_ROWS, B=B_ROWS, D=D_ROWS, E=C_ROWS, O=C_ROWS, S=S_ROWS)

    def copies(seq, row, to, rows, sem):
        return [pltpu.make_async_copy(src.at[seq, pl.ds(row, rows), :], raw.at[pl.ds(to, rows), pl.ds(side * WIDE, WIDE)],
                                      in_sem.at[sem, side]) for side, src in enumerate((ck_ref, cv_ref))]

    def units(half, j, to, sem, act):
        @pl.loop(0, PER_HALF)
        def _(u):
            at = pos[half * 8 + j] + u

            @pl.when((u < cnt[half * 8 + j]) & (at < (C_UNITS if half else A_UNITS)))
            def _():
                row = pl.multiple_of(u * UNIT, UNIT)
                for copy in copies(order[j], row, pl.multiple_of(to + at * UNIT, UNIT), UNIT, sem + at):
                    act(copy)

    def each(act):
        @pl.when(core == 0)
        def _():
            for j in (1, 2):
                units(0, j, first["A"], 0, act)

        @pl.when(core == 1)
        def _():
            for j in (4, 7):
                units(1, j, first["E"], 0, act)
            for j in (5, 6):
                units(1, j, first["O"], C_UNITS, act)

        for t in range(4):
            seq = order[8 + 2 * t + (1 - core + t) % 2]
            for copy in copies(seq, 0, first["S"] + t * HALF, HALF, A_UNITS + t):
                act(copy)

        @pl.when(core == 0)
        def _():
            for k, j in enumerate(WHOLE_B + WHOLE_D):
                for copy in copies(order[j], 0, first["B"] + k * HALF, HALF, A_UNITS + 4 + k):
                    act(copy)

    def out_copy(k, name):
        return pltpu.make_async_copy(wide.at[pl.ds(first[name], size[name]), :], outs[k], out_sem.at[k])

    def widen(k, name):
        @pl.loop(0, size[name] // UNIT)
        def _(u):
            rows = pl.ds(pl.multiple_of(first[name] + u * UNIT, UNIT), UNIT)
            wide[rows, :] = raw[rows, :].astype(F32)

        out_copy(k, name).start()

    @pl.when(x_pos == 0)
    def _():
        each(lambda copy: copy.start())

    ga_out[...] = ga_ref[...].astype(F32).reshape(ga_out.shape)
    gm_out[...] = gm_ref[...].astype(F32).reshape(gm_out.shape)
    half = cos_ref.shape[1]
    freq = lax.broadcasted_iota(jnp.int32, (1, half), 1).astype(F32)
    inv_freq = jnp.exp(freq * (-2.0 / (2 * half) * math.log(ROPE_BASE)))
    big = (16 * lax.broadcasted_iota(jnp.int32, (32, half), 0)).astype(F32) * inv_freq
    small = lax.broadcasted_iota(jnp.int32, (16, half), 0).astype(F32) * inv_freq
    cos_a, sin_a, cos_b, sin_b = jnp.cos(big), jnp.sin(big), jnp.cos(small), jnp.sin(small)
    for r in range(32):
        rows = slice(16 * r, 16 * r + 16)
        ca, sa = cos_a[r:r + 1], sin_a[r:r + 1]
        cos_ref[rows, :] = ca * cos_b - sa * sin_b
        sin_ref[rows, :] = sa * cos_b + ca * sin_b

    @pl.when(x_pos == 0)
    def _():
        each(lambda copy: copy.wait())

        @pl.when(core == 0)
        def _():
            widen(0, "A")
            widen(5, "S")
            widen(1, "B")
            widen(2, "D")
            for k, name in enumerate("ABD"):
                out_copy(k, name).wait()

        @pl.when(core == 1)
        def _():
            widen(5, "S")
            widen(3, "E")
            widen(4, "O")
            for k, name in enumerate("EO"):
                out_copy(3 + k, name).wait()

        out_copy(5, "S").wait()


def plan_and_pack(start_pos, cache_k, cache_v, ga, gm):
    any_spec = pl.BlockSpec(memory_space=pl.ANY)
    smem = pl.BlockSpec(memory_space=pltpu.SMEM)
    vmem = pl.BlockSpec(memory_space=pltpu.VMEM)
    total = A_ROWS + B_ROWS + D_ROWS + S_ROWS
    n_copy = A_UNITS + 4 + len(WHOLE_B + WHOLE_D)
    return pl.pallas_call(
        pack_kernel,
        out_shape=[jax.ShapeDtypeStruct((80,), jnp.int32), jax.ShapeDtypeStruct((1,), jnp.int32)]
        + [jax.ShapeDtypeStruct((2 * HEAD, HALF), F32)] * 2 + [jax.ShapeDtypeStruct((1, ga.shape[0]), F32)] * 2
        + [pltpu.HBM((n, KV_WIDE), F32) for n in (A_ROWS, B_ROWS, D_ROWS, C_ROWS, C_ROWS, S_ROWS)],
        in_specs=[smem, any_spec, any_spec, vmem, vmem],
        out_specs=[smem, smem] + [vmem] * 4 + [any_spec] * 6,
        scratch_shapes=[pltpu.SMEM((16,), jnp.int32)] * 4 + [
            pltpu.VMEM((total, KV_WIDE), BF16),
            pltpu.VMEM((total, KV_WIDE), F32),
            pltpu.SemaphoreType.DMA((n_copy, 2)),
            pltpu.SemaphoreType.DMA((6,)),
        ],
        compiler_params=pltpu.CompilerParams(vmem_limit_bytes=VMEM_ALL),
        cost_estimate=pl.CostEstimate(flops=20_000_000, bytes_accessed=16_000_000, transcendentals=0),
        name="pack",
    )(start_pos, cache_k, cache_v, ga, gm)


def pack_full_kernel(order_ref, ck_ref, cv_ref, out_ref, raw, wide, sem):
    d = WIDE

    @pl.loop(0, 8)
    def _(j):
        seq = order_ref[j]
        copies = (
            pltpu.make_async_copy(ck_ref.at[seq], raw.at[:, pl.ds(0, d)], sem.at[0]),
            pltpu.make_async_copy(cv_ref.at[seq], raw.at[:, pl.ds(d, d)], sem.at[1]),
        )
        for copy in copies:
            copy.start()
        for copy in copies:
            copy.wait()
        wide[...] = raw[...].astype(F32)
        out = pltpu.make_async_copy(wide, out_ref.at[j], sem.at[2])
        out.start()
        out.wait()


def pack_full(order, cache_k, cache_v):
    any_spec = pl.BlockSpec(memory_space=pl.ANY)
    return pl.pallas_call(
        pack_full_kernel,
        out_shape=jax.ShapeDtypeStruct((8, HALF, KV_WIDE), F32),
        in_specs=[pl.BlockSpec(memory_space=pltpu.SMEM), any_spec, any_spec],
        out_specs=any_spec,
        scratch_shapes=[
            pltpu.VMEM((HALF, KV_WIDE), BF16),
            pltpu.VMEM((HALF, KV_WIDE), F32),
            pltpu.SemaphoreType.DMA((3,)),
        ],
        name="pack_full",
    )(order, cache_k, cache_v)


def blank_kernel(*refs):
    pass


def blank(count):
    return pl.pallas_call(
        blank_kernel,
        out_shape=[jax.ShapeDtypeStruct((8, HALF, KV_WIDE), F32)] * count,
        out_specs=[pl.BlockSpec(memory_space=pl.ANY)] * count,
        name="blank",
    )()


W_CHUNK = 384
W_SLOTS = 3


def heads_kernel(q_ref, k_ref, v_ref, out_ref, raw_q, raw_k, raw_v, sem):
    n_chunk = q_ref.shape[0] // W_CHUNK

    def copies(i, b):
        rows = pl.ds(pl.multiple_of(i * W_CHUNK, W_CHUNK), W_CHUNK)
        return [pltpu.make_async_copy(src.at[rows], dst.at[b], sem.at[b, j])
                for j, (src, dst) in enumerate(((q_ref, raw_q), (k_ref, raw_k), (v_ref, raw_v)))]

    def sorter(n_head):
        per = HEAD // n_head
        want = lax.broadcasted_iota(jnp.int32, (HEAD, HEAD), 0)
        have = lax.broadcasted_iota(jnp.int32, (HEAD, HEAD), 1)
        return jnp.where((want % per) * n_head + want // per == have, 1.0, 0.0).astype(BF16)

    for i in range(W_SLOTS):
        for copy in copies(i, i):
            copy.start()
    sort8, sort4 = sorter(8), sorter(4)

    @pl.loop(0, n_chunk)
    def _(i):
        b = lax.rem(i, W_SLOTS)
        for copy in copies(i, b):
            copy.wait()
        for part in range(W_CHUNK // 64):
            to = pl.multiple_of(i * W_CHUNK, W_CHUNK) + part * 64
            for raw, n_head, sort, first in ((raw_q, 8, sort8, 0), (raw_k, 4, sort4, 2), (raw_v, 4, sort4, 3)):
                per = HEAD // n_head
                for sub in range(64 // per):
                    block = raw[b, part * 64 + sub * per:part * 64 + (sub + 1) * per].reshape(HEAD, HEAD)
                    moved = dot(sort, block).astype(BF16)
                    for h in range(n_head):
                        g, col = (h // 2, h % 2) if n_head == 8 else (h, first)
                        out_ref[g, pl.ds(to + sub * per, per), col * HEAD:(col + 1) * HEAD] = moved[h * per:(h + 1) * per]

        @pl.when(i + W_SLOTS < n_chunk)
        def _():
            for copy in copies(i + W_SLOTS, b):
                copy.start()


def split_heads(w_q, w_k, w_v):
    d = w_q.shape[0]
    any_spec = pl.BlockSpec(memory_space=pl.ANY)
    return pl.pallas_call(
        heads_kernel,
        out_shape=pltpu.VMEM((4, d, WIDE), BF16),
        in_specs=[any_spec] * 3,
        out_specs=pl.BlockSpec(memory_space=pltpu.VMEM),
        scratch_shapes=[
            pltpu.VMEM((W_SLOTS, W_CHUNK, 8, HEAD), BF16),
            pltpu.VMEM((W_SLOTS, W_CHUNK, 4, HEAD), BF16),
            pltpu.VMEM((W_SLOTS, W_CHUNK, 4, HEAD), BF16),
            pltpu.SemaphoreType.DMA((W_SLOTS, 3)),
        ],
        compiler_params=pltpu.CompilerParams(vmem_limit_bytes=VMEM_BESIDE),
        cost_estimate=pl.CostEstimate(flops=5_000_000_000, bytes_accessed=20_000_000, transcendentals=0),
        name="heads",
    )(w_q, w_k, w_v)


def layer_kernel(n_att, n_ff, n_out, slot, tab_ref, over_ref, ga_ref, gm_ref, cos_ref, sin_ref, wh_ref, h_ref, wo_ref,
                 wg_ref, wu_ref, wd_ref, ck_ref, cv_ref, sib_ref, full_ref, fullf_ref, *rest):
    refs = iter(rest)
    a_ref, b_ref, d_ref, e_ref, o_ref = [next(refs) for _ in range(5)]
    if slot > 0:
        next(refs)
    out_refs = [next(refs) for _ in range(n_out)]
    final_ref, h_rows, act, acc, stage, hist, ring_a, ring_b, sem, own_sem, ring_sem, out_sem = refs
    base = ROW * slot
    seq, start, x_pos, core = tab_ref[base], tab_ref[base + 4], tab_ref[base + 5], tab_ref[base + 6]
    place = tab_ref[base + 7]
    ovf = over_ref[0] > 0
    far = x_pos == 1

    def whole_copies(half):
        to = stage.at[pl.ds(half * HALF, HALF), :]
        fits = far & jnp.logical_not(ovf)
        found = [
            ((x_pos == 0) & (core != half), sib_ref.at[pl.ds(slot * HALF, HALF), :]),
            (far & ovf & (core == half), full_ref.at[place]),
            (far & ovf & (core != half), fullf_ref.at[place]),
        ]
        if half == 0:
            for who, places, ref in ((0, WHOLE_B, b_ref), (1, WHOLE_D, d_ref)):
                mine = 2 * slot + (who + slot) % 2
                if mine in places:
                    found.append((fits & (core == who), ref.at[pl.ds(places.index(mine) * HALF, HALF), :]))
        return [(c, pltpu.make_async_copy(src, to, sem.at[half])) for c, src in found]

    def unit_copies(half, u):
        at = pl.multiple_of((tab_ref[base + 8 + half] + u) * UNIT, UNIT)
        live = far & jnp.logical_not(ovf) & (u < tab_ref[base + 10 + half])
        to = stage.at[pl.ds(pl.multiple_of(half * HALF + u * UNIT, UNIT), UNIT), :]
        if half == 0:
            found = [(live & (core == 1), a_ref)] if slot < 2 else []
        else:
            found = [(live & (core == who), ref) for who, ref in ((0, e_ref), (1, o_ref))] if slot >= 2 else []
        return [(c, pltpu.make_async_copy(src.at[pl.ds(at, UNIT), :], to, sem.at[2 + u])) for c, src in found]

    def own_copies(half):
        rows = pl.ds(half * HALF, HALF)
        return (
            pltpu.make_async_copy(ck_ref.at[seq], hist.at[rows, pl.ds(0, WIDE)], own_sem.at[0]),
            pltpu.make_async_copy(cv_ref.at[seq], hist.at[rows, pl.ds(WIDE, WIDE)], own_sem.at[1]),
        )

    def history(act_on):
        for half in range(2):
            for cond, copy in whole_copies(half):
                @pl.when(cond)
                def _(copy=copy):
                    act_on(copy)

            @pl.when((x_pos == 0) & (core == half))
            def _(half=half):
                for copy in own_copies(half):
                    act_on(copy)

        packed = 0 if slot < 2 else 1

        @pl.loop(0, PER_HALF)
        def _(u):
            for cond, copy in unit_copies(packed, u):
                @pl.when(cond)
                def _(copy=copy):
                    act_on(copy)

    def up_copies(j):
        at = lax.rem(j, DEPTH)
        cols = pl.ds(pl.multiple_of(j * BLK, BLK), BLK)
        return [
            pltpu.make_async_copy(wg_ref.at[:, cols], ring_a.at[2 * at], ring_sem.at[at, 0]),
            pltpu.make_async_copy(wu_ref.at[:, cols], ring_a.at[2 * at + 1], ring_sem.at[at, 1]),
        ]

    def out_copy(i):
        at = lax.rem(i, DEPTH_B)
        rows = pl.ds(pl.multiple_of(i * OUT_BLK, OUT_BLK), OUT_BLK)
        return pltpu.make_async_copy(wo_ref.at[rows, :], ring_b.at[at, pl.ds(0, OUT_BLK), :], ring_sem.at[at, 2])

    def down_copy(j):
        at = lax.rem(j + n_att, DEPTH_B)
        rows = pl.ds(pl.multiple_of(j * BLK, BLK), BLK)
        return pltpu.make_async_copy(wd_ref.at[rows, :], ring_b.at[at], ring_sem.at[at, 2])

    row_copy = pltpu.make_async_copy(h_ref.at[seq], h_rows, own_sem.at[2])
    row_copy.start()
    history(lambda copy: copy.start())
    for i in range(DEPTH_B):
        out_copy(i).start()
    for j in range(DEPTH):
        for copy in up_copies(j):
            copy.start()
    row_copy.wait()
    act[...] = rms_norm(h_rows[...].astype(F32), ga_ref[...])
    acc[...] = h_rows[...].astype(F32)
    history(lambda copy: copy.wait())
    for half in range(2):
        @pl.when((x_pos == 1) | (core != half))
        def _(half=half):
            rows = pl.ds(half * HALF, HALF)
            hist[rows, :] = stage[rows, :].astype(BF16)

    @pl.loop(0, n_att)
    def _(i):
        out_copy(i).wait()
        cos, sin = cos_ref[pl.ds(start, HEAD), :], sin_ref[pl.ds(start, HEAD), :]
        a = act[...]
        off = pl.multiple_of(i * HEAD, HEAD)
        row = lax.broadcasted_iota(jnp.int32, (HEAD, HEAD), 0)
        v_old = jnp.where(row < start, hist[:, pl.ds(off + WIDE, HEAD)], jnp.zeros((), BF16))
        qkv = dot(a, wh_ref[i])
        kv = qkv[:, 512:]
        k_all = jnp.concatenate([hist[:, pl.ds(off, HEAD)], rotate(kv[:, :HEAD], cos, sin).astype(BF16)], axis=0)
        v_all = jnp.concatenate([v_old, kv[:, HEAD:].astype(BF16)], axis=0)
        qs = [(rotate(qkv[:, j * HEAD:(j + 1) * HEAD], cos, sin) * 0.0625).astype(BF16) for j in range(2)]
        row = lax.broadcasted_iota(jnp.int32, (HEAD, 512), 0)
        col = lax.broadcasted_iota(jnp.int32, (HEAD, 512), 1)
        ok = (col < start) | ((col >= HEAD) & (col - HEAD <= row))
        scores = [jnp.where(ok, dot_t(q, k_all), MASK_FLOOR) for q in qs]
        tops = [jnp.max(s, axis=-1, keepdims=True) for s in scores]
        probs = [jnp.exp(s - top) for s, top in zip(scores, tops)]
        dens = [jnp.sum(p, axis=-1, keepdims=True) for p in probs]
        nums = [dot(p.astype(BF16), v_all) for p in probs]
        heads = [(num / den).astype(BF16) for num, den in zip(nums, dens)]
        acc[...] += dot(jnp.concatenate(heads, axis=-1), ring_b[lax.rem(i, DEPTH_B), :OUT_BLK, :])

        @pl.when(i + DEPTH_B < n_att)
        def _():
            out_copy(i + DEPTH_B).start()

        @pl.when(i + DEPTH_B >= n_att)
        def _():
            down_copy(i + DEPTH_B - n_att).start()

    res = acc[...].astype(BF16).astype(F32)
    act[...] = rms_norm(res, gm_ref[...])
    acc[...] = res

    @pl.loop(0, n_ff)
    def _(j):
        at = lax.rem(j, DEPTH)
        for copy in up_copies(j):
            copy.wait()
        down_copy(j).wait()
        c = act[...]
        mid = (gelu_tanh(dot(c, ring_a[2 * at])) * dot(c, ring_a[2 * at + 1])).astype(BF16)
        acc[...] += dot(mid, ring_b[lax.rem(j + n_att, DEPTH_B)])

        @pl.when(j + DEPTH < n_ff)
        def _():
            for copy in up_copies(j + DEPTH):
                copy.start()

        @pl.when(j + DEPTH_B < n_ff)
        def _():
            down_copy(j + DEPTH_B).start()

    size = acc.shape[0] // n_out
    copies = []
    for k in range(n_out):
        rows = pl.ds(k * size, size)
        rounded = acc[rows, :].astype(BF16)
        act[rows, :] = rounded
        acc[rows, :] = rounded.astype(F32)
        copies.append(pltpu.make_async_copy(acc.at[rows, :], out_refs[k], out_sem.at[k]))
        copies[-1].start()
    copies.append(pltpu.make_async_copy(act, final_ref.at[seq], own_sem.at[3]))
    copies[-1].start()
    for copy in copies:
        copy.wait()


def run_layer(slot, table, over, hidden, ga, gm, cos, sin, wh, wo, wg, wu, wd, ck, cv, sib, full, fullf, pieces, final, n_out):
    n_ff = wg.shape[1] // BLK
    any_spec = pl.BlockSpec(memory_space=pl.ANY)
    smem = pl.BlockSpec(memory_space=pltpu.SMEM)
    vmem = pl.BlockSpec(memory_space=pltpu.VMEM)
    d = hidden.shape[2]
    args = list(pieces) + ([final] if final is not None else [])
    flops = 2 * HEAD * d * (KV_WIDE * 2 + WIDE * 2 + 3 * wg.shape[1]) + 1_100_000_000
    return pl.pallas_call(
        functools.partial(layer_kernel, 4, n_ff, n_out, slot),
        out_shape=[pltpu.HBM((HEAD // n_out, d), F32)] * n_out + [jax.ShapeDtypeStruct(hidden.shape, BF16)],
        in_specs=[smem, smem] + [vmem] * 5 + [any_spec] * (10 + len(args)),
        out_specs=[any_spec] * (n_out + 1),
        input_output_aliases={17 + len(pieces): n_out} if final is not None else {},
        scratch_shapes=[
            pltpu.VMEM((HEAD, d), BF16),
            pltpu.VMEM((HEAD, d), BF16),
            pltpu.VMEM((HEAD, d), F32),
            pltpu.VMEM((HEAD, KV_WIDE), F32),
            pltpu.VMEM((HEAD, KV_WIDE), BF16),
            pltpu.VMEM((2 * DEPTH, d, BLK), BF16),
            pltpu.VMEM((DEPTH_B, BLK, d), BF16),
            pltpu.SemaphoreType.DMA((2 + PER_HALF,)),
            pltpu.SemaphoreType.DMA((4,)),
            pltpu.SemaphoreType.DMA((DEPTH_B, 3)),
            pltpu.SemaphoreType.DMA((n_out,)),
        ],
        compiler_params=pltpu.CompilerParams(vmem_limit_bytes=VMEM_BESIDE),
        cost_estimate=pl.CostEstimate(flops=flops, bytes_accessed=160_000_000, transcendentals=0),
    )(table, over, ga, gm, cos, sin, wh, hidden, wo, wg, wu, wd, ck, cv, sib, full, fullf, *args)


def window_kernel(sc_ref, h_ref, ga_ref, cos_ref, sin_ref, wh_ref, ck_ref, cv_ref, ok_ref, ov_ref):
    step = pl.program_id(0)
    lo = lax.axis_index('cp') * HALF
    a_rows, inside = [], []
    for j in range(2):
        first = lo - sc_ref[2 * step + j]
        want = first + lax.broadcasted_iota(jnp.int32, (HALF, HEAD), 0)
        have = lax.broadcasted_iota(jnp.int32, (HALF, HEAD), 1)
        pick = jnp.where(want == have, 1.0, 0.0).astype(BF16)
        a_rows.append(dot(pick, h_ref[j]))
        idx = first + lax.broadcasted_iota(jnp.int32, (HALF, HEAD), 0)
        inside.append((idx >= 0) & (idx < HEAD))
    a = rms_norm(jnp.concatenate(a_rows, axis=0), ga_ref[...])
    here = pl.ds(pl.multiple_of(lo, HALF), HALF)
    cos = jnp.concatenate([cos_ref[here, :]] * 2, axis=0)
    sin = jnp.concatenate([sin_ref[here, :]] * 2, axis=0)
    for g in range(4):
        kv = dot(a, wh_ref[g, :, 512:])
        k = rotate(kv[:, :HEAD], cos, sin).astype(BF16)
        v = kv[:, HEAD:].astype(BF16)
        cols = slice(g * HEAD, (g + 1) * HEAD)
        for j in range(2):
            rows = slice(j * HALF, (j + 1) * HALF)
            ok_ref[j, :, cols] = jnp.where(inside[j], k[rows], ck_ref[j, :, cols])
            ov_ref[j, :, cols] = jnp.where(inside[j], v[rows], cv_ref[j, :, cols])


def write_windows(scalars, hidden, ga, cos, sin, wh, cache_k, cache_v):
    n_seq, rows, width = cache_k.shape
    d = hidden.shape[2]
    one = pl.Buffered(1)
    cache_spec = pl.BlockSpec((2, rows, width), lambda i, sc: (i, 0, 0))
    return pl.pallas_call(
        window_kernel,
        out_shape=[jax.ShapeDtypeStruct(cache_k.shape, BF16)] * 2,
        grid_spec=pltpu.PrefetchScalarGridSpec(
            num_scalar_prefetch=1,
            grid=(n_seq // 2,),
            in_specs=[
                pl.BlockSpec((2, HEAD, d), lambda i, sc: (i, 0, 0)),
                pl.BlockSpec((1, d), lambda i, sc: (0, 0), pipeline_mode=one),
                pl.BlockSpec((512, HALF), lambda i, sc: (0, 0), pipeline_mode=one),
                pl.BlockSpec((512, HALF), lambda i, sc: (0, 0), pipeline_mode=one),
                pl.BlockSpec(memory_space=pltpu.VMEM),
                cache_spec,
                cache_spec,
            ],
            out_specs=[cache_spec, cache_spec],
        ),
        compiler_params=pltpu.CompilerParams(vmem_limit_bytes=VMEM_BESIDE),
        cost_estimate=pl.CostEstimate(flops=2 * n_seq * rows * d * 2 * width, bytes_accessed=60_000_000, transcendentals=0),
        name="cache_window",
    )(scalars, hidden, ga, cos, sin, wh, cache_k, cache_v)


def place_kernel(where, blk, tab_ref, *rest):
    n_part = len(where)
    parts = rest[:n_part]
    out_ref, wide, narrow, in_sem, out_sem = rest[-5:]
    slots = wide.shape[0]
    jobs = [(k, b) for k in range(n_part) for b in range(parts[k].shape[0] // blk)]

    def load(n):
        k, b = jobs[n]
        return pltpu.make_async_copy(parts[k].at[pl.ds(b * blk, blk), :], wide.at[n % slots], in_sem.at[n % slots])

    def store(n):
        k, b = jobs[n]
        entry, first = where[k]
        return pltpu.make_async_copy(narrow.at[n % slots], out_ref.at[tab_ref[entry], pl.ds(first + b * blk, blk), :],
                                     out_sem.at[n % slots])

    for n in range(min(slots, len(jobs))):
        load(n).start()
    for n in range(len(jobs)):
        load(n).wait()
        if n >= slots:
            store(n - slots).wait()

        @pl.loop(0, blk // 16)
        def _(r, n=n):
            rows = pl.ds(pl.multiple_of(r * 16, 16), 16)
            narrow[n % slots, rows, :] = wide[n % slots, rows, :].astype(BF16)

        store(n).start()
        if n + slots < len(jobs):
            load(n + slots).start()
    for n in range(max(0, len(jobs) - slots), len(jobs)):
        store(n).wait()


def place_rows(table, parts, where, out, blk):
    d = parts[0].shape[1]
    any_spec = pl.BlockSpec(memory_space=pl.ANY)
    n_part = len(parts)
    slots = min(8, sum(p.shape[0] // blk for p in parts))
    return pl.pallas_call(
        functools.partial(place_kernel, where, blk),
        out_shape=jax.ShapeDtypeStruct(out.shape, BF16),
        in_specs=[pl.BlockSpec(memory_space=pltpu.SMEM)] + [any_spec] * (n_part + 1),
        out_specs=any_spec,
        scratch_shapes=[
            pltpu.VMEM((slots, blk, d), F32),
            pltpu.VMEM((slots, blk, d), BF16),
            pltpu.SemaphoreType.DMA((slots,)),
            pltpu.SemaphoreType.DMA((slots,)),
        ],
        input_output_aliases={n_part + 1: 0},
        compiler_params=pltpu.CompilerParams(vmem_limit_bytes=VMEM_ALL),
        cost_estimate=pl.CostEstimate(flops=10_000_000, bytes_accessed=sum(p.size for p in parts) * 6, transcendentals=0),
    )(table, *parts, out)


def solution(mesh):
    d2d = [(0, 1), (1, 0), (2, 3), (3, 2)]
    cross = [(0, 2), (1, 3), (2, 0), (3, 1)]

    def send(x, pairs, axis='cp'):
        x = lax.ppermute(x, axis, pairs)
        return x

    def body(hidden, start_pos, cache_k, cache_v, w_q, w_k, w_v, w_o, w_gate, w_up, w_down, norm_attn, norm_mlp):
        n_seq, _, d = hidden.shape
        i32 = jnp.int32
        table, over, cos, sin, ga, gm, *mine = plan_and_pack(start_pos, cache_k, cache_v, norm_attn, norm_mlp)
        piece_a, piece_b, piece_d, piece_e, piece_o, piece_s = mine
        got_a = send(piece_a, [(0, 3)])
        sib = send(piece_s, [(0, 1), (1, 0)])
        got_b = send(piece_b, [(0, 2)])
        got_d = send(piece_d, [(0, 3)])
        got_a, piece_e, piece_o = lax.optimization_barrier((got_a, piece_e, piece_o))
        got_e = send(piece_e, [(1, 2)])
        got_o = send(piece_o, [(1, 3)])

        def send_all(_):
            sid = jnp.arange(n_seq, dtype=i32)
            before = (start_pos[None, :] < start_pos[:, None]) | (
                (start_pos[None, :] == start_pos[:, None]) & (sid[None, :] < sid[:, None]))
            rank = jnp.sum(before.astype(i32), axis=1)
            order = jnp.sum((rank[None, :] == sid[:, None]).astype(i32) * sid[None, :], axis=1)
            got = lax.ppermute(pack_full(order, cache_k, cache_v), 'cp', [(0, 2), (1, 3)])
            return got, lax.ppermute(got, 'cp', [(2, 3), (3, 2)])

        full, full_f = lax.cond(over[0] > 0, send_all, lambda _: tuple(blank(2)), 0)

        w_q, w_k, w_v, full, full_f = lax.optimization_barrier((w_q, w_k, w_v, full, full_f))
        wh = pltpu.with_memory_space_constraint(split_heads(w_q, w_k, w_v), pltpu.VMEM)
        wo = w_o.reshape(-1, d)

        out = None
        tab = table
        parts, where = [], []
        for t in range(4):
            pieces = (got_a, got_b if t > 0 else got_a) + ((got_d, got_e, got_o) if t > 1 else (got_a,) * 3)
            *own, out = run_layer(t, tab, over, hidden, ga, gm, cos, sin, wh, wo, w_gate, w_up, w_down,
                                  cache_k, cache_v, sib, full, full_f, pieces, out, 1)
            tab, own = lax.optimization_barrier((tab, own))
            for rows in own:
                crs = send(rows, cross)
                near = send(rows, d2d)
                dia = send(crs, d2d)
                parts.append((near, crs, dia))
                where.append([(ROW * t + k, 0) for k in (1, 2, 3)])
        start_late, _ = lax.optimization_barrier((start_pos, tab))
        new_k, new_v = write_windows(start_late, hidden, ga, cos, sin, wh, cache_k, cache_v)
        early = [(t, k) for t in range(4) for k in range(3) if t < 3 or k == 0]
        for chosen, blk in ((early, HALF), ([(3, 1)], 32), ([(3, 2)], 32)):
            out = place_rows(tab, [parts[c][k] for c, k in chosen], [where[c][k] for c, k in chosen], out, blk)
        return out, new_k, new_v

    group_spec = P('dp', None, None)
    cache_spec = P('dp', 'cp', None)
    whole_spec = P()
    return jax.shard_map(
        body,
        mesh=mesh,
        in_specs=(group_spec, P('dp'), cache_spec, cache_spec) + (whole_spec,) * 9,
        out_specs=(group_spec, cache_spec, cache_spec),
        check_vma=False,
    )
```

time: 1640 us -> 518 us (0.32)
  matrix products: 846 us -> 0 us
  Pallas kernels: 0 us -> 282 us
  local copies, waits for them, and re-layouts: 227 us -> 0.01 us
  waiting for transfers between devices: 404 us -> 212 us
  other arithmetic: 135 us -> 0 us
  starting transfers between devices: 0.08 us -> 21.3 us
    dot_general x11 -> x0, matrix products: 846 us -> none  [the longest x1 220 us: finish_layer(): jnp.einsum('bcd,df->bcf', normed_mlp, w_gate, preferred_element_type=jnp....]
    psum x1 -> x0, waiting for transfers between devices: 404 us -> none  [local_layer(): packed = lax.psum(packed, 'cp')]
    pallas_call x0 -> x11, Pallas kernels: none -> 282 us  [the longest x4 216 us: run_layer(): pl.pallas_call(functools.partial(layer_kernel, 4, n_ff, n_out, slot), out...]
    ppermute x0 -> x18, waiting for transfers between devices: none -> 212 us  [send(): x = lax.ppermute(x, axis, pairs)]
    gather x96 -> x0, local copies, waits for them, and re-layouts: 116 us -> none
    concatenate x2 -> x0, other arithmetic: 41.9 us -> none  [the longest x1 23.2 us: local_layer(): jnp.concatenate([hist_num * rescale[..., None], (hist_den * rescale)[...,...]
    concatenate x2 -> x0, local copies, waits for them, and re-layouts: 35.2 us -> none  [rotate(): jnp.concatenate([first * cos_tab - second * sin_tab, second * cos_tab + f...]
    sub x2 -> x0, other arithmetic: 31.5 us -> none  [rotate(): first * cos_tab - second * sin_tab]
  transfers between devices with their start and end apart: 2 -> 18, of which waited for: 1 -> 7; matrix products, arithmetic and copies ran while one was open for 19% -> 0% of each run, Pallas kernels for 0% -> 31%
where the time goes in v3:
time: 518 us; the launch traced here: 517 us
  Pallas kernels  282 us (54%)
  waiting for transfers between devices  212 us (41%)
  starting transfers between devices  21.3 us (4%)
    pallas_call x4, Pallas kernels, run_layer(): pl.pallas_call(functools.partial(layer_kernel, 4, n_ff, n_out, slot), out...  216 us
    ppermute x18, waiting for transfers between devices, send(): x = lax.ppermute(x, axis, pairs)  212 us
    pallas_call x1, Pallas kernels, write_windows(): pl.pallas_call(window_kernel, out_shape=[jax.ShapeDtypeStruct(cache_k.sha...  29.5 us
    ppermute x18, starting transfers between devices, send(): x = lax.ppermute(x, axis, pairs)  21.3 us
    pallas_call x3, Pallas kernels, place_rows(): pl.pallas_call(functools.partial(place_kernel, where, blk), out_shape=jax...  19.3 us
  transfers between devices with their start and end apart: 18, of which 7 were waited for; matrix products, arithmetic and copies ran while one was open for 0% of the time, Pallas kernels for 31%

profile of v3, /device:TPU:0, one launch (start us, length us, event | category | flops | bytes accessed | tf_op | source)
XLA Modules:
  0.0 516.8 jit_solution(1426382724680934855)
XLA Ops:
  0.6 0.0 copy-start.2
  0.6 9.2 %pack.1 = (s32[80]{0:T(128)}, s32[1]{0:T(128)}, f32[512,128]{1,0:T(8,128)}, f32[512,128]{1,0:T(8,128)}, f32[1,2304]{1,0:T(1,128)}, /*index=5*/f32[1,2304]{1,0:T(...) custom-call(s32[16]{0:T(128)} %sc_ref, ...), custom_call_target="tpu_custom_call" | custom-call | flops 20000000 | bytes 16000000 | tf_op jit(solution)/shard_map/pack/pallas_call | solution.py:216
  9.9 1.9 collective-permute-start.2
  11.8 2.4 collective-permute-start.3
  14.1 2.6 collective-permute-start.5
  16.8 3.0 collective-permute-start.4
  20.4 8.0 %heads.1.wh_ref = bf16[4,2304,1024]{2,1,0:T(8,128)(2,1)S(1)} custom-call(bf16[2304,8,256]{2,1,0:T(8,128)(2,1)} %q_ref, bf16[2304,4,256]{2,1,0:T(4,128)(2,1)} %k_ref, bf16[2304,4,256]{2,1,0:T(4,128)(2,1)} %v_ref), custom_call_target="tpu_custom_call" | custom-call | flops 5000000000 | bytes 20000000 | tf_op jit(solution)/shard_map/heads/pallas_call | solution.py:332
  28.4 0.1 collective-permute-done.3.rest_0_.rest_1_.rest_2_.rest_3_.rest_4_
  28.5 1.5 collective-permute-start.6
  30.0 1.5 collective-permute-start.7
  31.5 54.0 %shard_map.148 = (f32[256,2304]{1,0:T(8,128)}, bf16[16,256,2304]{2,1,0:T(8,128)(2,1)}) custom-call(s32[80]{0:T(128)} %get-tuple-element.85.tab_ref, s32[1]{0:T(128)} %get-tuple-element.54.over_ref, f32[1,2304]{1,0:T(1,128)} %get-tuple-element.55.ga_ref, f32[1,2304]{1,0:T(1,128)} %get-tuple-element.56.gm_ref, f32[512,128]{1,0:T(8,128)} %get-tuple-element.57.cos_ref, ...), custom_call_target="tpu_custom_call" | custom-call | flops 40962666496 | bytes 160000000 | tf_op jit(solution)/shard_map/pallas_call | solution.py:530
  85.6 13.1 %collective-permute-done.4.rest_1_ = f32[384,2048]{1,0:T(8,128)} collective-permute-done((f32[384,2048]{1,0:T(8,128)}, f32[384,2048]{1,0:T(8,128)}, u32[]{:S(2)}, u32[]{:S(2)}) %collective-permute-start.4) | collective-permute-done | bytes 3145760 | tf_op jit(solution)/shard_map/ppermute | solution.py:672
  98.7 54.0 %shard_map.149 = (f32[256,2304]{1,0:T(8,128)}, bf16[16,256,2304]{2,1,0:T(8,128)(2,1)}) custom-call(s32[80]{0:T(128)} %get-tuple-element.85.tab_ref, s32[1]{0:T(128)} %get-tuple-element.54.over_ref, f32[1,2304]{1,0:T(1,128)} %get-tuple-element.55.ga_ref, f32[1,2304]{1,0:T(1,128)} %get-tuple-element.56.gm_ref, ...), custom_call_target="tpu_custom_call", output_to_operand_aliasing={{1}: (22, {})} | custom-call | flops 40962666496 | bytes 160000000 | tf_op jit(solution)/shard_map/pallas_call | solution.py:530
  152.8 53.9 %shard_map.150 = (f32[256,2304]{1,0:T(8,128)}, bf16[16,256,2304]{2,1,0:T(8,128)(2,1)}) custom-call(s32[80]{0:T(128)} %get-tuple-element.85.tab_ref, s32[1]{0:T(128)} %get-tuple-element.54.over_ref, f32[1,2304]{1,0:T(1,128)} %get-tuple-element.55.ga_ref, f32[1,2304]{1,0:T(1,128)} %get-tuple-element.56.gm_ref, ...), custom_call_target="tpu_custom_call", output_to_operand_aliasing={{1}: (22, {})} | custom-call | flops 40962666496 | bytes 160000000 | tf_op jit(solution)/shard_map/pallas_call | solution.py:530
  206.7 53.9 %shard_map.151 = (f32[256,2304]{1,0:T(8,128)}, bf16[16,256,2304]{2,1,0:T(8,128)(2,1)}) custom-call(s32[80]{0:T(128)} %get-tuple-element.85.tab_ref, s32[1]{0:T(128)} %get-tuple-element.54.over_ref, f32[1,2304]{1,0:T(1,128)} %get-tuple-element.55.ga_ref, f32[1,2304]{1,0:T(1,128)} %get-tuple-element.56.gm_ref, ...), custom_call_target="tpu_custom_call", output_to_operand_aliasing={{1}: (22, {})} | custom-call | flops 40962666496 | bytes 160000000 | tf_op jit(solution)/shard_map/pallas_call | solution.py:530
  260.7 0.0 collective-permute-start.19
  260.7 2.6 collective-permute-start.8
  263.4 0.0 collective-permute-start.17
  263.4 0.2 collective-permute-start.16
  263.6 1.8 collective-permute-start.14
  265.4 0.2 collective-permute-done.19.rest_9_
  265.6 2.6 collective-permute-start.11
  268.2 47.6 %collective-permute-done.8.rest_0_ = f32[256,2304]{1,0:T(8,128)} collective-permute-done((f32[256,2304]{1,0:T(8,128)}, f32[256,2304]{1,0:T(8,128)}, u32[]{:S(2)}, u32[]{:S(2)}) %collective-permute-start.8) | collective-permute-done | bytes 2359328 | tf_op jit(solution)/shard_map/ppermute | solution.py:672
  315.8 50.6 %collective-permute-done.17.rest_7_ = f32[256,2304]{1,0:T(8,128)} collective-permute-done((f32[256,2304]{1,0:T(8,128)}, f32[256,2304]{1,0:T(8,128)}, u32[]{:S(2)}, u32[]{:S(2)}) %collective-permute-start.17) | collective-permute-done | bytes 2359328 | tf_op jit(solution)/shard_map/ppermute | solution.py:672
  366.3 0.5 collective-permute-start.18
  366.8 50.0 %collective-permute-done.14.rest_4_ = f32[256,2304]{1,0:T(8,128)} collective-permute-done((f32[256,2304]{1,0:T(8,128)}, f32[256,2304]{1,0:T(8,128)}, u32[]{:S(2)}, u32[]{:S(2)}) %collective-permute-start.14) | collective-permute-done | bytes 2359328 | tf_op jit(solution)/shard_map/ppermute | solution.py:672
  416.9 50.3 %collective-permute-done.11.rest_1_ = f32[256,2304]{1,0:T(8,128)} collective-permute-done((f32[256,2304]{1,0:T(8,128)}, f32[256,2304]{1,0:T(8,128)}, u32[]{:S(2)}, u32[]{:S(2)}) %collective-permute-start.11) | collective-permute-done | bytes 2359328 | tf_op jit(solution)/shard_map/ppermute | solution.py:672
  467.2 0.5 collective-permute-start.9
  467.7 29.5 %cache_window.1 = (bf16[16,128,1024]{2,1,0:T(8,128)(2,1)}, bf16[16,128,1024]{2,1,0:T(8,128)(2,1)}) custom-call(s32[16]{0:T(128)S(1)} %copy-done.3, bf16[16,256,2304]{2,1,0:T(8,128)(2,1)} %h_ref.9, f32[1,2304]{1,0:T(1,128)} %get-tuple-element.55.ga_ref, f32[512,128]{1,0:T(8,128)} %get-tuple-element.57.cos_ref, f32[512,128]{1,0:T(8,128)} %get-tuple-element.58.sin_ref, ...), custom_call_target="tpu_custom_call" | custom-call | flops 19327352832 | bytes 60000000 | tf_op jit(solution)/shard_map/cache_window/pallas_call | solution.py:586
  497.3 13.1 %shard_map.152.rest_1_ = bf16[16,256,2304]{2,1,0:T(8,128)(2,1)} custom-call(s32[80]{0:T(128)} %get-tuple-element.85.tab_ref, f32[256,2304]{1,0:T(8,128)} %collective-permute-done.10.rest_0_, f32[256,2304]{1,0:T(8,128)} %collective-permute-done.11.rest_1_, f32[256,2304]{1,0:T(8,128)} %collective-permute-done.12.rest_2_, ...), custom_call_target="tpu_custom_call", output_to_operand_aliasing={{}: (11, {})} | custom-call | flops 10000000 | bytes 35389440 | tf_op jit(solution)/shard_map/pallas_call | solution.py:650
  510.5 3.1 shard_map.153.rest_1_
  513.5 3.1 shard_map.154
  (20 shorter events, 0.1 us)
Async XLA Ops:
  0.6 19.7 %copy-start.2 = (s32[16]{0:T(128)S(1)}, s32[16]{0:T(128)}, u32[]{:S(2)}) copy-start(s32[16]{0:T(128)} %sc_ref) | copy-start | bytes 196
  9.9 21.7 %collective-permute-start.2 = (f32[512,2048]{1,0:T(8,128)}, f32[512,2048]{1,0:T(8,128)}, u32[]{:S(2)}, u32[]{:S(2)}) collective-permute-start(f32[512,2048]{1,0:T(8,128)} %get-tuple-element.64), channel_id=1, source_target_pairs={{0,1},{1,0},{4,5},{5,4}} | collective-permute-start | bytes 12582920 | tf_op jit(solution)/shard_map/ppermute | solution.py:672
  11.8 16.7 %collective-permute-start.3 = (f32[160,2048]{1,0:T(8,128)}, f32[160,2048]{1,0:T(8,128)}, u32[]{:S(2)}, u32[]{:S(2)}) collective-permute-start(f32[160,2048]{1,0:T(8,128)} %get-tuple-element.67), channel_id=1, source_target_pairs={{0,3},{4,7}} | collective-permute-start | bytes 3932168 | tf_op jit(solution)/shard_map/ppermute | solution.py:672
  14.1 138.6 %collective-permute-start.5 = (f32[256,2048]{1,0:T(8,128)}, f32[256,2048]{1,0:T(8,128)}, u32[]{:S(2)}, u32[]{:S(2)}) collective-permute-start(f32[256,2048]{1,0:T(8,128)} %get-tuple-element.77), channel_id=1, source_target_pairs={{0,3},{4,7}} | collective-permute-start | bytes 6291464 | tf_op jit(solution)/shard_map/ppermute | solution.py:672
  16.8 81.9 %collective-permute-start.4 = (f32[384,2048]{1,0:T(8,128)}, f32[384,2048]{1,0:T(8,128)}, u32[]{:S(2)}, u32[]{:S(2)}) collective-permute-start(f32[384,2048]{1,0:T(8,128)} %get-tuple-element.73), channel_id=1, source_target_pairs={{0,2},{4,6}} | collective-permute-start | bytes 9437192 | tf_op jit(solution)/shard_map/ppermute | solution.py:672
  28.5 124.2 %collective-permute-start.6 = (f32[80,2048]{1,0:T(8,128)}, f32[80,2048]{1,0:T(8,128)}, u32[]{:S(2)}, u32[]{:S(2)}) collective-permute-start(f32[80,2048]{1,0:T(8,128)} %get-tuple-element.78), channel_id=1, source_target_pairs={{1,2},{5,6}} | collective-permute-start | bytes 1966088 | tf_op jit(solution)/shard_map/ppermute | solution.py:672
  30.0 122.7 %collective-permute-start.7 = (f32[80,2048]{1,0:T(8,128)}, f32[80,2048]{1,0:T(8,128)}, u32[]{:S(2)}, u32[]{:S(2)}) collective-permute-start(f32[80,2048]{1,0:T(8,128)} %get-tuple-element.79), channel_id=1, source_target_pairs={{1,3},{5,7}} | collective-permute-start | bytes 1966088 | tf_op jit(solution)/shard_map/ppermute | solution.py:672
  206.7 261.0 %copy-start.3 = (s32[16]{0:T(128)S(1)}, s32[16]{0:T(128)}, u32[]{:S(2)}) copy-start(s32[16]{0:T(128)} %sc_ref) | copy-start | bytes 196
  260.7 4.9 collective-permute-start.19
  260.7 55.1 %collective-permute-start.8 = (f32[256,2304]{1,0:T(8,128)}, f32[256,2304]{1,0:T(8,128)}, u32[]{:S(2)}, u32[]{:S(2)}) collective-permute-start(f32[256,2304]{1,0:T(8,128)} %get-tuple-element.86), channel_id=1, source_target_pairs={{0,2},{1,3},{2,0},{3,1},{4,6},{5,7},{6,4},{7,5}} | collective-permute-start | bytes 7077896 | tf_op jit(solution)/shard_map/ppermute | solution.py:672
  263.4 103.0 %collective-permute-start.17 = (f32[256,2304]{1,0:T(8,128)}, f32[256,2304]{1,0:T(8,128)}, u32[]{:S(2)}, u32[]{:S(2)}) collective-permute-start(f32[256,2304]{1,0:T(8,128)} %get-tuple-element.89), channel_id=1, source_target_pairs={{0,2},{1,3},{2,0},{3,1},{4,6},{5,7},{6,4},{7,5}} | collective-permute-start | bytes 7077896 | tf_op jit(solution)/shard_map/ppermute | solution.py:672
  263.4 102.9 %collective-permute-start.16 = (f32[256,2304]{1,0:T(8,128)}, f32[256,2304]{1,0:T(8,128)}, u32[]{:S(2)}, u32[]{:S(2)}) collective-permute-start(f32[256,2304]{1,0:T(8,128)} %get-tuple-element.89), channel_id=1, source_target_pairs={{0,1},{1,0},{2,3},{3,2},{4,5},{5,4},{6,7},{7,6}} | collective-permute-start | bytes 7077896 | tf_op jit(solution)/shard_map/ppermute | solution.py:672
  263.6 153.3 %collective-permute-start.14 = (f32[256,2304]{1,0:T(8,128)}, f32[256,2304]{1,0:T(8,128)}, u32[]{:S(2)}, u32[]{:S(2)}) collective-permute-start(f32[256,2304]{1,0:T(8,128)} %get-tuple-element.88), channel_id=1, source_target_pairs={{0,2},{1,3},{2,0},{3,1},{4,6},{5,7},{6,4},{7,5}} | collective-permute-start | bytes 7077896 | tf_op jit(solution)/shard_map/ppermute | solution.py:672
  265.6 201.7 %collective-permute-start.11 = (f32[256,2304]{1,0:T(8,128)}, f32[256,2304]{1,0:T(8,128)}, u32[]{:S(2)}, u32[]{:S(2)}) collective-permute-start(f32[256,2304]{1,0:T(8,128)} %get-tuple-element.87), channel_id=1, source_target_pairs={{0,2},{1,3},{2,0},{3,1},{4,6},{5,7},{6,4},{7,5}} | collective-permute-start | bytes 7077896 | tf_op jit(solution)/shard_map/ppermute | solution.py:672
  315.8 151.5 %collective-permute-start.13 = (f32[256,2304]{1,0:T(8,128)}, f32[256,2304]{1,0:T(8,128)}, u32[]{:S(2)}, u32[]{:S(2)}) collective-permute-start(f32[256,2304]{1,0:T(8,128)} %get-tuple-element.88), channel_id=1, source_target_pairs={{0,1},{1,0},{2,3},{3,2},{4,5},{5,4},{6,7},{7,6}} | collective-permute-start | bytes 7077896 | tf_op jit(solution)/shard_map/ppermute | solution.py:672
  366.3 130.9 %collective-permute-start.10 = (f32[256,2304]{1,0:T(8,128)}, f32[256,2304]{1,0:T(8,128)}, u32[]{:S(2)}, u32[]{:S(2)}) collective-permute-start(f32[256,2304]{1,0:T(8,128)} %get-tuple-element.87), channel_id=1, source_target_pairs={{0,1},{1,0},{2,3},{3,2},{4,5},{5,4},{6,7},{7,6}} | collective-permute-start | bytes 7077896 | tf_op jit(solution)/shard_map/ppermute | solution.py:672
  366.3 130.9 %collective-permute-start.18 = (f32[256,2304]{1,0:T(8,128)}, f32[256,2304]{1,0:T(8,128)}, u32[]{:S(2)}, u32[]{:S(2)}) collective-permute-start(f32[256,2304]{1,0:T(8,128)} %collective-permute-done.17.rest_7_), channel_id=1, source_target_pairs={{0,1},{1,0},{2,3},{3,2},{4,5},{5,4},{6,7},{7,6}} | collective-permute-start | bytes 7077896 | tf_op jit(solution)/shard_map/ppermute | solution.py:672
  416.9 80.4 %collective-permute-start.15 = (f32[256,2304]{1,0:T(8,128)}, f32[256,2304]{1,0:T(8,128)}, u32[]{:S(2)}, u32[]{:S(2)}) collective-permute-start(f32[256,2304]{1,0:T(8,128)} %collective-permute-done.14.rest_4_), channel_id=1, source_target_pairs={{0,1},{1,0},{2,3},{3,2},{4,5},{5,4},{6,7},{7,6}} | collective-permute-start | bytes 7077896 | tf_op jit(solution)/shard_map/ppermute | solution.py:672
  467.2 30.1 %collective-permute-start.12 = (f32[256,2304]{1,0:T(8,128)}, f32[256,2304]{1,0:T(8,128)}, u32[]{:S(2)}, u32[]{:S(2)}) collective-permute-start(f32[256,2304]{1,0:T(8,128)} %collective-permute-done.11.rest_1_), channel_id=1, source_target_pairs={{0,1},{1,0},{2,3},{3,2},{4,5},{5,4},{6,7},{7,6}} | collective-permute-start | bytes 7077896 | tf_op jit(solution)/shard_map/ppermute | solution.py:672
  467.2 46.3 %collective-permute-start.9 = (f32[256,2304]{1,0:T(8,128)}, f32[256,2304]{1,0:T(8,128)}, u32[]{:S(2)}, u32[]{:S(2)}) collective-permute-start(f32[256,2304]{1,0:T(8,128)} %collective-permute-done.8.rest_0_), channel_id=1, source_target_pairs={{0,1},{1,0},{2,3},{3,2},{4,5},{5,4},{6,7},{7,6}} | collective-permute-start | bytes 7077896 | tf_op jit(solution)/shard_map/ppermute | solution.py:672

commit v4 on v3

--- a/solution.py
+++ b/solution.py
@@ -26,6 +26,7 @@
 B_ROWS, D_ROWS, S_ROWS = len(WHOLE_B) * HALF, len(WHOLE_D) * HALF, 4 * HALF
 ROW = 16
 OUT_BLK = 512
+STEP_ROWS = 64
 BLK = 768
 VMEM_BESIDE = 48_100_000
 VMEM_ALL = 66_900_000
@@ -130,34 +131,33 @@
                 for copy in copies(order[j], row, pl.multiple_of(to + at * UNIT, UNIT), UNIT, sem + at):
                     act(copy)
 
-    def each(act):
-        @pl.when(core == 0)
-        def _():
+    def reads(name, act):
+        if name == "A":
             for j in (1, 2):
                 units(0, j, first["A"], 0, act)
-
-        @pl.when(core == 1)
-        def _():
+        elif name == "E":
             for j in (4, 7):
                 units(1, j, first["E"], 0, act)
+        elif name == "O":
             for j in (5, 6):
                 units(1, j, first["O"], C_UNITS, act)
-
-        for t in range(4):
-            seq = order[8 + 2 * t + (1 - core + t) % 2]
-            for copy in copies(seq, 0, first["S"] + t * HALF, HALF, A_UNITS + t):
-                act(copy)
-
-        @pl.when(core == 0)
-        def _():
-            for k, j in enumerate(WHOLE_B + WHOLE_D):
-                for copy in copies(order[j], 0, first["B"] + k * HALF, HALF, A_UNITS + 4 + k):
+        elif name == "S":
+            for t in range(4):
+                seq = order[8 + 2 * t + (1 - core + t) % 2]
+                for copy in copies(seq, 0, first["S"] + t * HALF, HALF, A_UNITS + t):
+                    act(copy)
+        else:
+            places, sem = (WHOLE_B, A_UNITS + 4) if name == "B" else (WHOLE_D, A_UNITS + 4 + len(WHOLE_B))
+            for k, j in enumerate(places):
+                for copy in copies(order[j], 0, first[name] + k * HALF, HALF, sem + k):
                     act(copy)
 
     def out_copy(k, name):
         return pltpu.make_async_copy(wide.at[pl.ds(first[name], size[name]), :], outs[k], out_sem.at[k])
 
     def widen(k, name):
+        reads(name, lambda copy: copy.wait())
+
         @pl.loop(0, size[name] // UNIT)
         def _(u):
             rows = pl.ds(pl.multiple_of(first[name] + u * UNIT, UNIT), UNIT)
@@ -165,9 +165,11 @@
 
         out_copy(k, name).start()
 
-    @pl.when(x_pos == 0)
-    def _():
-        each(lambda copy: copy.start())
+    for who, names in enumerate(("ASBD", "SEO")):
+        @pl.when((x_pos == 0) & (core == who))
+        def _(names=names):
+            for name in names:
+                reads(name, lambda copy: copy.start())
 
     ga_out[...] = ga_ref[...].astype(F32).reshape(ga_out.shape)
     gm_out[...] = gm_ref[...].astype(F32).reshape(gm_out.shape)
@@ -183,28 +185,13 @@
         cos_ref[rows, :] = ca * cos_b - sa * sin_b
         sin_ref[rows, :] = sa * cos_b + ca * sin_b
 
-    @pl.when(x_pos == 0)
-    def _():
-        each(lambda copy: copy.wait())
-
-        @pl.when(core == 0)
-        def _():
-            widen(0, "A")
-            widen(5, "S")
-            widen(1, "B")
-            widen(2, "D")
-            for k, name in enumerate("ABD"):
-                out_copy(k, name).wait()
-
-        @pl.when(core == 1)
-        def _():
-            widen(5, "S")
-            widen(3, "E")
-            widen(4, "O")
-            for k, name in enumerate("EO"):
-                out_copy(3 + k, name).wait()
-
-        out_copy(5, "S").wait()
+    for who, names in enumerate(("ASBD", "SEO")):
+        @pl.when((x_pos == 0) & (core == who))
+        def _(names=names):
+            for name in names:
+                widen("ABDEOS".index(name), name)
+            for name in names:
+                out_copy("ABDEOS".index(name), name).wait()
 
 
 def plan_and_pack(start_pos, cache_k, cache_v, ga, gm):
@@ -346,13 +333,13 @@
     )(w_q, w_k, w_v)
 
 
-def layer_kernel(n_att, n_ff, n_out, slot, tab_ref, over_ref, ga_ref, gm_ref, cos_ref, sin_ref, wh_ref, h_ref, wo_ref,
+def layer_kernel(n_att, n_ff, sizes, slot, tab_ref, over_ref, ga_ref, gm_ref, cos_ref, sin_ref, wh_ref, h_ref, wo_ref,
                  wg_ref, wu_ref, wd_ref, ck_ref, cv_ref, sib_ref, full_ref, fullf_ref, *rest):
     refs = iter(rest)
     a_ref, b_ref, d_ref, e_ref, o_ref = [next(refs) for _ in range(5)]
     if slot > 0:
         next(refs)
-    out_refs = [next(refs) for _ in range(n_out)]
+    out_refs = [next(refs) for _ in sizes]
     final_ref, h_rows, act, acc, stage, hist, ring_a, ring_b, sem, own_sem, ring_sem, out_sem = refs
     base = ROW * slot
     seq, start, x_pos, core = tab_ref[base], tab_ref[base + 4], tab_ref[base + 5], tab_ref[base + 6]
@@ -441,13 +428,20 @@
             copy.start()
     row_copy.wait()
     act[...] = rms_norm(h_rows[...].astype(F32), ga_ref[...])
-    acc[...] = h_rows[...].astype(F32)
+
+    @pl.loop(0, HEAD // UNIT)
+    def _(u):
+        rows = pl.ds(pl.multiple_of(u * UNIT, UNIT), UNIT)
+        acc[rows, :] = h_rows[rows, :].astype(F32)
+
     history(lambda copy: copy.wait())
     for half in range(2):
         @pl.when((x_pos == 1) | (core != half))
         def _(half=half):
-            rows = pl.ds(half * HALF, HALF)
-            hist[rows, :] = stage[rows, :].astype(BF16)
+            @pl.loop(0, PER_HALF)
+            def _(u):
+                rows = pl.ds(pl.multiple_of(half * HALF + u * UNIT, UNIT), UNIT)
+                hist[rows, :] = stage[rows, :].astype(BF16)
 
     @pl.loop(0, n_att)
     def _(i):
@@ -504,22 +498,30 @@
         def _():
             down_copy(j + DEPTH_B).start()
 
-    size = acc.shape[0] // n_out
     copies = []
-    for k in range(n_out):
-        rows = pl.ds(k * size, size)
-        rounded = acc[rows, :].astype(BF16)
-        act[rows, :] = rounded
-        acc[rows, :] = rounded.astype(F32)
-        copies.append(pltpu.make_async_copy(acc.at[rows, :], out_refs[k], out_sem.at[k]))
-        copies[-1].start()
-    copies.append(pltpu.make_async_copy(act, final_ref.at[seq], own_sem.at[3]))
-    copies[-1].start()
+    first = 0
+    for k, size in enumerate(sizes):
+        for r in range(0, size, STEP_ROWS):
+            block = first // STEP_ROWS
+
+            @pl.loop(0, STEP_ROWS // UNIT)
+            def _(u, first=first):
+                rows = pl.ds(pl.multiple_of(first + u * UNIT, UNIT), UNIT)
+                rounded = acc[rows, :].astype(BF16)
+                act[rows, :] = rounded
+                acc[rows, :] = rounded.astype(F32)
+
+            rows, to = pl.ds(first, STEP_ROWS), pl.ds(r, STEP_ROWS)
+            copies.append(pltpu.make_async_copy(acc.at[rows, :], out_refs[k].at[to, :], out_sem.at[block, 0]))
+            copies.append(pltpu.make_async_copy(act.at[rows, :], final_ref.at[seq, rows, :], out_sem.at[block, 1]))
+            for copy in copies[-2:]:
+                copy.start()
+            first += STEP_ROWS
     for copy in copies:
         copy.wait()
 
 
-def run_layer(slot, table, over, hidden, ga, gm, cos, sin, wh, wo, wg, wu, wd, ck, cv, sib, full, fullf, pieces, final, n_out):
+def run_layer(slot, table, over, hidden, ga, gm, cos, sin, wh, wo, wg, wu, wd, ck, cv, sib, full, fullf, pieces, final, sizes):
     n_ff = wg.shape[1] // BLK
     any_spec = pl.BlockSpec(memory_space=pl.ANY)
     smem = pl.BlockSpec(memory_space=pltpu.SMEM)
@@ -528,11 +530,11 @@
     args = list(pieces) + ([final] if final is not None else [])
     flops = 2 * HEAD * d * (KV_WIDE * 2 + WIDE * 2 + 3 * wg.shape[1]) + 1_100_000_000
     return pl.pallas_call(
-        functools.partial(layer_kernel, 4, n_ff, n_out, slot),
-        out_shape=[pltpu.HBM((HEAD // n_out, d), F32)] * n_out + [jax.ShapeDtypeStruct(hidden.shape, BF16)],
+        functools.partial(layer_kernel, 4, n_ff, sizes, slot),
+        out_shape=[pltpu.HBM((n, d), F32) for n in sizes] + [jax.ShapeDtypeStruct(hidden.shape, BF16)],
         in_specs=[smem, smem] + [vmem] * 5 + [any_spec] * (10 + len(args)),
-        out_specs=[any_spec] * (n_out + 1),
-        input_output_aliases={17 + len(pieces): n_out} if final is not None else {},
+        out_specs=[any_spec] * (len(sizes) + 1),
+        input_output_aliases={17 + len(pieces): len(sizes)} if final is not None else {},
         scratch_shapes=[
             pltpu.VMEM((HEAD, d), BF16),
             pltpu.VMEM((HEAD, d), BF16),
@@ -542,9 +544,9 @@
             pltpu.VMEM((2 * DEPTH, d, BLK), BF16),
             pltpu.VMEM((DEPTH_B, BLK, d), BF16),
             pltpu.SemaphoreType.DMA((2 + PER_HALF,)),
-            pltpu.SemaphoreType.DMA((4,)),
+            pltpu.SemaphoreType.DMA((3,)),
             pltpu.SemaphoreType.DMA((DEPTH_B, 3)),
-            pltpu.SemaphoreType.DMA((n_out,)),
+            pltpu.SemaphoreType.DMA((HEAD // STEP_ROWS, 2)),
         ],
         compiler_params=pltpu.CompilerParams(vmem_limit_bytes=VMEM_BESIDE),
         cost_estimate=pl.CostEstimate(flops=flops, bytes_accessed=160_000_000, transcendentals=0),
@@ -706,19 +708,27 @@
         for t in range(4):
             pieces = (got_a, got_b if t > 0 else got_a) + ((got_d, got_e, got_o) if t > 1 else (got_a,) * 3)
             *own, out = run_layer(t, tab, over, hidden, ga, gm, cos, sin, wh, wo, w_gate, w_up, w_down,
-                                  cache_k, cache_v, sib, full, full_f, pieces, out, 1)
+                                  cache_k, cache_v, sib, full, full_f, pieces, out, (192, 64) if t == 3 else (HEAD,))
             tab, own = lax.optimization_barrier((tab, own))
-            for rows in own:
-                crs = send(rows, cross)
-                near = send(rows, d2d)
+            if t < 3:
+                crs = send(own[0], cross)
+                near = send(own[0], d2d)
                 dia = send(crs, d2d)
-                parts.append((near, crs, dia))
-                where.append([(ROW * t + k, 0) for k in (1, 2, 3)])
+                parts += [near, crs, dia]
+                where += [(ROW * t + k, 0) for k in (1, 2, 3)]
+        most, rest = own
+        crs_most, near_most = send(most, cross), send(most, d2d)
         start_late, _ = lax.optimization_barrier((start_pos, tab))
         new_k, new_v = write_windows(start_late, hidden, ga, cos, sin, wh, cache_k, cache_v)
-        early = [(t, k) for t in range(4) for k in range(3) if t < 3 or k == 0]
-        for chosen, blk in ((early, HALF), ([(3, 1)], 32), ([(3, 2)], 32)):
-            out = place_rows(tab, [parts[c][k] for c, k in chosen], [where[c][k] for c, k in chosen], out, blk)
+        rest, new_k = lax.optimization_barrier((rest, new_k))
+        crs_rest, near_rest = send(rest, cross), send(rest, d2d)
+        dia_most, dia_rest = send(crs_most, d2d), send(crs_rest, d2d)
+        last = ROW * 3
+        out = place_rows(tab, parts + [near_most], where + [(last + 1, 0)], out, 64)
+        out = place_rows(tab, [crs_most, near_rest], [(last + 2, 0), (last + 1, 192)], out, 64)
+        out = place_rows(tab, [dia_most], [(last + 3, 0)], out, 64)
+        out = place_rows(tab, [crs_rest], [(last + 2, 192)], out, 16)
+        out = place_rows(tab, [dia_rest], [(last + 3, 192)], out, 16)
         return out, new_k, new_v
 
     group_spec = P('dp', None, None)

time: 518 us -> 497 us (0.959)
  waiting for transfers between devices: 212 us -> 185 us
    ppermute x18 -> x21, waiting for transfers between devices: 212 us -> 185 us  [send(): x = lax.ppermute(x, axis, pairs)]
    pallas_call x3 -> x5, Pallas kernels: 19.3 us -> 23.9 us  [place_rows(): pl.pallas_call(functools.partial(place_kernel, where, blk), out_shape=jax...]
    ppermute x18 -> x21, starting transfers between devices: 21.3 us -> 20.2 us  [send(): x = lax.ppermute(x, axis, pairs)]
  transfers between devices with their start and end apart: 18 -> 21, of which waited for: 7 -> 7; matrix products, arithmetic and copies ran while one was open for 0% -> 0% of each run, Pallas kernels for 31% -> 34%
where the time goes in v4:
time: 497 us; the launch traced here: 496 us
  Pallas kernels  285 us (57%)
  waiting for transfers between devices  185 us (37%)
  starting transfers between devices  20.2 us (4%)
    pallas_call x4, Pallas kernels, run_layer(): pl.pallas_call(functools.partial(layer_kernel, 4, n_ff, sizes, slot), out...  215 us
    ppermute x21, waiting for transfers between devices, send(): x = lax.ppermute(x, axis, pairs)  185 us
    pallas_call x1, Pallas kernels, write_windows(): pl.pallas_call(window_kernel, out_shape=[jax.ShapeDtypeStruct(cache_k.sha...  29.5 us
    pallas_call x5, Pallas kernels, place_rows(): pl.pallas_call(functools.partial(place_kernel, where, blk), out_shape=jax...  23.9 us
    ppermute x21, starting transfers between devices, send(): x = lax.ppermute(x, axis, pairs)  20.2 us
  transfers between devices with their start and end apart: 21, of which 7 were waited for; matrix products, arithmetic and copies ran while one was open for 0% of the time, Pallas kernels for 34%

profile of v4, /device:TPU:0, one launch (start us, length us, event | category | flops | bytes accessed | tf_op | source)
XLA Modules:
  0.0 495.5 jit_solution(13642108098070167019)
XLA Ops:
  0.6 8.3 %pack.1 = (s32[80]{0:T(128)}, s32[1]{0:T(128)}, f32[512,128]{1,0:T(8,128)}, f32[512,128]{1,0:T(8,128)}, f32[1,2304]{1,0:T(1,128)}, /*index=5*/f32[1,2304]{1,0:T(...) custom-call(s32[16]{0:T(128)} %sc_ref, ...), custom_call_target="tpu_custom_call" | custom-call | flops 20000000 | bytes 16000000 | tf_op jit(solution)/shard_map/pack/pallas_call | solution.py:203
  8.9 1.9 collective-permute-start.2
  10.9 2.3 collective-permute-start.3
  13.2 2.6 collective-permute-start.5
  15.8 2.9 collective-permute-start.4
  19.4 8.0 %heads.1.wh_ref = bf16[4,2304,1024]{2,1,0:T(8,128)(2,1)S(1)} custom-call(bf16[2304,8,256]{2,1,0:T(8,128)(2,1)} %q_ref, bf16[2304,4,256]{2,1,0:T(4,128)(2,1)} %k_ref, bf16[2304,4,256]{2,1,0:T(4,128)(2,1)} %v_ref), custom_call_target="tpu_custom_call" | custom-call | flops 5000000000 | bytes 20000000 | tf_op jit(solution)/shard_map/heads/pallas_call | solution.py:319
  27.6 1.5 collective-permute-start.6
  29.1 1.5 collective-permute-start.7
  30.6 53.9 %shard_map.148 = (f32[256,2304]{1,0:T(8,128)}, bf16[16,256,2304]{2,1,0:T(8,128)(2,1)}) custom-call(s32[80]{0:T(128)} %get-tuple-element.90.tab_ref, s32[1]{0:T(128)} %get-tuple-element.58.over_ref, f32[1,2304]{1,0:T(1,128)} %get-tuple-element.59.ga_ref, f32[1,2304]{1,0:T(1,128)} %get-tuple-element.60.gm_ref, f32[512,128]{1,0:T(8,128)} %get-tuple-element.61.cos_ref, ...), custom_call_target="tpu_custom_call" | custom-call | flops 40962666496 | bytes 160000000 | tf_op jit(solution)/shard_map/pallas_call | solution.py:532
  84.5 13.3 %collective-permute-done.4.rest_1_ = f32[384,2048]{1,0:T(8,128)} collective-permute-done((f32[384,2048]{1,0:T(8,128)}, f32[384,2048]{1,0:T(8,128)}, u32[]{:S(2)}, u32[]{:S(2)}) %collective-permute-start.4) | collective-permute-done | bytes 3145760 | tf_op jit(solution)/shard_map/ppermute | solution.py:674
  97.8 53.8 %shard_map.149 = (f32[256,2304]{1,0:T(8,128)}, bf16[16,256,2304]{2,1,0:T(8,128)(2,1)}) custom-call(s32[80]{0:T(128)} %get-tuple-element.90.tab_ref, s32[1]{0:T(128)} %get-tuple-element.58.over_ref, f32[1,2304]{1,0:T(1,128)} %get-tuple-element.59.ga_ref, f32[1,2304]{1,0:T(1,128)} %get-tuple-element.60.gm_ref, ...), custom_call_target="tpu_custom_call", output_to_operand_aliasing={{1}: (22, {})} | custom-call | flops 40962666496 | bytes 160000000 | tf_op jit(solution)/shard_map/pallas_call | solution.py:532
  151.7 53.8 %shard_map.150 = (f32[256,2304]{1,0:T(8,128)}, bf16[16,256,2304]{2,1,0:T(8,128)(2,1)}) custom-call(s32[80]{0:T(128)} %get-tuple-element.90.tab_ref, s32[1]{0:T(128)} %get-tuple-element.58.over_ref, f32[1,2304]{1,0:T(1,128)} %get-tuple-element.59.ga_ref, f32[1,2304]{1,0:T(1,128)} %get-tuple-element.60.gm_ref, ...), custom_call_target="tpu_custom_call", output_to_operand_aliasing={{1}: (22, {})} | custom-call | flops 40962666496 | bytes 160000000 | tf_op jit(solution)/shard_map/pallas_call | solution.py:532
  205.5 53.8 %shard_map.151 = (f32[192,2304]{1,0:T(8,128)}, f32[64,2304]{1,0:T(8,128)}, bf16[16,256,2304]{2,1,0:T(8,128)(2,1)}) custom-call(s32[80]{0:T(128)} %get-tuple-element.90.tab_ref, s32[1]{0:T(128)} %get-tuple-element.58.over_ref, f32[1,2304]{1,0:T(1,128)} %get-tuple-element.59.ga_ref, ...), custom_call_target="tpu_custom_call", output_to_operand_aliasing={{2}: (22, {})} | custom-call | flops 40962666496 | bytes 160000000 | tf_op jit(solution)/shard_map/pallas_call | solution.py:532
  259.4 2.2 collective-permute-start.10
  261.6 29.5 %cache_window.1 = (bf16[16,128,1024]{2,1,0:T(8,128)(2,1)}, bf16[16,128,1024]{2,1,0:T(8,128)(2,1)}) custom-call(s32[16]{0:T(128)S(1)} %copy-done.10, bf16[16,256,2304]{2,1,0:T(8,128)(2,1)} %h_ref.9, f32[1,2304]{1,0:T(1,128)} %get-tuple-element.59.ga_ref, f32[512,128]{1,0:T(8,128)} %get-tuple-element.61.cos_ref, f32[512,128]{1,0:T(8,128)} %get-tuple-element.62.sin_ref, ...), custom_call_target="tpu_custom_call" | custom-call | flops 19327352832 | bytes 60000000 | tf_op jit(solution)/shard_map/cache_window/pallas_call | solution.py:588
  291.2 2.0 collective-permute-start.20
  293.2 20.9 %collective-permute-done.8.rest_0_ = f32[64,2304]{1,0:T(8,128)} collective-permute-done((f32[64,2304]{1,0:T(8,128)}, f32[64,2304]{1,0:T(8,128)}, u32[]{:S(2)}, u32[]{:S(2)}) %collective-permute-start.8) | collective-permute-done | bytes 589856 | tf_op jit(solution)/shard_map/ppermute | solution.py:674
  314.0 2.0 collective-permute-start.17
  316.1 48.4 %collective-permute-done.20.rest_7_ = f32[256,2304]{1,0:T(8,128)S(1)} collective-permute-done((f32[256,2304]{1,0:T(8,128)}, f32[256,2304]{1,0:T(8,128)S(1)}, u32[]{:S(2)}, u32[]{:S(2)}) %collective-permute-start.20) | collective-permute-done | bytes 2359328 | tf_op jit(solution)/shard_map/ppermute | solution.py:674
  364.5 1.4 copy-done
  365.9 49.1 %collective-permute-done.17.rest_4_ = f32[256,2304]{1,0:T(8,128)S(1)} collective-permute-done((f32[256,2304]{1,0:T(8,128)}, f32[256,2304]{1,0:T(8,128)S(1)}, u32[]{:S(2)}, u32[]{:S(2)}) %collective-permute-start.17) | collective-permute-done | bytes 2359328 | tf_op jit(solution)/shard_map/ppermute | solution.py:674
  415.0 50.3 %collective-permute-done.14.rest_1_ = f32[256,2304]{1,0:T(8,128)S(1)} collective-permute-done((f32[256,2304]{1,0:T(8,128)}, f32[256,2304]{1,0:T(8,128)S(1)}, u32[]{:S(2)}, u32[]{:S(2)}) %collective-permute-start.14) | collective-permute-done | bytes 2359328 | tf_op jit(solution)/shard_map/ppermute | solution.py:674
  465.4 0.5 collective-permute-start.11
  465.9 0.5 collective-permute-start.9
  466.4 0.4 copy-done.3
  466.8 3.1 collective-permute-done.15.rest_2_
  469.9 1.4 copy-done.8
  471.4 13.0 %shard_map.152.rest_2_ = bf16[16,256,2304]{2,1,0:T(8,128)(2,1)} custom-call(s32[80]{0:T(128)} %get-tuple-element.90.tab_ref, f32[256,2304]{1,0:T(8,128)} %copy-done.5, f32[256,2304]{1,0:T(8,128)} %copy-done.3, f32[256,2304]{1,0:T(8,128)} %copy-done.8, f32[256,2304]{1,0:T(8,128)} %copy-done.4, ...), custom_call_target="tpu_custom_call", output_to_operand_aliasing={{}: (11, {})} | custom-call | flops 10000000 | bytes 34504704 | tf_op jit(solution)/shard_map/pallas_call | solution.py:652
  484.3 3.1 shard_map.153.rest_1_
  487.4 2.9 shard_map.154.rest_1_
  490.3 2.5 shard_map.155.rest_1_
  492.9 2.5 shard_map.156
  (46 shorter events, 0.5 us)
Async XLA Ops:
  0.6 18.7 %copy-start.9 = (s32[16]{0:T(128)S(1)}, s32[16]{0:T(128)}, u32[]{:S(2)}) copy-start(s32[16]{0:T(128)} %sc_ref) | copy-start | bytes 196
  8.9 21.7 %collective-permute-start.2 = (f32[512,2048]{1,0:T(8,128)}, f32[512,2048]{1,0:T(8,128)}, u32[]{:S(2)}, u32[]{:S(2)}) collective-permute-start(f32[512,2048]{1,0:T(8,128)} %get-tuple-element.68), channel_id=1, source_target_pairs={{0,1},{1,0},{4,5},{5,4}} | collective-permute-start | bytes 12582920 | tf_op jit(solution)/shard_map/ppermute | solution.py:674
  10.9 16.7 %collective-permute-start.3 = (f32[160,2048]{1,0:T(8,128)}, f32[160,2048]{1,0:T(8,128)}, u32[]{:S(2)}, u32[]{:S(2)}) collective-permute-start(f32[160,2048]{1,0:T(8,128)} %get-tuple-element.71), channel_id=1, source_target_pairs={{0,3},{4,7}} | collective-permute-start | bytes 3932168 | tf_op jit(solution)/shard_map/ppermute | solution.py:674
  13.2 138.5 %collective-permute-start.5 = (f32[256,2048]{1,0:T(8,128)}, f32[256,2048]{1,0:T(8,128)}, u32[]{:S(2)}, u32[]{:S(2)}) collective-permute-start(f32[256,2048]{1,0:T(8,128)} %get-tuple-element.81), channel_id=1, source_target_pairs={{0,3},{4,7}} | collective-permute-start | bytes 6291464 | tf_op jit(solution)/shard_map/ppermute | solution.py:674
  15.8 82.0 %collective-permute-start.4 = (f32[384,2048]{1,0:T(8,128)}, f32[384,2048]{1,0:T(8,128)}, u32[]{:S(2)}, u32[]{:S(2)}) collective-permute-start(f32[384,2048]{1,0:T(8,128)} %get-tuple-element.77), channel_id=1, source_target_pairs={{0,2},{4,6}} | collective-permute-start | bytes 9437192 | tf_op jit(solution)/shard_map/ppermute | solution.py:674
  27.6 124.1 %collective-permute-start.6 = (f32[80,2048]{1,0:T(8,128)}, f32[80,2048]{1,0:T(8,128)}, u32[]{:S(2)}, u32[]{:S(2)}) collective-permute-start(f32[80,2048]{1,0:T(8,128)} %get-tuple-element.82), channel_id=1, source_target_pairs={{1,2},{5,6}} | collective-permute-start | bytes 1966088 | tf_op jit(solution)/shard_map/ppermute | solution.py:674
  29.1 122.6 %collective-permute-start.7 = (f32[80,2048]{1,0:T(8,128)}, f32[80,2048]{1,0:T(8,128)}, u32[]{:S(2)}, u32[]{:S(2)}) collective-permute-start(f32[80,2048]{1,0:T(8,128)} %get-tuple-element.83), channel_id=1, source_target_pairs={{1,3},{5,7}} | collective-permute-start | bytes 1966088 | tf_op jit(solution)/shard_map/ppermute | solution.py:674
  205.5 56.1 %copy-start.10 = (s32[16]{0:T(128)S(1)}, s32[16]{0:T(128)}, u32[]{:S(2)}) copy-start(s32[16]{0:T(128)} %sc_ref) | copy-start | bytes 196
  259.3 56.7 %collective-permute-start.22 = (f32[192,2304]{1,0:T(8,128)}, f32[192,2304]{1,0:T(8,128)}, u32[]{:S(2)}, u32[]{:S(2)}) collective-permute-start(f32[192,2304]{1,0:T(8,128)} %get-tuple-element.95), channel_id=1, source_target_pairs={{0,1},{1,0},{2,3},{3,2},{4,5},{5,4},{6,7},{7,6}} | collective-permute-start | bytes 5308424 | tf_op jit(solution)/shard_map/ppermute | solution.py:674
  259.4 56.7 %collective-permute-start.10 = (f32[192,2304]{1,0:T(8,128)}, f32[192,2304]{1,0:T(8,128)}, u32[]{:S(2)}, u32[]{:S(2)}) collective-permute-start(f32[192,2304]{1,0:T(8,128)} %get-tuple-element.95), channel_id=1, source_target_pairs={{0,2},{1,3},{2,0},{3,1},{4,6},{5,7},{6,4},{7,5}} | collective-permute-start | bytes 5308424 | tf_op jit(solution)/shard_map/ppermute | solution.py:674
  291.1 22.9 %collective-permute-start.8 = (f32[64,2304]{1,0:T(8,128)}, f32[64,2304]{1,0:T(8,128)}, u32[]{:S(2)}, u32[]{:S(2)}) collective-permute-start(f32[64,2304]{1,0:T(8,128)} %get-tuple-element.94), channel_id=1, source_target_pairs={{0,2},{1,3},{2,0},{3,1},{4,6},{5,7},{6,4},{7,5}} | collective-permute-start | bytes 1769480 | tf_op jit(solution)/shard_map/ppermute | solution.py:674
  291.2 73.3 %collective-permute-start.20 = (f32[256,2304]{1,0:T(8,128)}, f32[256,2304]{1,0:T(8,128)S(1)}, u32[]{:S(2)}, u32[]{:S(2)}) collective-permute-start(f32[256,2304]{1,0:T(8,128)} %get-tuple-element.98), channel_id=1, source_target_pairs={{0,2},{1,3},{2,0},{3,1},{4,6},{5,7},{6,4},{7,5}} | collective-permute-start | bytes 7077896 | tf_op jit(solution)/shard_map/ppermute | solution.py:674
  293.2 71.3 %collective-permute-start.19 = (f32[256,2304]{1,0:T(8,128)}, f32[256,2304]{1,0:T(8,128)S(1)}, u32[]{:S(2)}, u32[]{:S(2)}) collective-permute-start(f32[256,2304]{1,0:T(8,128)} %get-tuple-element.98), channel_id=1, source_target_pairs={{0,1},{1,0},{2,3},{3,2},{4,5},{5,4},{6,7},{7,6}} | collective-permute-start | bytes 7077896 | tf_op jit(solution)/shard_map/ppermute | solution.py:674
  314.0 101.0 %collective-permute-start.17 = (f32[256,2304]{1,0:T(8,128)}, f32[256,2304]{1,0:T(8,128)S(1)}, u32[]{:S(2)}, u32[]{:S(2)}) collective-permute-start(f32[256,2304]{1,0:T(8,128)} %get-tuple-element.97), channel_id=1, source_target_pairs={{0,2},{1,3},{2,0},{3,1},{4,6},{5,7},{6,4},{7,5}} | collective-permute-start | bytes 7077896 | tf_op jit(solution)/shard_map/ppermute | solution.py:674
  316.0 149.3 %collective-permute-start.14 = (f32[256,2304]{1,0:T(8,128)}, f32[256,2304]{1,0:T(8,128)S(1)}, u32[]{:S(2)}, u32[]{:S(2)}) collective-permute-start(f32[256,2304]{1,0:T(8,128)} %get-tuple-element.96), channel_id=1, source_target_pairs={{0,2},{1,3},{2,0},{3,1},{4,6},{5,7},{6,4},{7,5}} | collective-permute-start | bytes 7077896 | tf_op jit(solution)/shard_map/ppermute | solution.py:674
  316.1 149.3 %collective-permute-start.16 = (f32[256,2304]{1,0:T(8,128)}, f32[256,2304]{1,0:T(8,128)S(1)}, u32[]{:S(2)}, u32[]{:S(2)}) collective-permute-start(f32[256,2304]{1,0:T(8,128)} %get-tuple-element.97), channel_id=1, source_target_pairs={{0,1},{1,0},{2,3},{3,2},{4,5},{5,4},{6,7},{7,6}} | collective-permute-start | bytes 7077896 | tf_op jit(solution)/shard_map/ppermute | solution.py:674
  364.5 1.4 copy-start
  364.5 101.4 %collective-permute-start.13 = (f32[256,2304]{1,0:T(8,128)}, f32[256,2304]{1,0:T(8,128)S(1)}, u32[]{:S(2)}, u32[]{:S(2)}) collective-permute-start(f32[256,2304]{1,0:T(8,128)} %get-tuple-element.96), channel_id=1, source_target_pairs={{0,1},{1,0},{2,3},{3,2},{4,5},{5,4},{6,7},{7,6}} | collective-permute-start | bytes 7077896 | tf_op jit(solution)/shard_map/ppermute | solution.py:674
  365.9 100.1 %copy-start.1 = (f32[256,2304]{1,0:T(8,128)}, f32[256,2304]{1,0:T(8,128)S(1)}, u32[]{:S(2)}) copy-start(f32[256,2304]{1,0:T(8,128)S(1)} %collective-permute-done.19.rest_6_) | copy-start | bytes 7077892
  365.9 100.1 %collective-permute-start.21 = (f32[256,2304]{1,0:T(8,128)S(1)}, f32[256,2304]{1,0:T(8,128)S(1)}, u32[]{:S(2)}, u32[]{:S(2)}) collective-permute-start(f32[256,2304]{1,0:T(8,128)S(1)} %collective-permute-done.20.rest_7_), channel_id=1, source_target_pairs={{0,1},{1,0},{2,3},{3,2},{4,5},{5,4},{6,7},{7,6}} | collective-permute-start | bytes 7077896 | tf_op jit(solution)/shard_map/ppermute | solution.py:674
  415.0 51.4 %copy-start.2 = (f32[256,2304]{1,0:T(8,128)}, f32[256,2304]{1,0:T(8,128)S(1)}, u32[]{:S(2)}) copy-start(f32[256,2304]{1,0:T(8,128)S(1)} %collective-permute-done.17.rest_4_) | copy-start | bytes 7077892
  415.0 51.4 %collective-permute-start.18 = (f32[256,2304]{1,0:T(8,128)S(1)}, f32[256,2304]{1,0:T(8,128)S(1)}, u32[]{:S(2)}, u32[]{:S(2)}) collective-permute-start(f32[256,2304]{1,0:T(8,128)S(1)} %collective-permute-done.17.rest_4_), channel_id=1, source_target_pairs={{0,1},{1,0},{2,3},{3,2},{4,5},{5,4},{6,7},{7,6}} | collective-permute-start | bytes 7077896 | tf_op jit(solution)/shard_map/ppermute | solution.py:674
  465.4 1.4 copy-start.3
  465.4 4.5 collective-permute-start.15
  465.4 4.5 copy-start.4
  465.4 22.0 %collective-permute-start.11 = (f32[192,2304]{1,0:T(8,128)}, f32[192,2304]{1,0:T(8,128)}, u32[]{:S(2)}, u32[]{:S(2)}) collective-permute-start(f32[192,2304]{1,0:T(8,128)} %collective-permute-done.10.rest_0_), channel_id=1, source_target_pairs={{0,1},{1,0},{2,3},{3,2},{4,5},{5,4},{6,7},{7,6}} | collective-permute-start | bytes 5308424 | tf_op jit(solution)/shard_map/ppermute | solution.py:674
  465.9 4.0 copy-start.5
  465.9 18.4 %collective-permute-start.12 = (f32[64,2304]{1,0:T(8,128)}, f32[64,2304]{1,0:T(8,128)}, u32[]{:S(2)}, u32[]{:S(2)}) collective-permute-start(f32[64,2304]{1,0:T(8,128)} %get-tuple-element.94), channel_id=1, source_target_pairs={{0,1},{1,0},{2,3},{3,2},{4,5},{5,4},{6,7},{7,6}} | collective-permute-start | bytes 1769480 | tf_op jit(solution)/shard_map/ppermute | solution.py:674
  465.9 4.0 copy-start.6
  465.9 26.9 %collective-permute-start.9 = (f32[64,2304]{1,0:T(8,128)}, f32[64,2304]{1,0:T(8,128)}, u32[]{:S(2)}, u32[]{:S(2)}) collective-permute-start(f32[64,2304]{1,0:T(8,128)} %collective-permute-done.8.rest_0_), channel_id=1, source_target_pairs={{0,1},{1,0},{2,3},{3,2},{4,5},{5,4},{6,7},{7,6}} | collective-permute-start | bytes 1769480 | tf_op jit(solution)/shard_map/ppermute | solution.py:674
  466.8 3.1 copy-start.7
  469.9 1.4 copy-start.8

commit v5 on v4

--- a/solution.py
+++ b/solution.py
@@ -28,7 +28,7 @@
 OUT_BLK = 512
 STEP_ROWS = 64
 BLK = 768
-VMEM_BESIDE = 48_100_000
+VMEM_BESIDE = 47_500_000
 VMEM_ALL = 66_900_000
 DEPTH = 2
 DEPTH_B = 3
@@ -104,17 +104,15 @@
                 for half in range(2):
                     table[ROW * t + 8 + half] = pos[half * 8 + place]
                     table[ROW * t + 10 + half] = jnp.clip((length[rank] - HALF * half + UNIT - 1) // UNIT, 0, PER_HALF)
-    table[64] = over
-    return x_pos, core, over
-
-
-def pack_kernel(start_ref, ck_ref, cv_ref, ga_ref, gm_ref, table, over_ref, cos_ref, sin_ref, ga_out, gm_out, *rest):
-    outs = rest[:6]
-    order, length, pos, cnt, raw, wide, in_sem, out_sem = rest[6:]
-    x_pos, core, over = make_plan(start_ref, table, order, length, pos, cnt)
-    over_ref[0] = over
-    first = dict(A=0, B=A_ROWS, D=A_ROWS + B_ROWS, E=0, O=C_ROWS, S=A_ROWS + B_ROWS + D_ROWS)
-    size = dict(A=A_ROWS, B=B_ROWS, D=D_ROWS, E=C_ROWS, O=C_ROWS, S=S_ROWS)
+    return over
+
+
+PIECE_ROWS = dict(A=A_ROWS, B=B_ROWS, D=D_ROWS, E=C_ROWS, O=C_ROWS, S=S_ROWS)
+
+
+def pack_kernel(by_core, first, ck_ref, cv_ref, table, order, pos, cnt, outs, raw, wide, in_sem, out_sem):
+    me = lax.axis_index('cp')
+    x_pos, core = me // 2, me % 2
 
     def copies(seq, row, to, rows, sem):
         return [pltpu.make_async_copy(src.at[seq, pl.ds(row, rows), :], raw.at[pl.ds(to, rows), pl.ds(side * WIDE, WIDE)],
@@ -132,91 +130,76 @@
                     act(copy)
 
     def reads(name, act):
-        if name == "A":
-            for j in (1, 2):
-                units(0, j, first["A"], 0, act)
-        elif name == "E":
-            for j in (4, 7):
-                units(1, j, first["E"], 0, act)
-        elif name == "O":
-            for j in (5, 6):
-                units(1, j, first["O"], C_UNITS, act)
-        elif name == "S":
-            for t in range(4):
-                seq = order[8 + 2 * t + (1 - core + t) % 2]
-                for copy in copies(seq, 0, first["S"] + t * HALF, HALF, A_UNITS + t):
-                    act(copy)
+        if name in "AEO":
+            half, places, sem = dict(A=(0, (1, 2), 0), E=(1, (4, 7), 0), O=(1, (5, 6), C_UNITS))[name]
+            for j in places:
+                units(half, j, first[name], sem, act)
+            return
+        if name == "S":
+            seqs, sem = [table[ROW * t + 1] for t in range(4)], 0
+        elif name == "D":
+            seqs, sem = [table[ROW * t + 3] for t in (2, 3)], 4
         else:
-            places, sem = (WHOLE_B, A_UNITS + 4) if name == "B" else (WHOLE_D, A_UNITS + 4 + len(WHOLE_B))
-            for k, j in enumerate(places):
-                for copy in copies(order[j], 0, first[name] + k * HALF, HALF, sem + k):
-                    act(copy)
-
-    def out_copy(k, name):
-        return pltpu.make_async_copy(wide.at[pl.ds(first[name], size[name]), :], outs[k], out_sem.at[k])
-
-    def widen(k, name):
+            seqs, sem = [order[j] for j in WHOLE_B], A_UNITS
+        for k, seq in enumerate(seqs):
+            for copy in copies(seq, 0, first[name] + k * HALF, HALF, sem + k):
+                act(copy)
+
+    def out_copy(name):
+        k = list(outs).index(name)
+        return pltpu.make_async_copy(wide.at[pl.ds(first[name], PIECE_ROWS[name]), :], outs[name], out_sem.at[k])
+
+    def widen(name):
         reads(name, lambda copy: copy.wait())
 
-        @pl.loop(0, size[name] // UNIT)
+        @pl.loop(0, PIECE_ROWS[name] // UNIT)
         def _(u):
             rows = pl.ds(pl.multiple_of(first[name] + u * UNIT, UNIT), UNIT)
             wide[rows, :] = raw[rows, :].astype(F32)
 
-        out_copy(k, name).start()
-
-    for who, names in enumerate(("ASBD", "SEO")):
+        out_copy(name).start()
+
+    for who, names in enumerate(by_core):
         @pl.when((x_pos == 0) & (core == who))
         def _(names=names):
             for name in names:
                 reads(name, lambda copy: copy.start())
-
-    ga_out[...] = ga_ref[...].astype(F32).reshape(ga_out.shape)
-    gm_out[...] = gm_ref[...].astype(F32).reshape(gm_out.shape)
-    half = cos_ref.shape[1]
-    freq = lax.broadcasted_iota(jnp.int32, (1, half), 1).astype(F32)
-    inv_freq = jnp.exp(freq * (-2.0 / (2 * half) * math.log(ROPE_BASE)))
-    big = (16 * lax.broadcasted_iota(jnp.int32, (32, half), 0)).astype(F32) * inv_freq
-    small = lax.broadcasted_iota(jnp.int32, (16, half), 0).astype(F32) * inv_freq
-    cos_a, sin_a, cos_b, sin_b = jnp.cos(big), jnp.sin(big), jnp.cos(small), jnp.sin(small)
-    for r in range(32):
-        rows = slice(16 * r, 16 * r + 16)
-        ca, sa = cos_a[r:r + 1], sin_a[r:r + 1]
-        cos_ref[rows, :] = ca * cos_b - sa * sin_b
-        sin_ref[rows, :] = sa * cos_b + ca * sin_b
-
-    for who, names in enumerate(("ASBD", "SEO")):
-        @pl.when((x_pos == 0) & (core == who))
-        def _(names=names):
             for name in names:
-                widen("ABDEOS".index(name), name)
+                widen(name)
             for name in names:
-                out_copy("ABDEOS".index(name), name).wait()
-
-
-def plan_and_pack(start_pos, cache_k, cache_v, ga, gm):
+                out_copy(name).wait()
+
+
+def pack_first_kernel(start_ref, ck_ref, cv_ref, table, over_ref, a_out, b_out, e_out, o_out, order, length, pos, cnt, *work):
+    over_ref[0] = make_plan(start_ref, table, order, length, pos, cnt)
+    outs = dict(A=a_out, B=b_out, E=e_out, O=o_out)
+    pack_kernel(("AB", "EO"), dict(A=0, B=A_ROWS, E=0, O=C_ROWS), ck_ref, cv_ref, table, order, pos, cnt, outs, *work)
+
+
+def pack_second_kernel(table, ck_ref, cv_ref, s_out, d_out, *work):
+    outs = dict(S=s_out, D=d_out)
+    pack_kernel(("SD", "S"), dict(S=0, D=S_ROWS), ck_ref, cv_ref, table, table, None, None, outs, *work)
+
+
+def pack_call(kernel, n_scalar, names, rows, n_copy):
     any_spec = pl.BlockSpec(memory_space=pl.ANY)
     smem = pl.BlockSpec(memory_space=pltpu.SMEM)
-    vmem = pl.BlockSpec(memory_space=pltpu.VMEM)
-    total = A_ROWS + B_ROWS + D_ROWS + S_ROWS
-    n_copy = A_UNITS + 4 + len(WHOLE_B + WHOLE_D)
+    planned = n_scalar > 0
     return pl.pallas_call(
-        pack_kernel,
-        out_shape=[jax.ShapeDtypeStruct((80,), jnp.int32), jax.ShapeDtypeStruct((1,), jnp.int32)]
-        + [jax.ShapeDtypeStruct((2 * HEAD, HALF), F32)] * 2 + [jax.ShapeDtypeStruct((1, ga.shape[0]), F32)] * 2
-        + [pltpu.HBM((n, KV_WIDE), F32) for n in (A_ROWS, B_ROWS, D_ROWS, C_ROWS, C_ROWS, S_ROWS)],
-        in_specs=[smem, any_spec, any_spec, vmem, vmem],
-        out_specs=[smem, smem] + [vmem] * 4 + [any_spec] * 6,
-        scratch_shapes=[pltpu.SMEM((16,), jnp.int32)] * 4 + [
-            pltpu.VMEM((total, KV_WIDE), BF16),
-            pltpu.VMEM((total, KV_WIDE), F32),
+        kernel,
+        out_shape=([pltpu.SMEM((80,), jnp.int32), pltpu.SMEM((1,), jnp.int32)] if planned else [])
+        + [pltpu.HBM((PIECE_ROWS[n], KV_WIDE), F32) for n in names],
+        in_specs=[smem, any_spec, any_spec],
+        out_specs=([smem] * 2 if planned else []) + [any_spec] * len(names),
+        scratch_shapes=[pltpu.SMEM((16,), jnp.int32)] * n_scalar + [
+            pltpu.VMEM((rows, KV_WIDE), BF16),
+            pltpu.VMEM((rows, KV_WIDE), F32),
             pltpu.SemaphoreType.DMA((n_copy, 2)),
-            pltpu.SemaphoreType.DMA((6,)),
+            pltpu.SemaphoreType.DMA((len(names),)),
         ],
         compiler_params=pltpu.CompilerParams(vmem_limit_bytes=VMEM_ALL),
-        cost_estimate=pl.CostEstimate(flops=20_000_000, bytes_accessed=16_000_000, transcendentals=0),
-        name="pack",
-    )(start_pos, cache_k, cache_v, ga, gm)
+        cost_estimate=pl.CostEstimate(flops=10_000_000, bytes_accessed=8_000_000, transcendentals=0),
+    )
 
 
 def pack_full_kernel(order_ref, ck_ref, cv_ref, out_ref, raw, wide, sem):
@@ -272,7 +255,8 @@
 W_SLOTS = 3
 
 
-def heads_kernel(q_ref, k_ref, v_ref, out_ref, raw_q, raw_k, raw_v, sem):
+def heads_kernel(q_ref, k_ref, v_ref, ga_ref, gm_ref, out_ref, cos_ref, sin_ref, ga_out, gm_out, raw_q, raw_k, raw_v,
+                 gain_a, gain_m, sem, gain_sem):
     n_chunk = q_ref.shape[0] // W_CHUNK
 
     def copies(i, b):
@@ -289,6 +273,22 @@
     for i in range(W_SLOTS):
         for copy in copies(i, i):
             copy.start()
+    gains = [pltpu.make_async_copy(src, dst, gain_sem.at[k])
+             for k, (src, dst) in enumerate(((ga_ref, gain_a), (gm_ref, gain_m)))]
+    for copy in gains:
+        copy.start()
+    half = cos_ref.shape[1]
+    freq = lax.broadcasted_iota(jnp.int32, (1, half), 1).astype(F32)
+    inv_freq = jnp.exp(freq * (-2.0 / (2 * half) * math.log(ROPE_BASE)))
+    big = (16 * lax.broadcasted_iota(jnp.int32, (32, half), 0)).astype(F32) * inv_freq
+    small = lax.broadcasted_iota(jnp.int32, (16, half), 0).astype(F32) * inv_freq
+    cos_a, sin_a, cos_b, sin_b = jnp.cos(big), jnp.sin(big), jnp.cos(small), jnp.sin(small)
+    for r in range(32):
+        rows = slice(16 * r, 16 * r + 16)
+        ca, sa = cos_a[r:r + 1], sin_a[r:r + 1]
+        cos_ref[rows, :] = ca * cos_b - sa * sin_b
+        sin_ref[rows, :] = sa * cos_b + ca * sin_b
+
     sort8, sort4 = sorter(8), sorter(4)
 
     @pl.loop(0, n_chunk)
@@ -312,25 +312,33 @@
             for copy in copies(i + W_SLOTS, b):
                 copy.start()
 
-
-def split_heads(w_q, w_k, w_v):
+    for copy, src, dst in zip(gains, (gain_a, gain_m), (ga_out, gm_out)):
+        copy.wait()
+        dst[...] = src[...].astype(F32).reshape(dst.shape)
+
+
+def split_heads(w_q, w_k, w_v, ga, gm):
     d = w_q.shape[0]
+    vmem = pl.BlockSpec(memory_space=pltpu.VMEM)
     any_spec = pl.BlockSpec(memory_space=pl.ANY)
     return pl.pallas_call(
         heads_kernel,
-        out_shape=pltpu.VMEM((4, d, WIDE), BF16),
-        in_specs=[any_spec] * 3,
-        out_specs=pl.BlockSpec(memory_space=pltpu.VMEM),
+        out_shape=[pltpu.VMEM((4, d, WIDE), BF16)] + [pltpu.VMEM((2 * HEAD, HALF), F32)] * 2 + [pltpu.VMEM((1, d), F32)] * 2,
+        in_specs=[any_spec] * 5,
+        out_specs=[vmem] * 5,
         scratch_shapes=[
             pltpu.VMEM((W_SLOTS, W_CHUNK, 8, HEAD), BF16),
             pltpu.VMEM((W_SLOTS, W_CHUNK, 4, HEAD), BF16),
             pltpu.VMEM((W_SLOTS, W_CHUNK, 4, HEAD), BF16),
+            pltpu.VMEM((d,), BF16),
+            pltpu.VMEM((d,), BF16),
             pltpu.SemaphoreType.DMA((W_SLOTS, 3)),
+            pltpu.SemaphoreType.DMA((2,)),
         ],
         compiler_params=pltpu.CompilerParams(vmem_limit_bytes=VMEM_BESIDE),
         cost_estimate=pl.CostEstimate(flops=5_000_000_000, bytes_accessed=20_000_000, transcendentals=0),
         name="heads",
-    )(w_q, w_k, w_v)
+    )(w_q, w_k, w_v, ga, gm)
 
 
 def layer_kernel(n_att, n_ff, sizes, slot, tab_ref, over_ref, ga_ref, gm_ref, cos_ref, sin_ref, wh_ref, h_ref, wo_ref,
@@ -593,9 +601,9 @@
             grid=(n_seq // 2,),
             in_specs=[
                 pl.BlockSpec((2, HEAD, d), lambda i, sc: (i, 0, 0)),
-                pl.BlockSpec((1, d), lambda i, sc: (0, 0), pipeline_mode=one),
-                pl.BlockSpec((512, HALF), lambda i, sc: (0, 0), pipeline_mode=one),
-                pl.BlockSpec((512, HALF), lambda i, sc: (0, 0), pipeline_mode=one),
+                pl.BlockSpec(memory_space=pltpu.VMEM),
+                pl.BlockSpec(memory_space=pltpu.VMEM),
+                pl.BlockSpec(memory_space=pltpu.VMEM),
                 pl.BlockSpec(memory_space=pltpu.VMEM),
                 cache_spec,
                 cache_spec,
@@ -677,11 +685,14 @@
     def body(hidden, start_pos, cache_k, cache_v, w_q, w_k, w_v, w_o, w_gate, w_up, w_down, norm_attn, norm_mlp):
         n_seq, _, d = hidden.shape
         i32 = jnp.int32
-        table, over, cos, sin, ga, gm, *mine = plan_and_pack(start_pos, cache_k, cache_v, norm_attn, norm_mlp)
-        piece_a, piece_b, piece_d, piece_e, piece_o, piece_s = mine
+        table, over, piece_a, piece_b, piece_e, piece_o = pack_call(
+            pack_first_kernel, 4, "ABEO", A_ROWS + B_ROWS, A_UNITS + len(WHOLE_B))(start_pos, cache_k, cache_v)
+        in_smem = lambda x: pltpu.with_memory_space_constraint(x, pltpu.SMEM)
         got_a = send(piece_a, [(0, 3)])
+        got_b = send(piece_b, [(0, 2), (2, 0), (3, 1)])
+        piece_s, piece_d = pack_call(
+            pack_second_kernel, 0, "SD", S_ROWS + D_ROWS, 4 + len(WHOLE_D))(in_smem(table), cache_k, cache_v)
         sib = send(piece_s, [(0, 1), (1, 0)])
-        got_b = send(piece_b, [(0, 2)])
         got_d = send(piece_d, [(0, 3)])
         got_a, piece_e, piece_o = lax.optimization_barrier((got_a, piece_e, piece_o))
         got_e = send(piece_e, [(1, 2)])
@@ -699,7 +710,8 @@
         full, full_f = lax.cond(over[0] > 0, send_all, lambda _: tuple(blank(2)), 0)
 
         w_q, w_k, w_v, full, full_f = lax.optimization_barrier((w_q, w_k, w_v, full, full_f))
-        wh = pltpu.with_memory_space_constraint(split_heads(w_q, w_k, w_v), pltpu.VMEM)
+        kept = split_heads(w_q, w_k, w_v, norm_attn, norm_mlp)
+        wh, cos, sin, ga, gm = [pltpu.with_memory_space_constraint(x, pltpu.VMEM) for x in kept]
         wo = w_o.reshape(-1, d)
 
         out = None
@@ -707,7 +719,7 @@
         parts, where = [], []
         for t in range(4):
             pieces = (got_a, got_b if t > 0 else got_a) + ((got_d, got_e, got_o) if t > 1 else (got_a,) * 3)
-            *own, out = run_layer(t, tab, over, hidden, ga, gm, cos, sin, wh, wo, w_gate, w_up, w_down,
+            *own, out = run_layer(t, in_smem(tab), in_smem(over), hidden, ga, gm, cos, sin, wh, wo, w_gate, w_up, w_down,
                                   cache_k, cache_v, sib, full, full_f, pieces, out, (192, 64) if t == 3 else (HEAD,))
             tab, own = lax.optimization_barrier((tab, own))
             if t < 3:
@@ -724,11 +736,11 @@
         crs_rest, near_rest = send(rest, cross), send(rest, d2d)
         dia_most, dia_rest = send(crs_most, d2d), send(crs_rest, d2d)
         last = ROW * 3
-        out = place_rows(tab, parts + [near_most], where + [(last + 1, 0)], out, 64)
-        out = place_rows(tab, [crs_most, near_rest], [(last + 2, 0), (last + 1, 192)], out, 64)
-        out = place_rows(tab, [dia_most], [(last + 3, 0)], out, 64)
-        out = place_rows(tab, [crs_rest], [(last + 2, 192)], out, 16)
-        out = place_rows(tab, [dia_rest], [(last + 3, 192)], out, 16)
+        out = place_rows(in_smem(tab), parts + [near_most], where + [(last + 1, 0)], out, 64)
+        out = place_rows(in_smem(tab), [crs_most, near_rest], [(last + 2, 0), (last + 1, 192)], out, 64)
+        out = place_rows(in_smem(tab), [dia_most], [(last + 3, 0)], out, 64)
+        out = place_rows(in_smem(tab), [crs_rest], [(last + 2, 192)], out, 16)
+        out = place_rows(in_smem(tab), [dia_rest], [(last + 3, 192)], out, 16)
         return out, new_k, new_v
 
     group_spec = P('dp', None, None)

time: 497 us -> 478 us (0.962)
  waiting for transfers between devices: 185 us -> 174 us
  Pallas kernels: 285 us -> 278 us
    ppermute x21, waiting for transfers between devices: 185 us -> 174 us  [send(): x = lax.ppermute(x, axis, pairs)]
    pallas_call x4, Pallas kernels: 215 us -> 210 us  [run_layer(): pl.pallas_call(functools.partial(layer_kernel, 4, n_ff, sizes, slot), out...]
    pallas_call x2 -> x3, Pallas kernels: 16.2 us -> 17.7 us  [the longest x1 7.99 us: split_heads(): pl.pallas_call(heads_kernel, out_shape=[pltpu.VMEM((4, d, WIDE), BF16)] +...]
  transfers between devices with their start and end apart: 21 -> 21, of which waited for: 7 -> 6; matrix products, arithmetic and copies ran while one was open for 0% -> 0% of each run, Pallas kernels for 34% -> 34%
where the time goes in v5:
time: 478 us; the launch traced here: 477 us
  Pallas kernels  278 us (58%)
  waiting for transfers between devices  174 us (36%)
  starting transfers between devices  21.8 us (5%)
    pallas_call x4, Pallas kernels, run_layer(): pl.pallas_call(functools.partial(layer_kernel, 4, n_ff, sizes, slot), out...  210 us
    ppermute x21, waiting for transfers between devices, send(): x = lax.ppermute(x, axis, pairs)  174 us
    pallas_call x1, Pallas kernels, write_windows(): pl.pallas_call(window_kernel, out_shape=[jax.ShapeDtypeStruct(cache_k.sha...  29.7 us
    ppermute x21, starting transfers between devices, send(): x = lax.ppermute(x, axis, pairs)  21.8 us
    pallas_call x5, Pallas kernels, place_rows(): pl.pallas_call(functools.partial(place_kernel, where, blk), out_shape=jax...  20.6 us
  transfers between devices with their start and end apart: 21, of which 6 were waited for; matrix products, arithmetic and copies ran while one was open for 0% of the time, Pallas kernels for 34%

profile of v5, /device:TPU:0, one launch (start us, length us, event | category | flops | bytes accessed | tf_op | source)
XLA Modules:
  0.0 477.4 jit_solution(17382631826819216593)
XLA Ops:
  0.6 5.0 %shard_map.148 = (s32[80]{0:T(128)S(4)}, s32[1]{0:T(128)S(4)}, f32[160,2048]{1,0:T(8,128)}, f32[384,2048]{1,0:T(8,128)}, f32[80,2048]{1,0:T(8,128)}, /*index=5*/f32[80,2048]{1,0:T(8,128)}) custom-call(s32[16]{0:T(128)} %sc_ref, bf16[16,128,1024]{2,1,0:T(8,128)(2,1)} %ck_ref.13, bf16[16,128,1024]{2,1,0:T(8,128)(2,1)} %cv_ref.13), custom_call_target="tpu_custom_call" | custom-call | flops 10000000 | bytes 8000000 | tf_op jit(solution)/shard_map/pallas_call | solution.py:688
  5.6 4.7 shard_map.149
  10.4 1.9 collective-permute-start.2
  12.3 2.4 collective-permute-start.3
  14.7 1.9 collective-permute-start.4
  16.6 6.1 %collective-permute-start.5 = (f32[256,2048]{1,0:T(8,128)}, f32[256,2048]{1,0:T(8,128)}, u32[]{:S(2)}, u32[]{:S(2)}) collective-permute-start(f32[256,2048]{1,0:T(8,128)} %get-tuple-element.83), channel_id=1, source_target_pairs={{0,3},{4,7}} | collective-permute-start | bytes 6291464 | tf_op jit(solution)/shard_map/ppermute | solution.py:682
  22.6 8.0 %heads.1 = (bf16[4,2304,1024]{2,1,0:T(8,128)(2,1)S(1)}, f32[512,128]{1,0:T(8,128)S(1)}, f32[512,128]{1,0:T(8,128)S(1)}, f32[1,2304]{1,0:T(1,128)S(1)}, f32[1,2304]{1,0:T(1,128)S(1)}) custom-call(bf16[2304,8,256]{2,1,0:T(8,128)(2,1)} %q_ref, bf16[2304,4,256]{2,1,0:T(4,128)(2,1)} %k_ref, bf16[2304,4,256]{2,1,0:T(4,128)(2,1)} %v_ref, bf16[2304]{0:T(1024)(128)(2,1)} %ga_ref.1, ...), custom_call_target="tpu_custom_call" | custom-call | flops 5000000000 | bytes 20000000 | tf_op jit(solution)/shard_map/heads/pallas_call | solution.py:324
  30.6 1.5 collective-permute-start.6
  32.2 1.5 collective-permute-start.7
  33.7 52.4 %shard_map.150 = (f32[256,2304]{1,0:T(8,128)}, bf16[16,256,2304]{2,1,0:T(8,128)(2,1)}) custom-call(s32[80]{0:T(128)S(4)} %get-tuple-element.92.table.tab_ref, s32[1]{0:T(128)S(4)} %get-tuple-element.59.over_ref, f32[1,2304]{1,0:T(1,128)S(1)} %get-tuple-element.65.ga_ref, f32[1,2304]{1,0:T(1,128)S(1)} %get-tuple-element.66.gm_ref, ...), custom_call_target="tpu_custom_call" | custom-call | flops 40962666496 | bytes 160000000 | tf_op jit(solution)/shard_map/pallas_call | solution.py:540
  86.1 0.6 collective-permute-done.4.rest_1_
  86.7 52.4 %shard_map.151 = (f32[256,2304]{1,0:T(8,128)}, bf16[16,256,2304]{2,1,0:T(8,128)(2,1)}) custom-call(s32[80]{0:T(128)S(4)} %get-tuple-element.92.table.tab_ref, s32[1]{0:T(128)S(4)} %get-tuple-element.59.over_ref, f32[1,2304]{1,0:T(1,128)S(1)} %get-tuple-element.65.ga_ref, f32[1,2304]{1,0:T(1,128)S(1)} %get-tuple-element.66.gm_ref, ...), custom_call_target="tpu_custom_call", output_to_operand_aliasing={{1}: (22, {})} | custom-call | flops 40962666496 | bytes 160000000 | tf_op jit(solution)/shard_map/pallas_call | solution.py:540
  139.2 52.4 %shard_map.152 = (f32[256,2304]{1,0:T(8,128)}, bf16[16,256,2304]{2,1,0:T(8,128)(2,1)}) custom-call(s32[80]{0:T(128)S(4)} %get-tuple-element.92.table.tab_ref, s32[1]{0:T(128)S(4)} %get-tuple-element.59.over_ref, f32[1,2304]{1,0:T(1,128)S(1)} %get-tuple-element.65.ga_ref, f32[1,2304]{1,0:T(1,128)S(1)} %get-tuple-element.66.gm_ref, ...), custom_call_target="tpu_custom_call", output_to_operand_aliasing={{1}: (22, {})} | custom-call | flops 40962666496 | bytes 160000000 | tf_op jit(solution)/shard_map/pallas_call | solution.py:540
  191.6 52.4 %shard_map.153 = (f32[192,2304]{1,0:T(8,128)}, f32[64,2304]{1,0:T(8,128)}, bf16[16,256,2304]{2,1,0:T(8,128)(2,1)}) custom-call(s32[80]{0:T(128)S(4)} %get-tuple-element.92.table.tab_ref, s32[1]{0:T(128)S(4)} %get-tuple-element.59.over_ref, f32[1,2304]{1,0:T(1,128)S(1)} %get-tuple-element.65.ga_ref, ...), custom_call_target="tpu_custom_call", output_to_operand_aliasing={{2}: (22, {})} | custom-call | flops 40962666496 | bytes 160000000 | tf_op jit(solution)/shard_map/pallas_call | solution.py:540
  244.0 1.4 collective-permute-start.22
  245.4 29.7 %cache_window.1 = (bf16[16,128,1024]{2,1,0:T(8,128)(2,1)}, bf16[16,128,1024]{2,1,0:T(8,128)(2,1)}) custom-call(s32[16]{0:T(128)S(1)} %copy-done.10, bf16[16,256,2304]{2,1,0:T(8,128)(2,1)} %h_ref.9, f32[1,2304]{1,0:T(1,128)S(1)} %get-tuple-element.65.ga_ref, f32[512,128]{1,0:T(8,128)S(1)} %get-tuple-element.67.cos_ref, ...), custom_call_target="tpu_custom_call" | custom-call | flops 19327352832 | bytes 60000000 | tf_op jit(solution)/shard_map/cache_window/pallas_call | solution.py:596
  275.1 2.0 collective-permute-start.8
  277.2 22.7 %collective-permute-done.8.rest_0_ = f32[64,2304]{1,0:T(8,128)} collective-permute-done((f32[64,2304]{1,0:T(8,128)}, f32[64,2304]{1,0:T(8,128)}, u32[]{:S(2)}, u32[]{:S(2)}) %collective-permute-start.8) | collective-permute-done | bytes 589856 | tf_op jit(solution)/shard_map/ppermute | solution.py:682
  299.9 2.0 collective-permute-start.14
  301.9 48.4 %collective-permute-done.20.rest_7_ = f32[256,2304]{1,0:T(8,128)S(1)} collective-permute-done((f32[256,2304]{1,0:T(8,128)}, f32[256,2304]{1,0:T(8,128)S(1)}, u32[]{:S(2)}, u32[]{:S(2)}) %collective-permute-start.20) | collective-permute-done | bytes 2359328 | tf_op jit(solution)/shard_map/ppermute | solution.py:682
  350.3 1.4 copy-done
  351.7 49.1 %collective-permute-done.17.rest_4_ = f32[256,2304]{1,0:T(8,128)S(1)} collective-permute-done((f32[256,2304]{1,0:T(8,128)}, f32[256,2304]{1,0:T(8,128)S(1)}, u32[]{:S(2)}, u32[]{:S(2)}) %collective-permute-start.17) | collective-permute-done | bytes 2359328 | tf_op jit(solution)/shard_map/ppermute | solution.py:682
  400.9 49.6 %collective-permute-done.14.rest_1_ = f32[256,2304]{1,0:T(8,128)S(1)} collective-permute-done((f32[256,2304]{1,0:T(8,128)}, f32[256,2304]{1,0:T(8,128)S(1)}, u32[]{:S(2)}, u32[]{:S(2)}) %collective-permute-start.14) | collective-permute-done | bytes 2359328 | tf_op jit(solution)/shard_map/ppermute | solution.py:682
  450.5 0.5 collective-permute-start.11
  451.1 0.5 collective-permute-start.9
  451.9 3.1 collective-permute-done.15.rest_2_
  455.1 1.4 copy-done.8
  456.5 12.3 %shard_map.154.rest_2_ = bf16[16,256,2304]{2,1,0:T(8,128)(2,1)} custom-call(s32[80]{0:T(128)S(4)} %get-tuple-element.92.table.tab_ref, f32[256,2304]{1,0:T(8,128)} %copy-done.5, f32[256,2304]{1,0:T(8,128)} %copy-done.3, f32[256,2304]{1,0:T(8,128)} %copy-done.8, f32[256,2304]{1,0:T(8,128)} %copy-done.4, ...), custom_call_target="tpu_custom_call", output_to_operand_aliasing={{}: (11, {})} | custom-call | flops 10000000 | bytes 34504704 | tf_op jit(solution)/shard_map/pallas_call | solution.py:660
  468.8 2.4 shard_map.155.rest_1_
  471.3 2.2 shard_map.156.rest_1_
  473.5 1.8 shard_map.157.rest_1_
  475.4 1.8 shard_map.158
  (47 shorter events, 0.5 us)
Async XLA Ops:
  5.6 17.0 %copy-start.9 = (s32[16]{0:T(128)S(1)}, s32[16]{0:T(128)}, u32[]{:S(2)}) copy-start(s32[16]{0:T(128)} %sc_ref) | copy-start | bytes 196
  10.4 23.3 %collective-permute-start.2 = (f32[512,2048]{1,0:T(8,128)}, f32[512,2048]{1,0:T(8,128)}, u32[]{:S(2)}, u32[]{:S(2)}) collective-permute-start(f32[512,2048]{1,0:T(8,128)} %get-tuple-element.70), channel_id=1, source_target_pairs={{0,1},{1,0},{4,5},{5,4}} | collective-permute-start | bytes 12582920 | tf_op jit(solution)/shard_map/ppermute | solution.py:682
  12.3 18.3 %collective-permute-start.3 = (f32[160,2048]{1,0:T(8,128)}, f32[160,2048]{1,0:T(8,128)}, u32[]{:S(2)}, u32[]{:S(2)}) collective-permute-start(f32[160,2048]{1,0:T(8,128)} %get-tuple-element.73), channel_id=1, source_target_pairs={{0,3},{4,7}} | collective-permute-start | bytes 3932168 | tf_op jit(solution)/shard_map/ppermute | solution.py:682
  14.7 72.1 %collective-permute-start.4 = (f32[384,2048]{1,0:T(8,128)}, f32[384,2048]{1,0:T(8,128)}, u32[]{:S(2)}, u32[]{:S(2)}) collective-permute-start(f32[384,2048]{1,0:T(8,128)} %get-tuple-element.79), channel_id=1, source_target_pairs={{0,2},{2,0},{3,1},{4,6},{6,4},{7,5}} | collective-permute-start | bytes 9437192 | tf_op jit(solution)/shard_map/ppermute | solution.py:682
  16.6 122.6 %collective-permute-start.5 = (f32[256,2048]{1,0:T(8,128)}, f32[256,2048]{1,0:T(8,128)}, u32[]{:S(2)}, u32[]{:S(2)}) collective-permute-start(f32[256,2048]{1,0:T(8,128)} %get-tuple-element.83), channel_id=1, source_target_pairs={{0,3},{4,7}} | collective-permute-start | bytes 6291464 | tf_op jit(solution)/shard_map/ppermute | solution.py:682
  30.6 108.5 %collective-permute-start.6 = (f32[80,2048]{1,0:T(8,128)}, f32[80,2048]{1,0:T(8,128)}, u32[]{:S(2)}, u32[]{:S(2)}) collective-permute-start(f32[80,2048]{1,0:T(8,128)} %get-tuple-element.84), channel_id=1, source_target_pairs={{1,2},{5,6}} | collective-permute-start | bytes 1966088 | tf_op jit(solution)/shard_map/ppermute | solution.py:682
  32.2 107.0 %collective-permute-start.7 = (f32[80,2048]{1,0:T(8,128)}, f32[80,2048]{1,0:T(8,128)}, u32[]{:S(2)}, u32[]{:S(2)}) collective-permute-start(f32[80,2048]{1,0:T(8,128)} %get-tuple-element.85), channel_id=1, source_target_pairs={{1,3},{5,7}} | collective-permute-start | bytes 1966088 | tf_op jit(solution)/shard_map/ppermute | solution.py:682
  191.6 53.9 %copy-start.10 = (s32[16]{0:T(128)S(1)}, s32[16]{0:T(128)}, u32[]{:S(2)}) copy-start(s32[16]{0:T(128)} %sc_ref) | copy-start | bytes 196
  244.0 55.9 %collective-permute-start.22 = (f32[192,2304]{1,0:T(8,128)}, f32[192,2304]{1,0:T(8,128)}, u32[]{:S(2)}, u32[]{:S(2)}) collective-permute-start(f32[192,2304]{1,0:T(8,128)} %get-tuple-element.97), channel_id=1, source_target_pairs={{0,1},{1,0},{2,3},{3,2},{4,5},{5,4},{6,7},{7,6}} | collective-permute-start | bytes 5308424 | tf_op jit(solution)/shard_map/ppermute | solution.py:682
  245.4 56.5 %collective-permute-start.10 = (f32[192,2304]{1,0:T(8,128)}, f32[192,2304]{1,0:T(8,128)}, u32[]{:S(2)}, u32[]{:S(2)}) collective-permute-start(f32[192,2304]{1,0:T(8,128)} %get-tuple-element.97), channel_id=1, source_target_pairs={{0,2},{1,3},{2,0},{3,1},{4,6},{5,7},{6,4},{7,5}} | collective-permute-start | bytes 5308424 | tf_op jit(solution)/shard_map/ppermute | solution.py:682
  275.1 24.8 %collective-permute-start.8 = (f32[64,2304]{1,0:T(8,128)}, f32[64,2304]{1,0:T(8,128)}, u32[]{:S(2)}, u32[]{:S(2)}) collective-permute-start(f32[64,2304]{1,0:T(8,128)} %get-tuple-element.96), channel_id=1, source_target_pairs={{0,2},{1,3},{2,0},{3,1},{4,6},{5,7},{6,4},{7,5}} | collective-permute-start | bytes 1769480 | tf_op jit(solution)/shard_map/ppermute | solution.py:682
  277.1 73.2 %collective-permute-start.20 = (f32[256,2304]{1,0:T(8,128)}, f32[256,2304]{1,0:T(8,128)S(1)}, u32[]{:S(2)}, u32[]{:S(2)}) collective-permute-start(f32[256,2304]{1,0:T(8,128)} %get-tuple-element.100), channel_id=1, source_target_pairs={{0,2},{1,3},{2,0},{3,1},{4,6},{5,7},{6,4},{7,5}} | collective-permute-start | bytes 7077896 | tf_op jit(solution)/shard_map/ppermute | solution.py:682
  277.2 73.2 %collective-permute-start.19 = (f32[256,2304]{1,0:T(8,128)}, f32[256,2304]{1,0:T(8,128)S(1)}, u32[]{:S(2)}, u32[]{:S(2)}) collective-permute-start(f32[256,2304]{1,0:T(8,128)} %get-tuple-element.100), channel_id=1, source_target_pairs={{0,1},{1,0},{2,3},{3,2},{4,5},{5,4},{6,7},{7,6}} | collective-permute-start | bytes 7077896 | tf_op jit(solution)/shard_map/ppermute | solution.py:682
  299.9 101.0 %collective-permute-start.17 = (f32[256,2304]{1,0:T(8,128)}, f32[256,2304]{1,0:T(8,128)S(1)}, u32[]{:S(2)}, u32[]{:S(2)}) collective-permute-start(f32[256,2304]{1,0:T(8,128)} %get-tuple-element.99), channel_id=1, source_target_pairs={{0,2},{1,3},{2,0},{3,1},{4,6},{5,7},{6,4},{7,5}} | collective-permute-start | bytes 7077896 | tf_op jit(solution)/shard_map/ppermute | solution.py:682
  299.9 150.6 %collective-permute-start.14 = (f32[256,2304]{1,0:T(8,128)}, f32[256,2304]{1,0:T(8,128)S(1)}, u32[]{:S(2)}, u32[]{:S(2)}) collective-permute-start(f32[256,2304]{1,0:T(8,128)} %get-tuple-element.98), channel_id=1, source_target_pairs={{0,2},{1,3},{2,0},{3,1},{4,6},{5,7},{6,4},{7,5}} | collective-permute-start | bytes 7077896 | tf_op jit(solution)/shard_map/ppermute | solution.py:682
  301.9 148.6 %collective-permute-start.16 = (f32[256,2304]{1,0:T(8,128)}, f32[256,2304]{1,0:T(8,128)S(1)}, u32[]{:S(2)}, u32[]{:S(2)}) collective-permute-start(f32[256,2304]{1,0:T(8,128)} %get-tuple-element.99), channel_id=1, source_target_pairs={{0,1},{1,0},{2,3},{3,2},{4,5},{5,4},{6,7},{7,6}} | collective-permute-start | bytes 7077896 | tf_op jit(solution)/shard_map/ppermute | solution.py:682
  350.3 1.4 copy-start
  350.3 100.7 %collective-permute-start.13 = (f32[256,2304]{1,0:T(8,128)}, f32[256,2304]{1,0:T(8,128)S(1)}, u32[]{:S(2)}, u32[]{:S(2)}) collective-permute-start(f32[256,2304]{1,0:T(8,128)} %get-tuple-element.98), channel_id=1, source_target_pairs={{0,1},{1,0},{2,3},{3,2},{4,5},{5,4},{6,7},{7,6}} | collective-permute-start | bytes 7077896 | tf_op jit(solution)/shard_map/ppermute | solution.py:682
  351.7 99.3 %copy-start.1 = (f32[256,2304]{1,0:T(8,128)}, f32[256,2304]{1,0:T(8,128)S(1)}, u32[]{:S(2)}) copy-start(f32[256,2304]{1,0:T(8,128)S(1)} %collective-permute-done.19.rest_6_) | copy-start | bytes 7077892
  351.7 99.3 %collective-permute-start.21 = (f32[256,2304]{1,0:T(8,128)S(1)}, f32[256,2304]{1,0:T(8,128)S(1)}, u32[]{:S(2)}, u32[]{:S(2)}) collective-permute-start(f32[256,2304]{1,0:T(8,128)S(1)} %collective-permute-done.20.rest_7_), channel_id=1, source_target_pairs={{0,1},{1,0},{2,3},{3,2},{4,5},{5,4},{6,7},{7,6}} | collective-permute-start | bytes 7077896 | tf_op jit(solution)/shard_map/ppermute | solution.py:682
  400.9 50.7 %copy-start.2 = (f32[256,2304]{1,0:T(8,128)}, f32[256,2304]{1,0:T(8,128)S(1)}, u32[]{:S(2)}) copy-start(f32[256,2304]{1,0:T(8,128)S(1)} %collective-permute-done.17.rest_4_) | copy-start | bytes 7077892
  400.9 50.7 %collective-permute-start.18 = (f32[256,2304]{1,0:T(8,128)S(1)}, f32[256,2304]{1,0:T(8,128)S(1)}, u32[]{:S(2)}, u32[]{:S(2)}) collective-permute-start(f32[256,2304]{1,0:T(8,128)S(1)} %collective-permute-done.17.rest_4_), channel_id=1, source_target_pairs={{0,1},{1,0},{2,3},{3,2},{4,5},{5,4},{6,7},{7,6}} | collective-permute-start | bytes 7077896 | tf_op jit(solution)/shard_map/ppermute | solution.py:682
  450.5 1.4 copy-start.3
  450.5 4.5 collective-permute-start.15
  450.5 4.5 copy-start.4
  450.5 20.7 %collective-permute-start.11 = (f32[192,2304]{1,0:T(8,128)}, f32[192,2304]{1,0:T(8,128)}, u32[]{:S(2)}, u32[]{:S(2)}) collective-permute-start(f32[192,2304]{1,0:T(8,128)} %collective-permute-done.10.rest_0_), channel_id=1, source_target_pairs={{0,1},{1,0},{2,3},{3,2},{4,5},{5,4},{6,7},{7,6}} | collective-permute-start | bytes 5308424 | tf_op jit(solution)/shard_map/ppermute | solution.py:682
  451.0 4.0 copy-start.5
  451.0 17.8 %collective-permute-start.12 = (f32[64,2304]{1,0:T(8,128)}, f32[64,2304]{1,0:T(8,128)}, u32[]{:S(2)}, u32[]{:S(2)}) collective-permute-start(f32[64,2304]{1,0:T(8,128)} %get-tuple-element.96), channel_id=1, source_target_pairs={{0,1},{1,0},{2,3},{3,2},{4,5},{5,4},{6,7},{7,6}} | collective-permute-start | bytes 1769480 | tf_op jit(solution)/shard_map/ppermute | solution.py:682
  451.1 4.0 copy-start.6
  451.1 24.3 %collective-permute-start.9 = (f32[64,2304]{1,0:T(8,128)}, f32[64,2304]{1,0:T(8,128)}, u32[]{:S(2)}, u32[]{:S(2)}) collective-permute-start(f32[64,2304]{1,0:T(8,128)} %collective-permute-done.8.rest_0_), channel_id=1, source_target_pairs={{0,1},{1,0},{2,3},{3,2},{4,5},{5,4},{6,7},{7,6}} | collective-permute-start | bytes 1769480 | tf_op jit(solution)/shard_map/ppermute | solution.py:682
  451.9 3.1 copy-start.7
  455.1 1.4 copy-start.8

commit v6 on v5

--- a/solution.py
+++ b/solution.py
@@ -159,47 +159,52 @@
 
         out_copy(name).start()
 
-    for who, names in enumerate(by_core):
-        @pl.when((x_pos == 0) & (core == who))
-        def _(names=names):
-            for name in names:
-                reads(name, lambda copy: copy.start())
-            for name in names:
-                widen(name)
-            for name in names:
-                out_copy(name).wait()
+    def begin(name):
+        reads(name, lambda copy: copy.start())
+
+    def end(name):
+        out_copy(name).wait()
+
+    def phase(do):
+        for who, names in enumerate(by_core):
+            @pl.when((x_pos == 0) & (core == who))
+            def _(names=names):
+                for name in names:
+                    do(name)
+
+    return [functools.partial(phase, do) for do in (begin, widen, end)]
 
 
 def pack_first_kernel(start_ref, ck_ref, cv_ref, table, over_ref, a_out, b_out, e_out, o_out, order, length, pos, cnt, *work):
     over_ref[0] = make_plan(start_ref, table, order, length, pos, cnt)
     outs = dict(A=a_out, B=b_out, E=e_out, O=o_out)
-    pack_kernel(("AB", "EO"), dict(A=0, B=A_ROWS, E=0, O=C_ROWS), ck_ref, cv_ref, table, order, pos, cnt, outs, *work)
-
-
-def pack_second_kernel(table, ck_ref, cv_ref, s_out, d_out, *work):
-    outs = dict(S=s_out, D=d_out)
-    pack_kernel(("SD", "S"), dict(S=0, D=S_ROWS), ck_ref, cv_ref, table, table, None, None, outs, *work)
-
-
-def pack_call(kernel, n_scalar, names, rows, n_copy):
+    for phase in pack_kernel(("AB", "EO"), dict(A=0, B=A_ROWS, E=0, O=C_ROWS), ck_ref, cv_ref, table, order, pos, cnt, outs, *work):
+        phase()
+
+
+def pack_work(rows, n_copy, n_out):
+    return [
+        pltpu.VMEM((rows, KV_WIDE), BF16),
+        pltpu.VMEM((rows, KV_WIDE), F32),
+        pltpu.SemaphoreType.DMA((n_copy, 2)),
+        pltpu.SemaphoreType.DMA((n_out,)),
+    ]
+
+
+def plan_and_pack(start_pos, cache_k, cache_v):
     any_spec = pl.BlockSpec(memory_space=pl.ANY)
     smem = pl.BlockSpec(memory_space=pltpu.SMEM)
-    planned = n_scalar > 0
     return pl.pallas_call(
-        kernel,
-        out_shape=([pltpu.SMEM((80,), jnp.int32), pltpu.SMEM((1,), jnp.int32)] if planned else [])
-        + [pltpu.HBM((PIECE_ROWS[n], KV_WIDE), F32) for n in names],
+        pack_first_kernel,
+        out_shape=[pltpu.SMEM((80,), jnp.int32), pltpu.SMEM((1,), jnp.int32)]
+        + [pltpu.HBM((PIECE_ROWS[n], KV_WIDE), F32) for n in "ABEO"],
         in_specs=[smem, any_spec, any_spec],
-        out_specs=([smem] * 2 if planned else []) + [any_spec] * len(names),
-        scratch_shapes=[pltpu.SMEM((16,), jnp.int32)] * n_scalar + [
-            pltpu.VMEM((rows, KV_WIDE), BF16),
-            pltpu.VMEM((rows, KV_WIDE), F32),
-            pltpu.SemaphoreType.DMA((n_copy, 2)),
-            pltpu.SemaphoreType.DMA((len(names),)),
-        ],
+        out_specs=[smem] * 2 + [any_spec] * 4,
+        scratch_shapes=[pltpu.SMEM((16,), jnp.int32)] * 4 + pack_work(A_ROWS + B_ROWS, A_UNITS + len(WHOLE_B), 4),
         compiler_params=pltpu.CompilerParams(vmem_limit_bytes=VMEM_ALL),
         cost_estimate=pl.CostEstimate(flops=10_000_000, bytes_accessed=8_000_000, transcendentals=0),
-    )
+        name="pack",
+    )(start_pos, cache_k, cache_v)
 
 
 def pack_full_kernel(order_ref, ck_ref, cv_ref, out_ref, raw, wide, sem):
@@ -255,8 +260,11 @@
 W_SLOTS = 3
 
 
-def heads_kernel(q_ref, k_ref, v_ref, ga_ref, gm_ref, out_ref, cos_ref, sin_ref, ga_out, gm_out, raw_q, raw_k, raw_v,
-                 gain_a, gain_m, sem, gain_sem):
+def heads_kernel(table, ck_ref, cv_ref, q_ref, k_ref, v_ref, ga_ref, gm_ref, out_ref, cos_ref, sin_ref, ga_out, gm_out,
+                 s_out, d_out, raw_q, raw_k, raw_v, gain_a, gain_m, sem, gain_sem, *work):
+    begin, widen, end = pack_kernel(("SD", "S"), dict(S=0, D=S_ROWS), ck_ref, cv_ref, table, table, None, None,
+                                    dict(S=s_out, D=d_out), *work)
+    begin()
     n_chunk = q_ref.shape[0] // W_CHUNK
 
     def copies(i, b):
@@ -312,20 +320,26 @@
             for copy in copies(i + W_SLOTS, b):
                 copy.start()
 
+        @pl.when(i == 0)
+        def _():
+            widen()
+
     for copy, src, dst in zip(gains, (gain_a, gain_m), (ga_out, gm_out)):
         copy.wait()
         dst[...] = src[...].astype(F32).reshape(dst.shape)
-
-
-def split_heads(w_q, w_k, w_v, ga, gm):
+    end()
+
+
+def split_heads(table, cache_k, cache_v, w_q, w_k, w_v, ga, gm):
     d = w_q.shape[0]
     vmem = pl.BlockSpec(memory_space=pltpu.VMEM)
     any_spec = pl.BlockSpec(memory_space=pl.ANY)
     return pl.pallas_call(
         heads_kernel,
-        out_shape=[pltpu.VMEM((4, d, WIDE), BF16)] + [pltpu.VMEM((2 * HEAD, HALF), F32)] * 2 + [pltpu.VMEM((1, d), F32)] * 2,
-        in_specs=[any_spec] * 5,
-        out_specs=[vmem] * 5,
+        out_shape=[pltpu.VMEM((4, d, WIDE), BF16)] + [pltpu.VMEM((2 * HEAD, HALF), F32)] * 2 + [pltpu.VMEM((1, d), F32)] * 2
+        + [pltpu.HBM((PIECE_ROWS[n], KV_WIDE), F32) for n in "SD"],
+        in_specs=[pl.BlockSpec(memory_space=pltpu.SMEM)] + [any_spec] * 7,
+        out_specs=[vmem] * 5 + [any_spec] * 2,
         scratch_shapes=[
             pltpu.VMEM((W_SLOTS, W_CHUNK, 8, HEAD), BF16),
             pltpu.VMEM((W_SLOTS, W_CHUNK, 4, HEAD), BF16),
@@ -334,11 +348,11 @@
             pltpu.VMEM((d,), BF16),
             pltpu.SemaphoreType.DMA((W_SLOTS, 3)),
             pltpu.SemaphoreType.DMA((2,)),
-        ],
+        ] + pack_work(S_ROWS + D_ROWS, 4 + len(WHOLE_D), 2),
         compiler_params=pltpu.CompilerParams(vmem_limit_bytes=VMEM_BESIDE),
         cost_estimate=pl.CostEstimate(flops=5_000_000_000, bytes_accessed=20_000_000, transcendentals=0),
         name="heads",
-    )(w_q, w_k, w_v, ga, gm)
+    )(table, cache_k, cache_v, w_q, w_k, w_v, ga, gm)
 
 
 def layer_kernel(n_att, n_ff, sizes, slot, tab_ref, over_ref, ga_ref, gm_ref, cos_ref, sin_ref, wh_ref, h_ref, wo_ref,
@@ -685,15 +699,10 @@
     def body(hidden, start_pos, cache_k, cache_v, w_q, w_k, w_v, w_o, w_gate, w_up, w_down, norm_attn, norm_mlp):
         n_seq, _, d = hidden.shape
         i32 = jnp.int32
-        table, over, piece_a, piece_b, piece_e, piece_o = pack_call(
-            pack_first_kernel, 4, "ABEO", A_ROWS + B_ROWS, A_UNITS + len(WHOLE_B))(start_pos, cache_k, cache_v)
+        table, over, piece_a, piece_b, piece_e, piece_o = plan_and_pack(start_pos, cache_k, cache_v)
         in_smem = lambda x: pltpu.with_memory_space_constraint(x, pltpu.SMEM)
         got_a = send(piece_a, [(0, 3)])
         got_b = send(piece_b, [(0, 2), (2, 0), (3, 1)])
-        piece_s, piece_d = pack_call(
-            pack_second_kernel, 0, "SD", S_ROWS + D_ROWS, 4 + len(WHOLE_D))(in_smem(table), cache_k, cache_v)
-        sib = send(piece_s, [(0, 1), (1, 0)])
-        got_d = send(piece_d, [(0, 3)])
         got_a, piece_e, piece_o = lax.optimization_barrier((got_a, piece_e, piece_o))
         got_e = send(piece_e, [(1, 2)])
         got_o = send(piece_o, [(1, 3)])
@@ -710,7 +719,9 @@
         full, full_f = lax.cond(over[0] > 0, send_all, lambda _: tuple(blank(2)), 0)
 
         w_q, w_k, w_v, full, full_f = lax.optimization_barrier((w_q, w_k, w_v, full, full_f))
-        kept = split_heads(w_q, w_k, w_v, norm_attn, norm_mlp)
+        *kept, piece_s, piece_d = split_heads(in_smem(table), cache_k, cache_v, w_q, w_k, w_v, norm_attn, norm_mlp)
+        sib = send(piece_s, [(0, 1), (1, 0)])
+        got_d = send(piece_d, [(0, 3)])
         wh, cos, sin, ga, gm = [pltpu.with_memory_space_constraint(x, pltpu.VMEM) for x in kept]
         wo = w_o.reshape(-1, d)
 

time: 478 us -> 491 us (1.027)
  waiting for transfers between devices: 174 us -> 185 us
    ppermute x21, waiting for transfers between devices: 174 us -> 185 us  [send(): x = lax.ppermute(x, axis, pairs)]
  transfers between devices with their start and end apart: 21 -> 21, of which waited for: 6 -> 6; matrix products, arithmetic and copies ran while one was open for 0% -> 0% of each run, Pallas kernels for 34% -> 31%
where the time goes in v6:
time: 491 us; the launch traced here: 490 us
  Pallas kernels  276 us (56%)
  waiting for transfers between devices  185 us (38%)
  starting transfers between devices  24.3 us (5%)
    pallas_call x4, Pallas kernels, run_layer(): pl.pallas_call(functools.partial(layer_kernel, 4, n_ff, sizes, slot), out...  210 us
    ppermute x21, waiting for transfers between devices, send(): x = lax.ppermute(x, axis, pairs)  185 us
    pallas_call x1, Pallas kernels, write_windows(): pl.pallas_call(window_kernel, out_shape=[jax.ShapeDtypeStruct(cache_k.sha...  29.7 us
    ppermute x21, starting transfers between devices, send(): x = lax.ppermute(x, axis, pairs)  24.3 us
    pallas_call x5, Pallas kernels, place_rows(): pl.pallas_call(functools.partial(place_kernel, where, blk), out_shape=jax...  20.6 us
    pallas_call x1, Pallas kernels, split_heads(): pl.pallas_call(heads_kernel, out_shape=[pltpu.VMEM((4, d, WIDE), BF16)] +...  11 us
  transfers between devices with their start and end apart: 21, of which 6 were waited for; matrix products, arithmetic and copies ran while one was open for 0% of the time, Pallas kernels for 31%

profile of v6, /device:TPU:0, one launch (start us, length us, event | category | flops | bytes accessed | tf_op | source)
XLA Modules:
  0.0 489.8 jit_solution(17618214282011046753)
XLA Ops:
  0.6 5.0 %pack.1 = (s32[80]{0:T(128)S(4)}, s32[1]{0:T(128)S(4)}, f32[160,2048]{1,0:T(8,128)}, f32[384,2048]{1,0:T(8,128)}, f32[80,2048]{1,0:T(8,128)}, /*index=5*/f32[80,2048]{1,0:T(8,128)}) custom-call(s32[16]{0:T(128)} %sc_ref, bf16[16,128,1024]{2,1,0:T(8,128)(2,1)} %ck_ref.13, bf16[16,128,1024]{2,1,0:T(8,128)(2,1)} %cv_ref.13), custom_call_target="tpu_custom_call" | custom-call | flops 10000000 | bytes 8000000 | tf_op jit(solution)/shard_map/pack/pallas_call | solution.py:197
  5.7 11.0 %heads.1 = (bf16[4,2304,1024]{2,1,0:T(8,128)(2,1)S(1)}, f32[512,128]{1,0:T(8,128)S(1)}, f32[512,128]{1,0:T(8,128)S(1)}, f32[1,2304]{1,0:T(1,128)S(1)}, f32[1,230...) custom-call(s32[80]{0:T(128)S(4)} %get-tuple-element.92.table.tab_ref, bf16[16,128,1024]{2,1,0:T(8,128)(2,1)} %ck_ref.13, ...), custom_call_target="tpu_custom_call" | custom-call | flops 5000000000 | bytes 20000000 | tf_op jit(solution)/shard_map/heads/pallas_call | solution.py:337
  16.7 1.9 collective-permute-start.2
  18.7 2.4 collective-permute-start.3
  21.0 1.9 collective-permute-start.4
  23.0 6.0 %collective-permute-start.5 = (f32[256,2048]{1,0:T(8,128)}, f32[256,2048]{1,0:T(8,128)}, u32[]{:S(2)}, u32[]{:S(2)}) collective-permute-start(f32[256,2048]{1,0:T(8,128)} %get-tuple-element.83), channel_id=1, source_target_pairs={{0,3},{4,7}} | collective-permute-start | bytes 6291464 | tf_op jit(solution)/shard_map/ppermute | solution.py:696
  29.0 12.1 %collective-permute-done.3.rest_0_.rest_1_.rest_2_.rest_3_.rest_4_ = f32[160,2048]{1,0:T(8,128)} collective-permute-done((f32[160,2048]{1,0:T(8,128)}, f32[160,2048]{1,0:T(8,128)}, u32[]{:S(2)}, u32[]{:S(2)}) %collective-permute-start.3) | collective-permute-done | bytes 1310752 | tf_op jit(solution)/shard_map/ppermute | solution.py:696
  41.1 1.6 collective-permute-start.6
  42.7 1.5 collective-permute-start.7
  44.2 52.4 %shard_map.148 = (f32[256,2304]{1,0:T(8,128)}, bf16[16,256,2304]{2,1,0:T(8,128)(2,1)}) custom-call(s32[80]{0:T(128)S(4)} %get-tuple-element.92.table.tab_ref, s32[1]{0:T(128)S(4)} %get-tuple-element.59.over_ref, f32[1,2304]{1,0:T(1,128)S(1)} %get-tuple-element.65.ga_ref, f32[1,2304]{1,0:T(1,128)S(1)} %get-tuple-element.66.gm_ref, ...), custom_call_target="tpu_custom_call" | custom-call | flops 40962666496 | bytes 160000000 | tf_op jit(solution)/shard_map/pallas_call | solution.py:554
  96.7 52.5 %shard_map.149 = (f32[256,2304]{1,0:T(8,128)}, bf16[16,256,2304]{2,1,0:T(8,128)(2,1)}) custom-call(s32[80]{0:T(128)S(4)} %get-tuple-element.92.table.tab_ref, s32[1]{0:T(128)S(4)} %get-tuple-element.59.over_ref, f32[1,2304]{1,0:T(1,128)S(1)} %get-tuple-element.65.ga_ref, f32[1,2304]{1,0:T(1,128)S(1)} %get-tuple-element.66.gm_ref, ...), custom_call_target="tpu_custom_call", output_to_operand_aliasing={{1}: (22, {})} | custom-call | flops 40962666496 | bytes 160000000 | tf_op jit(solution)/shard_map/pallas_call | solution.py:554
  149.2 52.4 %shard_map.150 = (f32[256,2304]{1,0:T(8,128)}, bf16[16,256,2304]{2,1,0:T(8,128)(2,1)}) custom-call(s32[80]{0:T(128)S(4)} %get-tuple-element.92.table.tab_ref, s32[1]{0:T(128)S(4)} %get-tuple-element.59.over_ref, f32[1,2304]{1,0:T(1,128)S(1)} %get-tuple-element.65.ga_ref, f32[1,2304]{1,0:T(1,128)S(1)} %get-tuple-element.66.gm_ref, ...), custom_call_target="tpu_custom_call", output_to_operand_aliasing={{1}: (22, {})} | custom-call | flops 40962666496 | bytes 160000000 | tf_op jit(solution)/shard_map/pallas_call | solution.py:554
  201.6 52.4 %shard_map.151 = (f32[192,2304]{1,0:T(8,128)}, f32[64,2304]{1,0:T(8,128)}, bf16[16,256,2304]{2,1,0:T(8,128)(2,1)}) custom-call(s32[80]{0:T(128)S(4)} %get-tuple-element.92.table.tab_ref, s32[1]{0:T(128)S(4)} %get-tuple-element.59.over_ref, f32[1,2304]{1,0:T(1,128)S(1)} %get-tuple-element.65.ga_ref, ...), custom_call_target="tpu_custom_call", output_to_operand_aliasing={{2}: (22, {})} | custom-call | flops 40962666496 | bytes 160000000 | tf_op jit(solution)/shard_map/pallas_call | solution.py:554
  254.0 3.9 collective-permute-start.22
  257.9 29.7 %cache_window.1 = (bf16[16,128,1024]{2,1,0:T(8,128)(2,1)}, bf16[16,128,1024]{2,1,0:T(8,128)(2,1)}) custom-call(s32[16]{0:T(128)S(1)} %copy-done.10, bf16[16,256,2304]{2,1,0:T(8,128)(2,1)} %h_ref.9, f32[1,2304]{1,0:T(1,128)S(1)} %get-tuple-element.65.ga_ref, f32[512,128]{1,0:T(8,128)S(1)} %get-tuple-element.67.cos_ref, ...), custom_call_target="tpu_custom_call" | custom-call | flops 19327352832 | bytes 60000000 | tf_op jit(solution)/shard_map/cache_window/pallas_call | solution.py:610
  287.6 2.0 collective-permute-start.8
  289.6 22.7 %collective-permute-done.8.rest_0_ = f32[64,2304]{1,0:T(8,128)} collective-permute-done((f32[64,2304]{1,0:T(8,128)}, f32[64,2304]{1,0:T(8,128)}, u32[]{:S(2)}, u32[]{:S(2)}) %collective-permute-start.8) | collective-permute-done | bytes 589856 | tf_op jit(solution)/shard_map/ppermute | solution.py:696
  312.3 2.0 collective-permute-start.14
  314.4 48.4 %collective-permute-done.20.rest_7_ = f32[256,2304]{1,0:T(8,128)S(1)} collective-permute-done((f32[256,2304]{1,0:T(8,128)}, f32[256,2304]{1,0:T(8,128)S(1)}, u32[]{:S(2)}, u32[]{:S(2)}) %collective-permute-start.20) | collective-permute-done | bytes 2359328 | tf_op jit(solution)/shard_map/ppermute | solution.py:696
  362.8 1.4 copy-done
  364.2 49.1 %collective-permute-done.17.rest_4_ = f32[256,2304]{1,0:T(8,128)S(1)} collective-permute-done((f32[256,2304]{1,0:T(8,128)}, f32[256,2304]{1,0:T(8,128)S(1)}, u32[]{:S(2)}, u32[]{:S(2)}) %collective-permute-start.17) | collective-permute-done | bytes 2359328 | tf_op jit(solution)/shard_map/ppermute | solution.py:696
  413.4 49.6 %collective-permute-done.14.rest_1_ = f32[256,2304]{1,0:T(8,128)S(1)} collective-permute-done((f32[256,2304]{1,0:T(8,128)}, f32[256,2304]{1,0:T(8,128)S(1)}, u32[]{:S(2)}, u32[]{:S(2)}) %collective-permute-start.14) | collective-permute-done | bytes 2359328 | tf_op jit(solution)/shard_map/ppermute | solution.py:696
  463.0 0.5 collective-permute-start.11
  463.6 0.5 collective-permute-start.9
  464.0 0.4 copy-done.3
  464.4 3.1 collective-permute-done.15.rest_2_
  467.6 1.4 copy-done.8
  469.0 12.3 %shard_map.152.rest_2_ = bf16[16,256,2304]{2,1,0:T(8,128)(2,1)} custom-call(s32[80]{0:T(128)S(4)} %get-tuple-element.92.table.tab_ref, f32[256,2304]{1,0:T(8,128)} %copy-done.5, f32[256,2304]{1,0:T(8,128)} %copy-done.3, f32[256,2304]{1,0:T(8,128)} %copy-done.8, f32[256,2304]{1,0:T(8,128)} %copy-done.4, ...), custom_call_target="tpu_custom_call", output_to_operand_aliasing={{}: (11, {})} | custom-call | flops 10000000 | bytes 34504704 | tf_op jit(solution)/shard_map/pallas_call | solution.py:674
  481.3 2.4 shard_map.153.rest_1_
  483.7 2.2 shard_map.154.rest_1_
  486.0 1.8 shard_map.155.rest_1_
  487.8 1.8 shard_map.156
  (46 shorter events, 0.2 us)
Async XLA Ops:
  0.6 5.1 %copy-start.9 = (s32[16]{0:T(128)S(1)}, s32[16]{0:T(128)}, u32[]{:S(2)}) copy-start(s32[16]{0:T(128)} %sc_ref) | copy-start | bytes 196
  16.7 27.5 %collective-permute-start.2 = (f32[512,2048]{1,0:T(8,128)}, f32[512,2048]{1,0:T(8,128)}, u32[]{:S(2)}, u32[]{:S(2)}) collective-permute-start(f32[512,2048]{1,0:T(8,128)} %get-tuple-element.70), channel_id=1, source_target_pairs={{0,1},{1,0},{4,5},{5,4}} | collective-permute-start | bytes 12582920 | tf_op jit(solution)/shard_map/ppermute | solution.py:696
  18.7 22.5 %collective-permute-start.3 = (f32[160,2048]{1,0:T(8,128)}, f32[160,2048]{1,0:T(8,128)}, u32[]{:S(2)}, u32[]{:S(2)}) collective-permute-start(f32[160,2048]{1,0:T(8,128)} %get-tuple-element.73), channel_id=1, source_target_pairs={{0,3},{4,7}} | collective-permute-start | bytes 3932168 | tf_op jit(solution)/shard_map/ppermute | solution.py:696
  21.0 75.6 %collective-permute-start.4 = (f32[384,2048]{1,0:T(8,128)}, f32[384,2048]{1,0:T(8,128)}, u32[]{:S(2)}, u32[]{:S(2)}) collective-permute-start(f32[384,2048]{1,0:T(8,128)} %get-tuple-element.79), channel_id=1, source_target_pairs={{0,2},{2,0},{3,1},{4,6},{6,4},{7,5}} | collective-permute-start | bytes 9437192 | tf_op jit(solution)/shard_map/ppermute | solution.py:696
  23.0 126.2 %collective-permute-start.5 = (f32[256,2048]{1,0:T(8,128)}, f32[256,2048]{1,0:T(8,128)}, u32[]{:S(2)}, u32[]{:S(2)}) collective-permute-start(f32[256,2048]{1,0:T(8,128)} %get-tuple-element.83), channel_id=1, source_target_pairs={{0,3},{4,7}} | collective-permute-start | bytes 6291464 | tf_op jit(solution)/shard_map/ppermute | solution.py:696
  41.1 108.0 %collective-permute-start.6 = (f32[80,2048]{1,0:T(8,128)}, f32[80,2048]{1,0:T(8,128)}, u32[]{:S(2)}, u32[]{:S(2)}) collective-permute-start(f32[80,2048]{1,0:T(8,128)} %get-tuple-element.84), channel_id=1, source_target_pairs={{1,2},{5,6}} | collective-permute-start | bytes 1966088 | tf_op jit(solution)/shard_map/ppermute | solution.py:696
  42.7 106.4 %collective-permute-start.7 = (f32[80,2048]{1,0:T(8,128)}, f32[80,2048]{1,0:T(8,128)}, u32[]{:S(2)}, u32[]{:S(2)}) collective-permute-start(f32[80,2048]{1,0:T(8,128)} %get-tuple-element.85), channel_id=1, source_target_pairs={{1,3},{5,7}} | collective-permute-start | bytes 1966088 | tf_op jit(solution)/shard_map/ppermute | solution.py:696
  201.6 56.4 %copy-start.10 = (s32[16]{0:T(128)S(1)}, s32[16]{0:T(128)}, u32[]{:S(2)}) copy-start(s32[16]{0:T(128)} %sc_ref) | copy-start | bytes 196
  254.0 58.4 %collective-permute-start.22 = (f32[192,2304]{1,0:T(8,128)}, f32[192,2304]{1,0:T(8,128)}, u32[]{:S(2)}, u32[]{:S(2)}) collective-permute-start(f32[192,2304]{1,0:T(8,128)} %get-tuple-element.97), channel_id=1, source_target_pairs={{0,1},{1,0},{2,3},{3,2},{4,5},{5,4},{6,7},{7,6}} | collective-permute-start | bytes 5308424 | tf_op jit(solution)/shard_map/ppermute | solution.py:696
  257.9 56.5 %collective-permute-start.10 = (f32[192,2304]{1,0:T(8,128)}, f32[192,2304]{1,0:T(8,128)}, u32[]{:S(2)}, u32[]{:S(2)}) collective-permute-start(f32[192,2304]{1,0:T(8,128)} %get-tuple-element.97), channel_id=1, source_target_pairs={{0,2},{1,3},{2,0},{3,1},{4,6},{5,7},{6,4},{7,5}} | collective-permute-start | bytes 5308424 | tf_op jit(solution)/shard_map/ppermute | solution.py:696
  287.6 24.8 %collective-permute-start.8 = (f32[64,2304]{1,0:T(8,128)}, f32[64,2304]{1,0:T(8,128)}, u32[]{:S(2)}, u32[]{:S(2)}) collective-permute-start(f32[64,2304]{1,0:T(8,128)} %get-tuple-element.96), channel_id=1, source_target_pairs={{0,2},{1,3},{2,0},{3,1},{4,6},{5,7},{6,4},{7,5}} | collective-permute-start | bytes 1769480 | tf_op jit(solution)/shard_map/ppermute | solution.py:696
  289.6 73.2 %collective-permute-start.20 = (f32[256,2304]{1,0:T(8,128)}, f32[256,2304]{1,0:T(8,128)S(1)}, u32[]{:S(2)}, u32[]{:S(2)}) collective-permute-start(f32[256,2304]{1,0:T(8,128)} %get-tuple-element.100), channel_id=1, source_target_pairs={{0,2},{1,3},{2,0},{3,1},{4,6},{5,7},{6,4},{7,5}} | collective-permute-start | bytes 7077896 | tf_op jit(solution)/shard_map/ppermute | solution.py:696
  289.6 73.2 %collective-permute-start.19 = (f32[256,2304]{1,0:T(8,128)}, f32[256,2304]{1,0:T(8,128)S(1)}, u32[]{:S(2)}, u32[]{:S(2)}) collective-permute-start(f32[256,2304]{1,0:T(8,128)} %get-tuple-element.100), channel_id=1, source_target_pairs={{0,1},{1,0},{2,3},{3,2},{4,5},{5,4},{6,7},{7,6}} | collective-permute-start | bytes 7077896 | tf_op jit(solution)/shard_map/ppermute | solution.py:696
  312.3 101.0 %collective-permute-start.17 = (f32[256,2304]{1,0:T(8,128)}, f32[256,2304]{1,0:T(8,128)S(1)}, u32[]{:S(2)}, u32[]{:S(2)}) collective-permute-start(f32[256,2304]{1,0:T(8,128)} %get-tuple-element.99), channel_id=1, source_target_pairs={{0,2},{1,3},{2,0},{3,1},{4,6},{5,7},{6,4},{7,5}} | collective-permute-start | bytes 7077896 | tf_op jit(solution)/shard_map/ppermute | solution.py:696
  312.3 150.6 %collective-permute-start.14 = (f32[256,2304]{1,0:T(8,128)}, f32[256,2304]{1,0:T(8,128)S(1)}, u32[]{:S(2)}, u32[]{:S(2)}) collective-permute-start(f32[256,2304]{1,0:T(8,128)} %get-tuple-element.98), channel_id=1, source_target_pairs={{0,2},{1,3},{2,0},{3,1},{4,6},{5,7},{6,4},{7,5}} | collective-permute-start | bytes 7077896 | tf_op jit(solution)/shard_map/ppermute | solution.py:696
  314.4 148.6 %collective-permute-start.16 = (f32[256,2304]{1,0:T(8,128)}, f32[256,2304]{1,0:T(8,128)S(1)}, u32[]{:S(2)}, u32[]{:S(2)}) collective-permute-start(f32[256,2304]{1,0:T(8,128)} %get-tuple-element.99), channel_id=1, source_target_pairs={{0,1},{1,0},{2,3},{3,2},{4,5},{5,4},{6,7},{7,6}} | collective-permute-start | bytes 7077896 | tf_op jit(solution)/shard_map/ppermute | solution.py:696
  362.8 1.4 copy-start
  362.8 100.7 %collective-permute-start.13 = (f32[256,2304]{1,0:T(8,128)}, f32[256,2304]{1,0:T(8,128)S(1)}, u32[]{:S(2)}, u32[]{:S(2)}) collective-permute-start(f32[256,2304]{1,0:T(8,128)} %get-tuple-element.98), channel_id=1, source_target_pairs={{0,1},{1,0},{2,3},{3,2},{4,5},{5,4},{6,7},{7,6}} | collective-permute-start | bytes 7077896 | tf_op jit(solution)/shard_map/ppermute | solution.py:696
  364.2 99.3 %copy-start.1 = (f32[256,2304]{1,0:T(8,128)}, f32[256,2304]{1,0:T(8,128)S(1)}, u32[]{:S(2)}) copy-start(f32[256,2304]{1,0:T(8,128)S(1)} %collective-permute-done.19.rest_6_) | copy-start | bytes 7077892
  364.2 99.3 %collective-permute-start.21 = (f32[256,2304]{1,0:T(8,128)S(1)}, f32[256,2304]{1,0:T(8,128)S(1)}, u32[]{:S(2)}, u32[]{:S(2)}) collective-permute-start(f32[256,2304]{1,0:T(8,128)S(1)} %collective-permute-done.20.rest_7_), channel_id=1, source_target_pairs={{0,1},{1,0},{2,3},{3,2},{4,5},{5,4},{6,7},{7,6}} | collective-permute-start | bytes 7077896 | tf_op jit(solution)/shard_map/ppermute | solution.py:696
  413.4 50.7 %copy-start.2 = (f32[256,2304]{1,0:T(8,128)}, f32[256,2304]{1,0:T(8,128)S(1)}, u32[]{:S(2)}) copy-start(f32[256,2304]{1,0:T(8,128)S(1)} %collective-permute-done.17.rest_4_) | copy-start | bytes 7077892
  413.4 50.7 %collective-permute-start.18 = (f32[256,2304]{1,0:T(8,128)S(1)}, f32[256,2304]{1,0:T(8,128)S(1)}, u32[]{:S(2)}, u32[]{:S(2)}) collective-permute-start(f32[256,2304]{1,0:T(8,128)S(1)} %collective-permute-done.17.rest_4_), channel_id=1, source_target_pairs={{0,1},{1,0},{2,3},{3,2},{4,5},{5,4},{6,7},{7,6}} | collective-permute-start | bytes 7077896 | tf_op jit(solution)/shard_map/ppermute | solution.py:696
  463.0 1.4 copy-start.3
  463.0 4.5 collective-permute-start.15
  463.0 4.5 copy-start.4
  463.0 20.7 %collective-permute-start.11 = (f32[192,2304]{1,0:T(8,128)}, f32[192,2304]{1,0:T(8,128)}, u32[]{:S(2)}, u32[]{:S(2)}) collective-permute-start(f32[192,2304]{1,0:T(8,128)} %collective-permute-done.10.rest_0_), channel_id=1, source_target_pairs={{0,1},{1,0},{2,3},{3,2},{4,5},{5,4},{6,7},{7,6}} | collective-permute-start | bytes 5308424 | tf_op jit(solution)/shard_map/ppermute | solution.py:696
  463.5 4.0 copy-start.5
  463.5 17.8 %collective-permute-start.12 = (f32[64,2304]{1,0:T(8,128)}, f32[64,2304]{1,0:T(8,128)}, u32[]{:S(2)}, u32[]{:S(2)}) collective-permute-start(f32[64,2304]{1,0:T(8,128)} %get-tuple-element.96), channel_id=1, source_target_pairs={{0,1},{1,0},{2,3},{3,2},{4,5},{5,4},{6,7},{7,6}} | collective-permute-start | bytes 1769480 | tf_op jit(solution)/shard_map/ppermute | solution.py:696
  463.6 4.0 copy-start.6
  463.6 24.3 %collective-permute-start.9 = (f32[64,2304]{1,0:T(8,128)}, f32[64,2304]{1,0:T(8,128)}, u32[]{:S(2)}, u32[]{:S(2)}) collective-permute-start(f32[64,2304]{1,0:T(8,128)} %collective-permute-done.8.rest_0_), channel_id=1, source_target_pairs={{0,1},{1,0},{2,3},{3,2},{4,5},{5,4},{6,7},{7,6}} | collective-permute-start | bytes 1769480 | tf_op jit(solution)/shard_map/ppermute | solution.py:696
  464.4 3.1 copy-start.7
  467.5 1.4 copy-start.8

commit v7 on v6

--- a/solution.py
+++ b/solution.py
@@ -320,7 +320,7 @@
             for copy in copies(i + W_SLOTS, b):
                 copy.start()
 
-        @pl.when(i == 0)
+        @pl.when(i == 2)
         def _():
             widen()
 
@@ -750,8 +750,8 @@
         out = place_rows(in_smem(tab), parts + [near_most], where + [(last + 1, 0)], out, 64)
         out = place_rows(in_smem(tab), [crs_most, near_rest], [(last + 2, 0), (last + 1, 192)], out, 64)
         out = place_rows(in_smem(tab), [dia_most], [(last + 3, 0)], out, 64)
-        out = place_rows(in_smem(tab), [crs_rest], [(last + 2, 192)], out, 16)
-        out = place_rows(in_smem(tab), [dia_rest], [(last + 3, 192)], out, 16)
+        out = place_rows(in_smem(tab), [crs_rest], [(last + 2, 192)], out, 32)
+        out = place_rows(in_smem(tab), [dia_rest], [(last + 3, 192)], out, 32)
         return out, new_k, new_v
 
     group_spec = P('dp', None, None)

time: 491 us -> 489 us (level)
  no operation moved by 1% of the time
where the time goes in v7:
time: 489 us; the launch traced here: 488 us
  Pallas kernels  275 us (56%)
  waiting for transfers between devices  185 us (38%)
  starting transfers between devices  24.4 us (5%)
    pallas_call x4, Pallas kernels, run_layer(): pl.pallas_call(functools.partial(layer_kernel, 4, n_ff, sizes, slot), out...  210 us
    ppermute x21, waiting for transfers between devices, send(): x = lax.ppermute(x, axis, pairs)  185 us
    pallas_call x1, Pallas kernels, write_windows(): pl.pallas_call(window_kernel, out_shape=[jax.ShapeDtypeStruct(cache_k.sha...  29.7 us
    ppermute x21, starting transfers between devices, send(): x = lax.ppermute(x, axis, pairs)  24.4 us
    pallas_call x5, Pallas kernels, place_rows(): pl.pallas_call(functools.partial(place_kernel, where, blk), out_shape=jax...  20.5 us
  transfers between devices with their start and end apart: 21, of which 6 were waited for; matrix products, arithmetic and copies ran while one was open for 0% of the time, Pallas kernels for 31%

profile of v7, /device:TPU:0, one launch (start us, length us, event | category | flops | bytes accessed | tf_op | source)
XLA Modules:
  0.0 488.4 jit_solution(1831268816025679935)
XLA Ops:
  0.6 5.0 %pack.1 = (s32[80]{0:T(128)S(4)}, s32[1]{0:T(128)S(4)}, f32[160,2048]{1,0:T(8,128)}, f32[384,2048]{1,0:T(8,128)}, f32[80,2048]{1,0:T(8,128)}, /*index=5*/f32[80,2048]{1,0:T(8,128)}) custom-call(s32[16]{0:T(128)} %sc_ref, bf16[16,128,1024]{2,1,0:T(8,128)(2,1)} %ck_ref.13, bf16[16,128,1024]{2,1,0:T(8,128)(2,1)} %cv_ref.13), custom_call_target="tpu_custom_call" | custom-call | flops 10000000 | bytes 8000000 | tf_op jit(solution)/shard_map/pack/pallas_call | solution.py:197
  5.7 9.8 %heads.1 = (bf16[4,2304,1024]{2,1,0:T(8,128)(2,1)S(1)}, f32[512,128]{1,0:T(8,128)S(1)}, f32[512,128]{1,0:T(8,128)S(1)}, f32[1,2304]{1,0:T(1,128)S(1)}, f32[1,230...) custom-call(s32[80]{0:T(128)S(4)} %get-tuple-element.92.table.tab_ref, bf16[16,128,1024]{2,1,0:T(8,128)(2,1)} %ck_ref.13, ...), custom_call_target="tpu_custom_call" | custom-call | flops 5000000000 | bytes 20000000 | tf_op jit(solution)/shard_map/heads/pallas_call | solution.py:337
  15.5 1.9 collective-permute-start.2
  17.4 2.4 collective-permute-start.3
  19.8 1.9 collective-permute-start.4
  21.7 6.0 %collective-permute-start.5 = (f32[256,2048]{1,0:T(8,128)}, f32[256,2048]{1,0:T(8,128)}, u32[]{:S(2)}, u32[]{:S(2)}) collective-permute-start(f32[256,2048]{1,0:T(8,128)} %get-tuple-element.83), channel_id=1, source_target_pairs={{0,3},{4,7}} | collective-permute-start | bytes 6291464 | tf_op jit(solution)/shard_map/ppermute | solution.py:696
  27.7 12.1 %collective-permute-done.3.rest_0_.rest_1_.rest_2_.rest_3_.rest_4_ = f32[160,2048]{1,0:T(8,128)} collective-permute-done((f32[160,2048]{1,0:T(8,128)}, f32[160,2048]{1,0:T(8,128)}, u32[]{:S(2)}, u32[]{:S(2)}) %collective-permute-start.3) | collective-permute-done | bytes 1310752 | tf_op jit(solution)/shard_map/ppermute | solution.py:696
  39.9 1.6 collective-permute-start.6
  41.5 1.5 collective-permute-start.7
  43.0 52.4 %shard_map.148 = (f32[256,2304]{1,0:T(8,128)}, bf16[16,256,2304]{2,1,0:T(8,128)(2,1)}) custom-call(s32[80]{0:T(128)S(4)} %get-tuple-element.92.table.tab_ref, s32[1]{0:T(128)S(4)} %get-tuple-element.59.over_ref, f32[1,2304]{1,0:T(1,128)S(1)} %get-tuple-element.65.ga_ref, f32[1,2304]{1,0:T(1,128)S(1)} %get-tuple-element.66.gm_ref, ...), custom_call_target="tpu_custom_call" | custom-call | flops 40962666496 | bytes 160000000 | tf_op jit(solution)/shard_map/pallas_call | solution.py:554
  95.4 52.5 %shard_map.149 = (f32[256,2304]{1,0:T(8,128)}, bf16[16,256,2304]{2,1,0:T(8,128)(2,1)}) custom-call(s32[80]{0:T(128)S(4)} %get-tuple-element.92.table.tab_ref, s32[1]{0:T(128)S(4)} %get-tuple-element.59.over_ref, f32[1,2304]{1,0:T(1,128)S(1)} %get-tuple-element.65.ga_ref, f32[1,2304]{1,0:T(1,128)S(1)} %get-tuple-element.66.gm_ref, ...), custom_call_target="tpu_custom_call", output_to_operand_aliasing={{1}: (22, {})} | custom-call | flops 40962666496 | bytes 160000000 | tf_op jit(solution)/shard_map/pallas_call | solution.py:554
  147.9 52.4 %shard_map.150 = (f32[256,2304]{1,0:T(8,128)}, bf16[16,256,2304]{2,1,0:T(8,128)(2,1)}) custom-call(s32[80]{0:T(128)S(4)} %get-tuple-element.92.table.tab_ref, s32[1]{0:T(128)S(4)} %get-tuple-element.59.over_ref, f32[1,2304]{1,0:T(1,128)S(1)} %get-tuple-element.65.ga_ref, f32[1,2304]{1,0:T(1,128)S(1)} %get-tuple-element.66.gm_ref, ...), custom_call_target="tpu_custom_call", output_to_operand_aliasing={{1}: (22, {})} | custom-call | flops 40962666496 | bytes 160000000 | tf_op jit(solution)/shard_map/pallas_call | solution.py:554
  200.3 52.4 %shard_map.151 = (f32[192,2304]{1,0:T(8,128)}, f32[64,2304]{1,0:T(8,128)}, bf16[16,256,2304]{2,1,0:T(8,128)(2,1)}) custom-call(s32[80]{0:T(128)S(4)} %get-tuple-element.92.table.tab_ref, s32[1]{0:T(128)S(4)} %get-tuple-element.59.over_ref, f32[1,2304]{1,0:T(1,128)S(1)} %get-tuple-element.65.ga_ref, ...), custom_call_target="tpu_custom_call", output_to_operand_aliasing={{2}: (22, {})} | custom-call | flops 40962666496 | bytes 160000000 | tf_op jit(solution)/shard_map/pallas_call | solution.py:554
  252.7 3.9 collective-permute-start.22
  256.7 29.7 %cache_window.1 = (bf16[16,128,1024]{2,1,0:T(8,128)(2,1)}, bf16[16,128,1024]{2,1,0:T(8,128)(2,1)}) custom-call(s32[16]{0:T(128)S(1)} %copy-done.10, bf16[16,256,2304]{2,1,0:T(8,128)(2,1)} %h_ref.9, f32[1,2304]{1,0:T(1,128)S(1)} %get-tuple-element.65.ga_ref, f32[512,128]{1,0:T(8,128)S(1)} %get-tuple-element.67.cos_ref, ...), custom_call_target="tpu_custom_call" | custom-call | flops 19327352832 | bytes 60000000 | tf_op jit(solution)/shard_map/cache_window/pallas_call | solution.py:610
  286.3 2.0 collective-permute-start.8
  288.4 22.7 %collective-permute-done.8.rest_0_ = f32[64,2304]{1,0:T(8,128)} collective-permute-done((f32[64,2304]{1,0:T(8,128)}, f32[64,2304]{1,0:T(8,128)}, u32[]{:S(2)}, u32[]{:S(2)}) %collective-permute-start.8) | collective-permute-done | bytes 589856 | tf_op jit(solution)/shard_map/ppermute | solution.py:696
  311.1 2.0 collective-permute-start.14
  313.1 48.4 %collective-permute-done.20.rest_7_ = f32[256,2304]{1,0:T(8,128)S(1)} collective-permute-done((f32[256,2304]{1,0:T(8,128)}, f32[256,2304]{1,0:T(8,128)S(1)}, u32[]{:S(2)}, u32[]{:S(2)}) %collective-permute-start.20) | collective-permute-done | bytes 2359328 | tf_op jit(solution)/shard_map/ppermute | solution.py:696
  361.6 1.4 copy-done
  363.0 49.1 %collective-permute-done.17.rest_4_ = f32[256,2304]{1,0:T(8,128)S(1)} collective-permute-done((f32[256,2304]{1,0:T(8,128)}, f32[256,2304]{1,0:T(8,128)S(1)}, u32[]{:S(2)}, u32[]{:S(2)}) %collective-permute-start.17) | collective-permute-done | bytes 2359328 | tf_op jit(solution)/shard_map/ppermute | solution.py:696
  412.1 49.6 %collective-permute-done.14.rest_1_ = f32[256,2304]{1,0:T(8,128)S(1)} collective-permute-done((f32[256,2304]{1,0:T(8,128)}, f32[256,2304]{1,0:T(8,128)S(1)}, u32[]{:S(2)}, u32[]{:S(2)}) %collective-permute-start.14) | collective-permute-done | bytes 2359328 | tf_op jit(solution)/shard_map/ppermute | solution.py:696
  461.7 0.5 collective-permute-start.11
  462.3 0.5 collective-permute-start.9
  462.8 0.4 copy-done.3
  463.2 3.1 collective-permute-done.15.rest_2_
  466.3 1.4 copy-done.8
  467.7 12.3 %shard_map.152.rest_2_ = bf16[16,256,2304]{2,1,0:T(8,128)(2,1)} custom-call(s32[80]{0:T(128)S(4)} %get-tuple-element.92.table.tab_ref, f32[256,2304]{1,0:T(8,128)} %copy-done.5, f32[256,2304]{1,0:T(8,128)} %copy-done.3, f32[256,2304]{1,0:T(8,128)} %copy-done.8, f32[256,2304]{1,0:T(8,128)} %copy-done.4, ...), custom_call_target="tpu_custom_call", output_to_operand_aliasing={{}: (11, {})} | custom-call | flops 10000000 | bytes 34504704 | tf_op jit(solution)/shard_map/pallas_call | solution.py:674
  480.0 2.4 shard_map.153.rest_1_
  482.5 2.2 shard_map.154.rest_1_
  484.7 1.8 shard_map.155.rest_1_
  486.5 1.8 shard_map.156
  (46 shorter events, 0.2 us)
Async XLA Ops:
  0.6 5.1 %copy-start.9 = (s32[16]{0:T(128)S(1)}, s32[16]{0:T(128)}, u32[]{:S(2)}) copy-start(s32[16]{0:T(128)} %sc_ref) | copy-start | bytes 196
  15.5 27.5 %collective-permute-start.2 = (f32[512,2048]{1,0:T(8,128)}, f32[512,2048]{1,0:T(8,128)}, u32[]{:S(2)}, u32[]{:S(2)}) collective-permute-start(f32[512,2048]{1,0:T(8,128)} %get-tuple-element.70), channel_id=1, source_target_pairs={{0,1},{1,0},{4,5},{5,4}} | collective-permute-start | bytes 12582920 | tf_op jit(solution)/shard_map/ppermute | solution.py:696
  17.4 22.5 %collective-permute-start.3 = (f32[160,2048]{1,0:T(8,128)}, f32[160,2048]{1,0:T(8,128)}, u32[]{:S(2)}, u32[]{:S(2)}) collective-permute-start(f32[160,2048]{1,0:T(8,128)} %get-tuple-element.73), channel_id=1, source_target_pairs={{0,3},{4,7}} | collective-permute-start | bytes 3932168 | tf_op jit(solution)/shard_map/ppermute | solution.py:696
  19.8 75.6 %collective-permute-start.4 = (f32[384,2048]{1,0:T(8,128)}, f32[384,2048]{1,0:T(8,128)}, u32[]{:S(2)}, u32[]{:S(2)}) collective-permute-start(f32[384,2048]{1,0:T(8,128)} %get-tuple-element.79), channel_id=1, source_target_pairs={{0,2},{2,0},{3,1},{4,6},{6,4},{7,5}} | collective-permute-start | bytes 9437192 | tf_op jit(solution)/shard_map/ppermute | solution.py:696
  21.7 126.2 %collective-permute-start.5 = (f32[256,2048]{1,0:T(8,128)}, f32[256,2048]{1,0:T(8,128)}, u32[]{:S(2)}, u32[]{:S(2)}) collective-permute-start(f32[256,2048]{1,0:T(8,128)} %get-tuple-element.83), channel_id=1, source_target_pairs={{0,3},{4,7}} | collective-permute-start | bytes 6291464 | tf_op jit(solution)/shard_map/ppermute | solution.py:696
  39.9 108.0 %collective-permute-start.6 = (f32[80,2048]{1,0:T(8,128)}, f32[80,2048]{1,0:T(8,128)}, u32[]{:S(2)}, u32[]{:S(2)}) collective-permute-start(f32[80,2048]{1,0:T(8,128)} %get-tuple-element.84), channel_id=1, source_target_pairs={{1,2},{5,6}} | collective-permute-start | bytes 1966088 | tf_op jit(solution)/shard_map/ppermute | solution.py:696
  41.5 106.4 %collective-permute-start.7 = (f32[80,2048]{1,0:T(8,128)}, f32[80,2048]{1,0:T(8,128)}, u32[]{:S(2)}, u32[]{:S(2)}) collective-permute-start(f32[80,2048]{1,0:T(8,128)} %get-tuple-element.85), channel_id=1, source_target_pairs={{1,3},{5,7}} | collective-permute-start | bytes 1966088 | tf_op jit(solution)/shard_map/ppermute | solution.py:696
  200.3 56.4 %copy-start.10 = (s32[16]{0:T(128)S(1)}, s32[16]{0:T(128)}, u32[]{:S(2)}) copy-start(s32[16]{0:T(128)} %sc_ref) | copy-start | bytes 196
  252.7 58.4 %collective-permute-start.22 = (f32[192,2304]{1,0:T(8,128)}, f32[192,2304]{1,0:T(8,128)}, u32[]{:S(2)}, u32[]{:S(2)}) collective-permute-start(f32[192,2304]{1,0:T(8,128)} %get-tuple-element.97), channel_id=1, source_target_pairs={{0,1},{1,0},{2,3},{3,2},{4,5},{5,4},{6,7},{7,6}} | collective-permute-start | bytes 5308424 | tf_op jit(solution)/shard_map/ppermute | solution.py:696
  256.7 56.5 %collective-permute-start.10 = (f32[192,2304]{1,0:T(8,128)}, f32[192,2304]{1,0:T(8,128)}, u32[]{:S(2)}, u32[]{:S(2)}) collective-permute-start(f32[192,2304]{1,0:T(8,128)} %get-tuple-element.97), channel_id=1, source_target_pairs={{0,2},{1,3},{2,0},{3,1},{4,6},{5,7},{6,4},{7,5}} | collective-permute-start | bytes 5308424 | tf_op jit(solution)/shard_map/ppermute | solution.py:696
  286.3 24.8 %collective-permute-start.8 = (f32[64,2304]{1,0:T(8,128)}, f32[64,2304]{1,0:T(8,128)}, u32[]{:S(2)}, u32[]{:S(2)}) collective-permute-start(f32[64,2304]{1,0:T(8,128)} %get-tuple-element.96), channel_id=1, source_target_pairs={{0,2},{1,3},{2,0},{3,1},{4,6},{5,7},{6,4},{7,5}} | collective-permute-start | bytes 1769480 | tf_op jit(solution)/shard_map/ppermute | solution.py:696
  288.3 73.2 %collective-permute-start.20 = (f32[256,2304]{1,0:T(8,128)}, f32[256,2304]{1,0:T(8,128)S(1)}, u32[]{:S(2)}, u32[]{:S(2)}) collective-permute-start(f32[256,2304]{1,0:T(8,128)} %get-tuple-element.100), channel_id=1, source_target_pairs={{0,2},{1,3},{2,0},{3,1},{4,6},{5,7},{6,4},{7,5}} | collective-permute-start | bytes 7077896 | tf_op jit(solution)/shard_map/ppermute | solution.py:696
  288.4 73.2 %collective-permute-start.19 = (f32[256,2304]{1,0:T(8,128)}, f32[256,2304]{1,0:T(8,128)S(1)}, u32[]{:S(2)}, u32[]{:S(2)}) collective-permute-start(f32[256,2304]{1,0:T(8,128)} %get-tuple-element.100), channel_id=1, source_target_pairs={{0,1},{1,0},{2,3},{3,2},{4,5},{5,4},{6,7},{7,6}} | collective-permute-start | bytes 7077896 | tf_op jit(solution)/shard_map/ppermute | solution.py:696
  311.1 101.0 %collective-permute-start.17 = (f32[256,2304]{1,0:T(8,128)}, f32[256,2304]{1,0:T(8,128)S(1)}, u32[]{:S(2)}, u32[]{:S(2)}) collective-permute-start(f32[256,2304]{1,0:T(8,128)} %get-tuple-element.99), channel_id=1, source_target_pairs={{0,2},{1,3},{2,0},{3,1},{4,6},{5,7},{6,4},{7,5}} | collective-permute-start | bytes 7077896 | tf_op jit(solution)/shard_map/ppermute | solution.py:696
  311.1 150.6 %collective-permute-start.14 = (f32[256,2304]{1,0:T(8,128)}, f32[256,2304]{1,0:T(8,128)S(1)}, u32[]{:S(2)}, u32[]{:S(2)}) collective-permute-start(f32[256,2304]{1,0:T(8,128)} %get-tuple-element.98), channel_id=1, source_target_pairs={{0,2},{1,3},{2,0},{3,1},{4,6},{5,7},{6,4},{7,5}} | collective-permute-start | bytes 7077896 | tf_op jit(solution)/shard_map/ppermute | solution.py:696
  313.1 148.6 %collective-permute-start.16 = (f32[256,2304]{1,0:T(8,128)}, f32[256,2304]{1,0:T(8,128)S(1)}, u32[]{:S(2)}, u32[]{:S(2)}) collective-permute-start(f32[256,2304]{1,0:T(8,128)} %get-tuple-element.99), channel_id=1, source_target_pairs={{0,1},{1,0},{2,3},{3,2},{4,5},{5,4},{6,7},{7,6}} | collective-permute-start | bytes 7077896 | tf_op jit(solution)/shard_map/ppermute | solution.py:696
  361.5 1.4 copy-start
  361.5 100.7 %collective-permute-start.13 = (f32[256,2304]{1,0:T(8,128)}, f32[256,2304]{1,0:T(8,128)S(1)}, u32[]{:S(2)}, u32[]{:S(2)}) collective-permute-start(f32[256,2304]{1,0:T(8,128)} %get-tuple-element.98), channel_id=1, source_target_pairs={{0,1},{1,0},{2,3},{3,2},{4,5},{5,4},{6,7},{7,6}} | collective-permute-start | bytes 7077896 | tf_op jit(solution)/shard_map/ppermute | solution.py:696
  363.0 99.3 %copy-start.1 = (f32[256,2304]{1,0:T(8,128)}, f32[256,2304]{1,0:T(8,128)S(1)}, u32[]{:S(2)}) copy-start(f32[256,2304]{1,0:T(8,128)S(1)} %collective-permute-done.19.rest_6_) | copy-start | bytes 7077892
  363.0 99.3 %collective-permute-start.21 = (f32[256,2304]{1,0:T(8,128)S(1)}, f32[256,2304]{1,0:T(8,128)S(1)}, u32[]{:S(2)}, u32[]{:S(2)}) collective-permute-start(f32[256,2304]{1,0:T(8,128)S(1)} %collective-permute-done.20.rest_7_), channel_id=1, source_target_pairs={{0,1},{1,0},{2,3},{3,2},{4,5},{5,4},{6,7},{7,6}} | collective-permute-start | bytes 7077896 | tf_op jit(solution)/shard_map/ppermute | solution.py:696
  412.1 50.7 %copy-start.2 = (f32[256,2304]{1,0:T(8,128)}, f32[256,2304]{1,0:T(8,128)S(1)}, u32[]{:S(2)}) copy-start(f32[256,2304]{1,0:T(8,128)S(1)} %collective-permute-done.17.rest_4_) | copy-start | bytes 7077892
  412.1 50.7 %collective-permute-start.18 = (f32[256,2304]{1,0:T(8,128)S(1)}, f32[256,2304]{1,0:T(8,128)S(1)}, u32[]{:S(2)}, u32[]{:S(2)}) collective-permute-start(f32[256,2304]{1,0:T(8,128)S(1)} %collective-permute-done.17.rest_4_), channel_id=1, source_target_pairs={{0,1},{1,0},{2,3},{3,2},{4,5},{5,4},{6,7},{7,6}} | collective-permute-start | bytes 7077896 | tf_op jit(solution)/shard_map/ppermute | solution.py:696
  461.7 1.4 copy-start.3
  461.7 4.5 collective-permute-start.15
  461.7 4.5 copy-start.4
  461.7 20.7 %collective-permute-start.11 = (f32[192,2304]{1,0:T(8,128)}, f32[192,2304]{1,0:T(8,128)}, u32[]{:S(2)}, u32[]{:S(2)}) collective-permute-start(f32[192,2304]{1,0:T(8,128)} %collective-permute-done.10.rest_0_), channel_id=1, source_target_pairs={{0,1},{1,0},{2,3},{3,2},{4,5},{5,4},{6,7},{7,6}} | collective-permute-start | bytes 5308424 | tf_op jit(solution)/shard_map/ppermute | solution.py:696
  462.2 4.0 copy-start.5
  462.3 17.8 %collective-permute-start.12 = (f32[64,2304]{1,0:T(8,128)}, f32[64,2304]{1,0:T(8,128)}, u32[]{:S(2)}, u32[]{:S(2)}) collective-permute-start(f32[64,2304]{1,0:T(8,128)} %get-tuple-element.96), channel_id=1, source_target_pairs={{0,1},{1,0},{2,3},{3,2},{4,5},{5,4},{6,7},{7,6}} | collective-permute-start | bytes 1769480 | tf_op jit(solution)/shard_map/ppermute | solution.py:696
  462.3 4.0 copy-start.6
  462.3 24.2 %collective-permute-start.9 = (f32[64,2304]{1,0:T(8,128)}, f32[64,2304]{1,0:T(8,128)}, u32[]{:S(2)}, u32[]{:S(2)}) collective-permute-start(f32[64,2304]{1,0:T(8,128)} %collective-permute-done.8.rest_0_), channel_id=1, source_target_pairs={{0,1},{1,0},{2,3},{3,2},{4,5},{5,4},{6,7},{7,6}} | collective-permute-start | bytes 1769480 | tf_op jit(solution)/shard_map/ppermute | solution.py:696
  463.2 3.1 copy-start.7
  466.3 1.4 copy-start.8
